TPU v7x, 256 devices: a whole 4x4x8 slice. The times are simulated.
256 devices in a mesh: dp: 8 (over x, core), expert: 32 (over z, y).
Axes of the slice: x: 4, y: 4, z: 8, core: 2. Of those that a mesh axis runs over, the one named last changes fastest.
Arguments:
- tokens: bfloat16 [5120, 262144], P(None, ('dp', 'expert')), may hold values from -24 to 24, as said below
- router: bfloat16 [5120, 160], P(None, 'expert'), may hold values from -1 to 1, as said below
- device_pick: int32 [3, 262144], P(None, 'dp'), may hold values from 0 to 31, as said below
- expert_pick: int32 [6, 262144], P(None, 'dp'), may hold values from 0 to 159, as said below
Outputs:
- gates: float32 [6, 262144], P(None, 'dp')
- device_max: float32 [32, 262144], P('expert', 'dp')
- balance: float32 [3], replicated
Inputs may be any that keep to these rules, and one draw needn't show every extreme that they name: tokens lie within the range; in each column the values are of order one, except in a few columns. router entries are of order 1 / sqrt(5120). `device_pick`: each column names 3 different devices. `expert_pick`: each column names 6 different experts, two on each device of the column's device_pick, in that order; the device of expert e is e // 5.
All inputs are finite; a program needn't handle non-finite values.
Results may differ from a plain program's by a relative error of at most 0.0003.
Values may be sent and summed in bfloat16 or wider, within the bound.
No kernel may reach another device: no remote copies, remote signals or barrier semaphores. Data moves between devices by JAX's collectives and lax.ppermute only.
A program may use at most 64 MiB of HBM per device.

v0:
```python
import jax
import jax.numpy as jnp
from jax import lax
from jax.sharding import Mesh
from jax.sharding import PartitionSpec as P

TOP = 6
DEV_TOP = 3
EXPERT = ("expert_0", "expert_1")
DP = ("dp_0", "dp_1")
DP_EXPERT = ("dp_0", "dp_1", "expert_0", "expert_1")


def gathered_by_axis(x, axes, dim):
    for axis in reversed(axes):
        x = lax.all_gather(x, axis, axis=dim, tiled=True)
    return x


def joined_along(tiles, dim):
    shape = list(tiles.shape[1:])
    shape[dim] *= tiles.shape[0]
    return jnp.moveaxis(tiles, 0, dim).reshape(shape)


def sent_to_all(x, axis):
    length = lax.axis_size(axis)
    return lax.all_to_all(jnp.broadcast_to(x[None], (length, *x.shape)), axis, 0, 0, tiled=True)


def gathered_copies(x, axis, dim):
    return joined_along(sent_to_all(x, axis), dim)


def by_axis(x, axes):
    for axis in axes:
        x = lax.psum(x, axis)
    return x


def local(tokens, router, device_pick, expert_pick):
    share = tokens.shape[1]
    num_devices = lax.axis_size(EXPERT)
    per_device = router.shape[1]
    num_experts = per_device * num_devices
    tok_rows = share * num_devices
    my_index = lax.axis_index(EXPERT)
    total_tokens = tok_rows * lax.axis_size(DP)
    scores = jnp.dot(
        tokens.T, gathered_by_axis(router, EXPERT, 1), preferred_element_type=jnp.float32
    ).T
    peak = jnp.max(scores, axis=0, keepdims=True)
    raised = jnp.exp(scores - peak)
    probs = raised / jnp.sum(raised, axis=0, keepdims=True)
    first_col = my_index * share
    experts_here = lax.dynamic_slice_in_dim(expert_pick, first_col, share, 1)
    devices_here = lax.dynamic_slice_in_dim(device_pick, first_col, share, 1)
    col_gates = jnp.take_along_axis(probs, experts_here, axis=0)
    col_maxima = jnp.max(probs.reshape(num_devices, per_device, share), axis=1)
    gates = gathered_copies(col_gates, EXPERT, 1)
    device_max = lax.all_to_all(col_maxima, EXPERT, split_axis=0, concat_axis=1, tiled=True)
    prob_sum = jnp.sum(probs, axis=1)
    all_ids = jnp.arange(num_experts, dtype=jnp.int32)
    counts = jnp.sum(
        (all_ids[:, None, None] == experts_here[None, :, :]).astype(jnp.float32), axis=(1, 2)
    )
    dev_ids = jnp.arange(num_devices, dtype=jnp.int32)
    sent_counts = jnp.sum(
        (dev_ids[:, None, None] == devices_here[None, :, :]).astype(jnp.float32), axis=(1, 2)
    )
    prob_sum, counts, sent_counts = (
        by_axis(prob_sum, DP_EXPERT),
        by_axis(counts, DP_EXPERT),
        by_axis(sent_counts, DP_EXPERT),
    )
    freq = counts * (num_experts / (TOP * total_tokens))
    prob = prob_sum / total_tokens
    dev_freq = jnp.mean(freq.reshape(num_devices, per_device), axis=1)
    dev_prob = jnp.sum(prob.reshape(num_devices, per_device), axis=1)
    sent = sent_counts * (num_devices / (DEV_TOP * total_tokens))
    balance = jnp.stack(
        [jnp.sum(freq * prob), jnp.sum(dev_freq * dev_prob), jnp.sum(sent * dev_prob)]
    )
    return (gates, device_max, balance)


def solution(mesh):
    torus = Mesh(mesh.devices.reshape(4, 2, 8, 4), ("dp_0", "dp_1", "expert_0", "expert_1"))
    return jax.shard_map(
        local,
        mesh=torus,
        in_specs=(P(None, DP_EXPERT), P(None, EXPERT), P(None, DP), P(None, DP)),
        out_specs=(P(None, DP), P(EXPERT, DP), P()),
        check_vma=False,
    )
```

profile of v0, /device:TPU:1, one launch (start us, length us, event | category | flops | bytes accessed | tf_op | source)
XLA Modules:
  0.0 191.8 jit_solution(3939025640600472953)
XLA Ops:
  7.2 0.0 copy-start
  7.2 0.0 all-gather.4.cloned.1.call-start
  7.2 12.0 %all-gather = bf16[4,5,5120]{2,1,0:T(8,128)(2,1)S(1)} all-gather(bf16[1,5,5120]{2,1,0:T(8,128)(2,1)} %bitcast.18), channel_id=1, replica_groups=mesh['dp_0'=4,'dp_1'=2,'expert_0'=8,'expert_1'=4] {'expert_1'}, dimensions={0}, use_global_device_ids=true | all-gather | bytes 256000 | tf_op jit(solution)/shard_map/all_gather | solution.py:16
  19.2 0.8 reshape.59
  20.0 0.0 all-gather.4.cloned.1.call-update
  20.0 41.2 %all-gather.4.cloned.1.call-done = bf16[8,20,5120]{2,1,0:T(8,128)(2,1)} async-done(((bf16[1,20,5120]{2,1,0:T(8,128)(2,1)}), bf16[8,20,5120]{2,1,0:T(8,128)(2,1)}) %all-gather.4.cloned.1.call-update) | async-done | bytes 1638416 | tf_op jit(solution)/shard_map/all_gather | solution.py:16
  61.2 1.7 reshape.60
  62.9 5.8 %fusion.4 = (f32[1024]{0:T(1024)S(1)}, f32[160,1024]{1,0:T(8,128)S(1)}) fusion(bf16[160,5120]{1,0:T(8,128)(2,1)S(1)} %reshape.60, bf16[5120,1024]{1,0:T(8,128)(2,1)} %param.4), kind=kOutput, calls=%fused_computation.20 | convolution fusion | flops 1677884416 | bytes 12783616 | tf_op jit(solution)/shard_map/dot_general | solution.py:49
  68.8 0.1 fusion.1
  68.9 0.2 fusion.2
  69.1 0.1 reshape.43
  69.2 0.3 reduce_max.19
  69.5 0.7 all_to_all.16
  70.3 6.6 %all-to-all-start.1 = ((f32[32,1,1024]{2,1,0:T(1,128)}), f32[32,1,1024]{2,1,0:T(1,128)S(1)}, u32[]{:S(2)}, u32[]{:S(2)}) async-start(f32[32,1,1024]{2,1,0:T(1,128)} %all_to_all.16), calls=%async_computation.1 | async-start | bytes 262144 | tf_op jit(solution)/shard_map/all_to_all | solution.py:61
  76.8 0.8 bitcast_or_fusion
  77.6 49.3 %gather_fusion = f32[6144]{0:T(1024)S(1)} fusion(f32[160,1024]{1,0:T(8,128)S(1)} %get-tuple-element.18, s32[6144]{0:T(1024)S(1)} %reshape.46), kind=kCustom, calls=%fused_computation | custom fusion | bytes 98304 | tf_op jit(solution)/shard_map/jit(take_along_axis)/gather | solution.py:58
  127.0 0.0 all-to-all-done.1
  127.0 1.1 broadcast_in_dim.7
  128.1 9.2 %all-to-all-start = ((f32[32,6,1024]{2,1,0:T(8,128)}), f32[32,6,1024]{2,1,0:T(8,128)S(1)}, u32[]{:S(2)}, u32[]{:S(2)}) async-start(f32[32,6,1024]{2,1,0:T(8,128)} %broadcast_in_dim.7), calls=%async_computation | async-start | bytes 2097152 | tf_op jit(solution)/shard_map/all_to_all | solution.py:28
  137.3 0.0 copy-done
  137.3 0.2 convert_reduce_fusion.1
  137.5 0.6 convert_reduce_fusion
  138.0 8.4 %all-reduce.2 = (f32[160]{0:T(256)S(1)}, f32[160]{0:T(256)S(1)}, f32[32]{0:T(128)S(1)}) all-reduce(f32[160]{0:T(256)S(1)} %get-tuple-element.17, f32[160]{0:T(256)S(1)} %convert_reduce_fusion, f32[32]{0:T(128)S(1)} %convert_reduce_fusion.1), channel_id=1, replica_groups=mesh['dp_0'=4,'dp_1'=2,'expert_0'=8,'expert_1'=4] {'dp_0'}, use_global_device_ids=true, to_apply=%region_9.10 | all-reduce | flops 352 | bytes 2816 | tf_op jit(solution)/shard_map/psum | solution.py:37
  146.4 10.2 %all-reduce.3 = (f32[160]{0:T(256)S(1)}, f32[160]{0:T(256)S(1)}, f32[32]{0:T(128)S(1)}) all-reduce(f32[160]{0:T(256)S(1)} %get-tuple-element.11, f32[160]{0:T(256)S(1)} %get-tuple-element.12, f32[32]{0:T(128)S(1)} %get-tuple-element.13), channel_id=1, replica_groups=mesh['dp_0'=4,'dp_1'=2,'expert_0'=8,'expert_1'=4] {'dp_1'}, use_global_device_ids=true, to_apply=%region_10.11 | all-reduce | flops 352 | bytes 2816 | tf_op jit(solution)/shard_map/psum | solution.py:37
  156.6 14.1 %all-reduce = (f32[160]{0:T(256)S(1)}, f32[160]{0:T(256)S(1)}, f32[32]{0:T(128)S(1)}) all-reduce(f32[160]{0:T(256)S(1)} %get-tuple-element.14, f32[160]{0:T(256)S(1)} %get-tuple-element.15, f32[32]{0:T(128)S(1)} %get-tuple-element.16), channel_id=1, replica_groups=mesh['dp_0'=4,'dp_1'=2,'expert_0'=8,'expert_1'=4] {'expert_0'}, use_global_device_ids=true, to_apply=%region_11.12 | all-reduce | flops 352 | bytes 2816 | tf_op jit(solution)/shard_map/psum | solution.py:37
  170.7 8.4 %all-reduce.1 = (f32[160]{0:T(256)S(1)}, f32[160]{0:T(256)S(1)}, f32[32]{0:T(128)S(1)}) all-reduce(f32[160]{0:T(256)S(1)} %get-tuple-element.5, f32[160]{0:T(256)S(1)} %get-tuple-element.6, f32[32]{0:T(128)S(1)} %get-tuple-element.7), channel_id=1, replica_groups=mesh['dp_0'=4,'dp_1'=2,'expert_0'=8,'expert_1'=4] {'expert_1'}, use_global_device_ids=true, to_apply=%region_12.13 | all-reduce | flops 352 | bytes 2816 | tf_op jit(solution)/shard_map/psum | solution.py:37
  179.1 0.6 multiply_reduce_fusion
  179.7 0.1 reshape.45
  179.8 0.1 reshape.44
  179.9 0.1 reduce_sum.86
  180.0 0.1 reduce_sum.85
  180.1 0.7 multiply_reduce_fusion.2
  180.8 2.5 %pad_maximum_fusion = f32[3]{0:T(128)} fusion(f32[1]{0:T(128)} %bitcast.8, f32[1]{0:T(128)} %bitcast.7, f32[1]{0:T(128)} %bitcast.6), kind=kLoop, calls=%fused_computation.12 | loop fusion | flops 6 | bytes 24 | tf_op jit(solution)/shard_map/stack | solution.py:81
  183.3 0.0 all-to-all-done
  183.3 1.0 copy.9
  184.3 0.7 copy.10
  (4 shorter events, 0.0 us)
Async XLA Ops:
  7.2 130.1 %copy-start = (s32[3,32768]{1,0:T(4,128)S(1)}, s32[3,32768]{1,0:T(4,128)}, u32[]{:S(2)}) copy-start(s32[3,32768]{1,0:T(4,128)} %param.6) | copy-start | bytes 1179652
  7.2 54.1 %all-gather.4.cloned.1.call-start = ((), (), s32[]{:S(2)}) async-start(), calls=%async_computation.2 | async-start | bytes 2211840 | tf_op jit(solution)/shard_map/all_gather | solution.py:16
  70.3 56.7 %all-to-all-start.1 = ((f32[32,1,1024]{2,1,0:T(1,128)}), f32[32,1,1024]{2,1,0:T(1,128)S(1)}, u32[]{:S(2)}, u32[]{:S(2)}) async-start(f32[32,1,1024]{2,1,0:T(1,128)} %all_to_all.16), calls=%async_computation.1 | async-start | bytes 262144 | tf_op jit(solution)/shard_map/all_to_all | solution.py:61
  128.1 55.2 %all-to-all-start = ((f32[32,6,1024]{2,1,0:T(8,128)}), f32[32,6,1024]{2,1,0:T(8,128)S(1)}, u32[]{:S(2)}, u32[]{:S(2)}) async-start(f32[32,6,1024]{2,1,0:T(8,128)} %broadcast_in_dim.7), calls=%async_computation | async-start | bytes 2097152 | tf_op jit(solution)/shard_map/all_to_all | solution.py:28
Sparse Core Ops, SparseCore 0:
  20.2 41.0 all-gather.3
where the time goes:
time: 195 us; the launch traced here: 192 us
  local copies, waits for them, and re-layouts  55.6 us (29%)
  blocking collectives  53 us (27%)
  waiting for transfers between devices  41.2 us (21%)
  starting transfers between devices  15.8 us (8%)
  between operations  14.2 us (7%)
  other arithmetic  6.14 us (3%)
  matrix products  5.85 us (3%)
    gather x3, local copies, waits for them, and re-layouts, local(): col_gates = jnp.take_along_axis(probs, experts_here, axis=0)  49.3 us
    all_gather x1, waiting for transfers between devices, gathered_by_axis(): x = lax.all_gather(x, axis, axis=dim, tiled=True)  41.2 us
    psum x4, blocking collectives, by_axis(): x = lax.psum(x, axis)  41 us
    all_gather x1, blocking collectives, gathered_by_axis(): x = lax.all_gather(x, axis, axis=dim, tiled=True)  12 us
    all_to_all x1, starting transfers between devices, sent_to_all(): lax.all_to_all(jnp.broadcast_to(x[None], (length, *x.shape)), axis, 0, 0,...  9.22 us
    all_to_all x1, starting transfers between devices, local(): lax.all_to_all(col_maxima, EXPERT, split_axis=0, concat_axis=1, tiled=True)  6.55 us
    dot_general x1, matrix products, local(): jnp.dot(tokens.T, gathered_by_axis(router, EXPERT, 1), preferred_element_...  5.85 us
    unnamed x6, local copies, waits for them, and re-layouts  4.1 us
  transfers between devices with their start and end apart: 3, of which 1 were waited for; matrix products, arithmetic and copies ran while one was open for 29% of the time, Pallas kernels for 0%

commit v1 on v0

v1 whole, which is shorter than its diff:
```python
import functools

import jax
import jax.numpy as jnp
from jax import lax
from jax.experimental import pallas as pl
from jax.experimental.pallas import tpu as pltpu
from jax.sharding import Mesh
from jax.sharding import PartitionSpec as P

TOP = 6
DEV_TOP = 3
EXPERT = ("expert_0", "expert_1")
DP = ("dp_0", "dp_1")
DP_EXPERT = ("dp_0", "dp_1", "expert_0", "expert_1")
BLOCK = 256
LANES = 128


def sent_to_all(x, axis):
    length = lax.axis_size(axis)
    return lax.all_to_all(jnp.broadcast_to(x[None], (length, *x.shape)), axis, 0, 0, tiled=True)


def lane_sum(x):
    parts = [x[:, i : i + LANES] for i in range(0, x.shape[1], LANES)]
    return functools.reduce(jnp.add, parts)


def route_kernel(num_devices, per_device, where, router, tokens, picks, devs, out, prob_acc, count_acc, sent_acc):
    step = pl.program_id(0)
    num_experts = num_devices * per_device
    block = tokens.shape[1]

    @pl.when(step == 0)
    def _():
        prob_acc[...] = jnp.zeros_like(prob_acc)
        count_acc[...] = jnp.zeros_like(count_acc)
        sent_acc[...] = jnp.zeros_like(sent_acc)

    scores = jnp.dot(router[...], tokens[...], preferred_element_type=jnp.float32)
    peak = jnp.max(scores, axis=0, keepdims=True)
    raised = jnp.exp(scores - peak)
    probs = raised / jnp.sum(raised, axis=0, keepdims=True)
    prob_acc[...] += lane_sum(probs)
    rows = lax.broadcasted_iota(jnp.int32, (num_experts, block), 0)
    ids = (rows % num_devices) * per_device + rows // num_devices
    chosen = []
    hits = jnp.zeros((num_experts, block), jnp.float32)
    for k in range(TOP):
        mask = ids == picks[k : k + 1, :]
        chosen.append(jnp.sum(jnp.where(mask, probs, 0.0), axis=0, keepdims=True))
        hits += jnp.where(mask, 1.0, 0.0)
    count_acc[...] += lane_sum(hits)
    dev_ids = lax.broadcasted_iota(jnp.int32, (num_devices, block), 0)
    sent = jnp.zeros((num_devices, block), jnp.float32)
    for k in range(DEV_TOP):
        sent += jnp.where(dev_ids == devs[k : k + 1, :], 1.0, 0.0)
    sent_acc[...] += lane_sum(sent)
    gates = jnp.concatenate(chosen, axis=0)
    maxima = functools.reduce(
        jnp.maximum, [probs[j * num_devices : (j + 1) * num_devices] for j in range(per_device)]
    )
    cols = pl.ds(step * block, block)
    for d in range(num_devices):
        out[d, 0:TOP, cols] = gates
        out[d, TOP : TOP + 1, cols] = maxima[d : d + 1]

    @pl.when(step == pl.num_programs(0) - 1)
    def _():
        def row(acc, width):
            line = jnp.sum(acc[...].T, axis=0, keepdims=True)
            return jnp.concatenate([line, jnp.zeros((1, width - line.shape[1]), jnp.float32)], axis=1)

        sums = jnp.concatenate(
            [row(prob_acc, 256), row(count_acc, 256), row(sent_acc, 512)], axis=1
        )
        for d in range(num_devices):
            out[d, TOP + 1 : TOP + 2, :] = sums


def spread_kernel(recv, gates, maxima, sums):
    num, _, share = recv.shape
    total = jnp.zeros((1, share), jnp.float32)
    for d in range(num):
        cols = slice(d * share, (d + 1) * share)
        gates[:, cols] = recv[d, 0:TOP, :]
        maxima[:, cols] = recv[d, TOP : TOP + 1, :]
        total += recv[d, TOP + 1 : TOP + 2, :]
    sums[...] = jnp.broadcast_to(total, sums.shape)


def local(tokens, router, device_pick, expert_pick):
    features, share = tokens.shape
    num_devices = lax.axis_size(EXPERT)
    per_device = router.shape[1]
    num_experts = per_device * num_devices
    total_tokens = share * num_devices * lax.axis_size(DP)
    my_index = lax.axis_index(EXPERT)
    core = lax.axis_index("dp_1")
    half = features // 2

    mine = lax.dynamic_slice_in_dim(router.T, core * half, half, 1)
    packed = sent_to_all(mine.reshape(per_device * half // LANES, LANES), EXPERT)
    ours = packed.reshape(num_devices, per_device, half).transpose(1, 0, 2).reshape(num_experts, half)
    theirs = lax.ppermute(ours, "dp_1", [(0, 1), (1, 0)])
    first = jnp.where(core == 0, ours, theirs)
    second = jnp.where(core == 0, theirs, ours)
    full = jnp.concatenate([first, second], axis=1)

    steps = share // BLOCK
    where = my_index.astype(jnp.int32).reshape(1)
    msg = pl.pallas_call(
        functools.partial(route_kernel, num_devices, per_device),
        out_shape=jax.ShapeDtypeStruct((num_devices, TOP + 2, share), jnp.float32),
        grid_spec=pltpu.PrefetchScalarGridSpec(
            num_scalar_prefetch=1,
            grid=(steps,),
            in_specs=[
                pl.BlockSpec((num_experts, features), lambda i, w: (0, 0)),
                pl.BlockSpec((features, BLOCK), lambda i, w: (0, i)),
                pl.BlockSpec((TOP, BLOCK), lambda i, w: (0, w[0] * steps + i)),
                pl.BlockSpec((DEV_TOP, BLOCK), lambda i, w: (0, w[0] * steps + i)),
            ],
            out_specs=pl.BlockSpec((num_devices, TOP + 2, share), lambda i, w: (0, 0, 0)),
            scratch_shapes=[
                pltpu.VMEM((num_experts, LANES), jnp.float32),
                pltpu.VMEM((num_experts, LANES), jnp.float32),
                pltpu.VMEM((num_devices, LANES), jnp.float32),
            ],
        ),
        compiler_params=pltpu.CompilerParams(
            dimension_semantics=("arbitrary",), vmem_limit_bytes=32 * 1024 * 1024
        ),
        name="route",
    )(where, full, tokens, expert_pick, device_pick)

    recv = lax.all_to_all(msg, EXPERT, 0, 0, tiled=True)
    gates, device_max, sums = pl.pallas_call(
        spread_kernel,
        out_shape=(
            jax.ShapeDtypeStruct((TOP, share * num_devices), jnp.float32),
            jax.ShapeDtypeStruct((1, share * num_devices), jnp.float32),
            jax.ShapeDtypeStruct((8, share), jnp.float32),
        ),
        compiler_params=pltpu.CompilerParams(vmem_limit_bytes=16 * 1024 * 1024),
        name="spread",
    )(recv)
    sums = jnp.sum(sent_to_all(sums[0:1, 0:768].reshape(6, LANES), DP), axis=0).reshape(768)
    prob_sum = sums[0:num_experts]
    counts = sums[256 : 256 + num_experts]
    sent_counts = sums[512 : 512 + num_devices]
    freq = counts * (num_experts / (TOP * total_tokens))
    prob = prob_sum / total_tokens
    dev_freq = jnp.mean(freq.reshape(per_device, num_devices), axis=0)
    dev_prob = jnp.sum(prob.reshape(per_device, num_devices), axis=0)
    sent = sent_counts * (num_devices / (DEV_TOP * total_tokens))
    balance = jnp.stack(
        [jnp.sum(freq * prob), jnp.sum(dev_freq * dev_prob), jnp.sum(sent * dev_prob)]
    )
    return (gates, device_max, balance)


def solution(mesh):
    torus = Mesh(mesh.devices.reshape(4, 2, 8, 4), ("dp_0", "dp_1", "expert_0", "expert_1"))
    return jax.shard_map(
        local,
        mesh=torus,
        in_specs=(P(None, DP_EXPERT), P(None, EXPERT), P(None, DP), P(None, DP)),
        out_specs=(P(None, DP), P(EXPERT, DP), P()),
        check_vma=False,
    )
```

time: 195 us -> 101 us (0.52); the launches traced: 192 us -> 100 us
  local copies, waits for them, and re-layouts: 55.6 us -> 7.47 us
  waiting for transfers between devices: 41.2 us -> 1.96 us
  blocking collectives: 53 us -> 76.6 us
  between operations: 14.2 us -> 0.72 us
  starting transfers between devices: 15.8 us -> 2.98 us
  Pallas kernels: 0 us -> 6.46 us
  matrix products: 5.85 us -> 0 us
  other arithmetic: 6.14 us -> 4.15 us
    all_to_all x0 -> x3, blocking collectives: none -> 76.6 us  [the longest x2 45.6 us: sent_to_all(): lax.all_to_all(jnp.broadcast_to(x[None], (length, *x.shape)), axis, 0, 0,...]
    gather x3 -> x0, local copies, waits for them, and re-layouts: 49.3 us -> none  [local(): col_gates = jnp.take_along_axis(probs, experts_here, axis=0)]
    all_gather x1 -> x0, waiting for transfers between devices: 41.2 us -> none  [gathered_by_axis(): x = lax.all_gather(x, axis, axis=dim, tiled=True)]
    psum x4 -> x0, blocking collectives: 41 us -> none  [by_axis(): x = lax.psum(x, axis)]
    all_to_all x2 -> x0, starting transfers between devices: 15.8 us -> none  [the longest x1 9.22 us: sent_to_all(): lax.all_to_all(jnp.broadcast_to(x[None], (length, *x.shape)), axis, 0, 0,...]
    all_gather x1 -> x0, blocking collectives: 12 us -> none  [gathered_by_axis(): x = lax.all_gather(x, axis, axis=dim, tiled=True)]
    pallas_call x0 -> x2, Pallas kernels: none -> 6.46 us  [the longest x1 5.34 us: local(): pl.pallas_call(functools.partial(route_kernel, num_devices, per_device),...]
    dot_general x1 -> x0, matrix products: 5.85 us -> none  [local(): jnp.dot(tokens.T, gathered_by_axis(router, EXPERT, 1), preferred_element_...]
  transfers between devices with their start and end apart: 3 -> 1, of which waited for: 1 -> 1; matrix products, arithmetic and copies ran while one was open for 29% -> 0% of each run, Pallas kernels for 0% -> 0%
where the time goes in v1:
time: 101 us; the launch traced here: 100 us
  blocking collectives  76.6 us (76%)
  local copies, waits for them, and re-layouts  7.47 us (7%)
  Pallas kernels  6.46 us (6%)
  other arithmetic  4.15 us (4%)
  starting transfers between devices  2.98 us (3%)
  waiting for transfers between devices  1.96 us (2%)
    all_to_all x2, blocking collectives, sent_to_all(): lax.all_to_all(jnp.broadcast_to(x[None], (length, *x.shape)), axis, 0, 0,...  45.6 us
    all_to_all x1, blocking collectives, local(): recv = lax.all_to_all(msg, EXPERT, 0, 0, tiled=True)  31.1 us
    unnamed x8, local copies, waits for them, and re-layouts  6.02 us
    pallas_call x1, Pallas kernels, local(): pl.pallas_call(functools.partial(route_kernel, num_devices, per_device),...  5.34 us
    ppermute x1, starting transfers between devices, local(): theirs = lax.ppermute(ours, 'dp_1', [(0, 1), (1, 0)])  2.98 us
    another operation x1, other arithmetic, local(): jnp.stack([jnp.sum(freq * prob), jnp.sum(dev_freq * dev_prob), jnp.sum(se...  2.47 us
  transfers between devices with their start and end apart: 1, of which 1 were waited for; matrix products, arithmetic and copies ran while one was open for 0% of the time, Pallas kernels for 0%

profile of v1, /device:TPU:1, one launch (start us, length us, event | category | flops | bytes accessed | tf_op | source)
XLA Modules:
  0.0 100.4 jit_solution(13924817080722444257)
XLA Ops:
  0.6 0.0 copy-start
  0.7 0.9 copy-done
  1.5 0.1 broadcast_in_dim.14
  1.6 0.1 broadcast_in_dim.15
  1.7 34.1 %all_to_all.15 = bf16[32,100,128]{2,1,0:T(8,128)(2,1)S(1)} all-to-all(bf16[32,100,128]{2,1,0:T(8,128)(2,1)S(1)} %broadcast_in_dim.15), channel_id=1, replica_groups=mesh['dp_0'=4,'dp_1'=2,'expert_0'=8,'expert_1'=4] {'expert_0','expert_1'}, dimensions={0} | all-to-all | bytes 1638400 | tf_op jit(solution)/shard_map/all_to_all | solution.py:22
  35.8 0.9 reshape.27
  36.7 0.3 copy.9
  37.0 3.0 %collective-permute-start = (bf16[160,2560]{1,0:T(8,128)(2,1)S(1)}, bf16[160,2560]{1,0:T(8,128)(2,1)S(1)}, u32[]{:S(2)}, u32[]{:S(2)}) collective-permute-start(bf16[160,2560]{1,0:T(8,128)(2,1)S(1)} %bitcast.13), channel_id=1, source_target_pairs={{0,32},{32,0},{1,33},{33,1},{2,34},{34,2},{3,35},{35,3},{4,36},{36... | collective-permute-start | bytes 2457608 | tf_op jit(solution)/shard_map/ppermute | solution.py:106
  40.0 2.0 %collective-permute-done = bf16[160,2560]{1,0:T(8,128)(2,1)S(1)} collective-permute-done((bf16[160,2560]{1,0:T(8,128)(2,1)S(1)}, bf16[160,2560]{1,0:T(8,128)(2,1)S(1)}, u32[]{:S(2)}, u32[]{:S(2)}) %collective-permute-start) | collective-permute-done | bytes 819232 | tf_op jit(solution)/shard_map/ppermute | solution.py:106
  41.9 0.2 broadcast_select_fusion.1
  42.1 0.0 copy-start.2
  42.1 0.0 copy-start.3
  42.1 0.2 pad_maximum_fusion.router
  42.3 1.0 %copy-done.2 = s32[6,32768]{1,0:T(8,128)S(1)} copy-done((s32[6,32768]{1,0:T(8,128)S(1)}, s32[6,32768]{1,0:T(8,128)}, u32[]{:S(2)}) %copy-start.2) | copy-done | bytes 786456
  43.3 0.1 copy-done.3
  43.5 0.0 copy-start.1
  43.5 4.0 %copy-done.1 = bf16[5120,1024]{1,0:T(8,128)(2,1)S(1)} copy-done((bf16[5120,1024]{1,0:T(8,128)(2,1)S(1)}, bf16[5120,1024]{1,0:T(8,128)(2,1)}, u32[]{:S(2)}) %copy-start.1) | copy-done | bytes 10485784
  47.4 5.3 %route.1 = f32[32,8,1024]{2,1,0:T(8,128)S(1)} custom-call(s32[1]{0:T(128)} %bitcast.where, bf16[160,5120]{1,0:T(8,128)(2,1)S(1)} %pad_maximum_fusion.router, bf16[5120,1024]{1,0:T(8,128)(2,1)S(1)} %copy-done.1, s32[6,32768]{1,0:T(8,128)S(1)} %copy-done.2, s32[3,32768]{1,0:T(4,128)S(1)} %copy-done.3), custom_call_target="tpu_custom_call" | custom-call | tf_op jit(solution)/shard_map/route/pallas_call | solution.py:113
  52.8 31.1 %all_to_all.16.recv = f32[32,8,1024]{2,1,0:T(8,128)S(1)} all-to-all(f32[32,8,1024]{2,1,0:T(8,128)S(1)} %route.1), channel_id=1, replica_groups=mesh['dp_0'=4,'dp_1'=2,'expert_0'=8,'expert_1'=4] {'expert_0','expert_1'}, dimensions={0} | all-to-all | bytes 2097152 | tf_op jit(solution)/shard_map/all_to_all | solution.py:138
  83.9 1.1 %spread.1 = (f32[6,32768]{1,0:T(8,128)}, f32[1,32768]{1,0:T(1,128)}, f32[8,1024]{1,0:T(8,128)S(1)}) custom-call(f32[32,8,1024]{2,1,0:T(8,128)S(1)} %all_to_all.16.recv), custom_call_target="tpu_custom_call" | custom-call | tf_op jit(solution)/shard_map/spread/pallas_call | solution.py:139
  85.0 11.5 %all_to_all.17 = f32[8,6,128]{2,1,0:T(8,128)S(1)} all-to-all(f32[8,6,128]{2,1,0:T(8,128)S(1)} %broadcast_in_dim.17), channel_id=1, replica_groups=mesh['dp_0'=4,'dp_1'=2,'expert_0'=8,'expert_1'=4] {'dp_0','dp_1'}, dimensions={0} | all-to-all | bytes 49152 | tf_op jit(solution)/shard_map/all_to_all | solution.py:22
  96.5 0.1 slice.23
  96.6 0.6 multiply_reduce_fusion
  97.2 0.7 multiply_reduce_fusion.2
  97.9 2.5 %pad_maximum_fusion.1 = f32[3]{0:T(128)} fusion(f32[1]{0:T(128)} %bitcast.7, f32[1]{0:T(128)} %bitcast.6, f32[1]{0:T(128)} %bitcast.5), kind=kLoop, calls=%fused_computation.10 | loop fusion | flops 6 | bytes 24 | tf_op jit(solution)/shard_map/stack | solution.py:158
  (5 shorter events, 0.1 us)
Async XLA Ops:
  0.6 0.9 copy-start
  37.0 4.9 %collective-permute-start = (bf16[160,2560]{1,0:T(8,128)(2,1)S(1)}, bf16[160,2560]{1,0:T(8,128)(2,1)S(1)}, u32[]{:S(2)}, u32[]{:S(2)}) collective-permute-start(bf16[160,2560]{1,0:T(8,128)(2,1)S(1)} %bitcast.13), channel_id=1, source_target_pairs={{0,32},{32,0},{1,33},{33,1},{2,34},{34,2},{3,35},{35,3},{4,36},{36... | collective-permute-start | bytes 2457608 | tf_op jit(solution)/shard_map/ppermute | solution.py:106
  42.1 1.2 %copy-start.2 = (s32[6,32768]{1,0:T(8,128)S(1)}, s32[6,32768]{1,0:T(8,128)}, u32[]{:S(2)}) copy-start(s32[6,32768]{1,0:T(8,128)} %picks.1) | copy-start | bytes 2359300
  42.1 1.3 %copy-start.3 = (s32[3,32768]{1,0:T(4,128)S(1)}, s32[3,32768]{1,0:T(4,128)}, u32[]{:S(2)}) copy-start(s32[3,32768]{1,0:T(4,128)} %devs.1) | copy-start | bytes 1179652
  43.5 4.0 %copy-start.1 = (bf16[5120,1024]{1,0:T(8,128)(2,1)S(1)}, bf16[5120,1024]{1,0:T(8,128)(2,1)}, u32[]{:S(2)}) copy-start(bf16[5120,1024]{1,0:T(8,128)(2,1)} %tokens.1) | copy-start | bytes 31457284

commit v2 on v1

--- a/solution.py
+++ b/solution.py
@@ -15,6 +15,10 @@
 DP_EXPERT = ("dp_0", "dp_1", "expert_0", "expert_1")
 BLOCK = 256
 LANES = 128
+ROWS = 8
+TOP_CODE = 65535.0
+MIDDLE = 32768
+TINY = 1e-30
 
 
 def sent_to_all(x, axis):
@@ -25,12 +29,47 @@
 def lane_sum(x):
     parts = [x[:, i : i + LANES] for i in range(0, x.shape[1], LANES)]
     return functools.reduce(jnp.add, parts)
+
+
+def fourth(x):
+    return jnp.square(jnp.square(x))
+
+
+def eighth(x):
+    return jnp.square(fourth(x))
+
+
+def eighth_root(x):
+    return jnp.sqrt(jnp.sqrt(jnp.sqrt(x)))
+
+
+def unit(code):
+    return code * (1.0 / TOP_CODE)
+
+
+def step_scale(code):
+    return jnp.maximum(eighth(unit(code)), TINY) * (1.0 / TOP_CODE)
+
+
+def coded_pair(x, limit):
+    coarse = jnp.minimum(jnp.floor(eighth_root(x * (1.0 / limit)) * TOP_CODE), TOP_CODE)
+    base = eighth(unit(coarse)) * limit
+    rest = jnp.where(base > 0.0, (x - base) / jnp.maximum(base, TINY), 0.0)
+    fine = jnp.round(jnp.clip(rest * coarse * (1.0 / 16.0), 0.0, 1.0) * TOP_CODE)
+    return coarse, fine
+
+
+def decoded_pair(coarse, fine, limit):
+    base = eighth(unit(coarse)) * limit
+    return base * (1.0 + unit(fine) * 16.0 / jnp.maximum(coarse, 1.0))
 
 
 def route_kernel(num_devices, per_device, where, router, tokens, picks, devs, out, prob_acc, count_acc, sent_acc):
     step = pl.program_id(0)
     num_experts = num_devices * per_device
     block = tokens.shape[1]
+    tiles = block // LANES
+    share = block * pl.num_programs(0)
 
     @pl.when(step == 0)
     def _():
@@ -57,37 +96,91 @@
     for k in range(DEV_TOP):
         sent += jnp.where(dev_ids == devs[k : k + 1, :], 1.0, 0.0)
     sent_acc[...] += lane_sum(sent)
-    gates = jnp.concatenate(chosen, axis=0)
+
+    largest = functools.reduce(jnp.maximum, chosen)
+    scale = jnp.minimum(jnp.floor(eighth_root(largest) * TOP_CODE) + 1.0, TOP_CODE)
+    inverse = 1.0 / step_scale(scale)
+    codes = [jnp.minimum(jnp.round(g * inverse), TOP_CODE) for g in chosen]
+    lines = jnp.concatenate([*codes, scale, scale], axis=0).astype(jnp.int32) - MIDDLE
     maxima = functools.reduce(
         jnp.maximum, [probs[j * num_devices : (j + 1) * num_devices] for j in range(per_device)]
     )
-    cols = pl.ds(step * block, block)
+    max_codes = jnp.round(jnp.sqrt(jnp.sqrt(maxima)) * TOP_CODE).astype(jnp.int32) - MIDDLE
+    max_codes = jnp.minimum(max_codes, MIDDLE - 1)
+    stacked = jnp.concatenate([lines[:, j * LANES : (j + 1) * LANES] for j in range(tiles)], axis=0)
+    last = lax.broadcasted_iota(jnp.int32, stacked.shape, 0) % ROWS == ROWS - 1
+    here = pl.ds(pl.multiple_of(step * tiles * ROWS, tiles * ROWS), tiles * ROWS)
     for d in range(num_devices):
-        out[d, 0:TOP, cols] = gates
-        out[d, TOP : TOP + 1, cols] = maxima[d : d + 1]
+        line = jnp.concatenate(
+            [
+                jnp.broadcast_to(max_codes[d : d + 1, j * LANES : (j + 1) * LANES], (ROWS, LANES))
+                for j in range(tiles)
+            ],
+            axis=0,
+        )
+        out[d, here, :] = jnp.where(last, line, stacked).astype(jnp.int16)
 
     @pl.when(step == pl.num_programs(0) - 1)
     def _():
-        def row(acc, width):
+        def row(acc):
             line = jnp.sum(acc[...].T, axis=0, keepdims=True)
-            return jnp.concatenate([line, jnp.zeros((1, width - line.shape[1]), jnp.float32)], axis=1)
-
+            missing = 2 * LANES - line.shape[1]
+            line = jnp.concatenate([line, jnp.zeros((1, missing), jnp.float32)], axis=1)
+            return line[:, :LANES], line[:, LANES:]
+
+        low, high = row(prob_acc)
+        low_coarse, low_fine = coded_pair(low, share)
+        high_coarse, high_fine = coded_pair(high, share)
+        count_low, count_high = row(count_acc)
+        sent_low, sent_high = row(sent_acc)
         sums = jnp.concatenate(
-            [row(prob_acc, 256), row(count_acc, 256), row(sent_acc, 512)], axis=1
+            [low_coarse, high_coarse, low_fine, high_fine, count_low, count_high, sent_low, sent_high], axis=0
         )
+        sums = (sums.astype(jnp.int32) - MIDDLE).astype(jnp.int16)
         for d in range(num_devices):
-            out[d, TOP + 1 : TOP + 2, :] = sums
+            out[d, pl.ds(share // LANES * ROWS, ROWS), :] = sums
 
 
 def spread_kernel(recv, gates, maxima, sums):
-    num, _, share = recv.shape
-    total = jnp.zeros((1, share), jnp.float32)
+    num, rows, _ = recv.shape
+    tiles = rows // ROWS - 1
+    share = tiles * LANES
+    total = jnp.zeros((ROWS, LANES), jnp.float32)
     for d in range(num):
-        cols = slice(d * share, (d + 1) * share)
-        gates[:, cols] = recv[d, 0:TOP, :]
-        maxima[:, cols] = recv[d, TOP : TOP + 1, :]
-        total += recv[d, TOP + 1 : TOP + 2, :]
-    sums[...] = jnp.broadcast_to(total, sums.shape)
+        codes = recv[d].astype(jnp.int32).astype(jnp.float32) + float(MIDDLE)
+        for j in range(tiles):
+            tile = codes[j * ROWS : (j + 1) * ROWS]
+            cols = slice(d * share + j * LANES, d * share + (j + 1) * LANES)
+            gates[:, cols] = tile[0:TOP] * step_scale(tile[TOP : TOP + 1])
+            maxima[:, cols] = fourth(unit(tile[TOP + 1 : TOP + 2]))
+        tile = codes[tiles * ROWS :]
+        probs = decoded_pair(tile[0:2], tile[2:4], share)
+        total += jnp.concatenate([probs, tile[4:8], jnp.zeros((2, LANES), jnp.float32)], axis=0)
+    sums[...] = total
+
+
+def balance_kernel(num_devices, per_device, total_tokens, where, own, first, second, third, out, slots):
+    place = where[0]
+    for k, part in enumerate((own, first, second, third)):
+        slots[(place + 4 - k) % 4] = part[...]
+    total = (slots[0] + slots[1]) + (slots[2] + slots[3])
+    num_experts = num_devices * per_device
+    prob = jnp.concatenate([total[0:1], total[1:2]], axis=1)[:, :num_experts] / total_tokens
+    freq = jnp.concatenate([total[2:3], total[3:4]], axis=1)[:, :num_experts] * (
+        num_experts / (TOP * total_tokens)
+    )
+    sent = total[4:5, :num_devices] * (num_devices / (DEV_TOP * total_tokens))
+
+    def by_device(x):
+        return functools.reduce(
+            jnp.add, [x[:, j * num_devices : (j + 1) * num_devices] for j in range(per_device)]
+        )
+
+    dev_prob = by_device(prob)
+    dev_freq = by_device(freq) / per_device
+    losses = [jnp.sum(a * b, axis=1, keepdims=True) for a, b in ((freq, prob), (dev_freq, dev_prob), (sent, dev_prob))]
+    lane = lax.broadcasted_iota(jnp.int32, (1, LANES), 1)
+    out[...] = jnp.where(lane == 0, losses[0], jnp.where(lane == 1, losses[1], losses[2]))
 
 
 def local(tokens, router, device_pick, expert_pick):
@@ -110,9 +203,10 @@
 
     steps = share // BLOCK
     where = my_index.astype(jnp.int32).reshape(1)
+    rows = (share // LANES + 1) * ROWS
     msg = pl.pallas_call(
         functools.partial(route_kernel, num_devices, per_device),
-        out_shape=jax.ShapeDtypeStruct((num_devices, TOP + 2, share), jnp.float32),
+        out_shape=jax.ShapeDtypeStruct((num_devices, rows, LANES), jnp.int16),
         grid_spec=pltpu.PrefetchScalarGridSpec(
             num_scalar_prefetch=1,
             grid=(steps,),
@@ -122,7 +216,7 @@
                 pl.BlockSpec((TOP, BLOCK), lambda i, w: (0, w[0] * steps + i)),
                 pl.BlockSpec((DEV_TOP, BLOCK), lambda i, w: (0, w[0] * steps + i)),
             ],
-            out_specs=pl.BlockSpec((num_devices, TOP + 2, share), lambda i, w: (0, 0, 0)),
+            out_specs=pl.BlockSpec((num_devices, rows, LANES), lambda i, w: (0, 0, 0)),
             scratch_shapes=[
                 pltpu.VMEM((num_experts, LANES), jnp.float32),
                 pltpu.VMEM((num_experts, LANES), jnp.float32),
@@ -130,7 +224,7 @@
             ],
         ),
         compiler_params=pltpu.CompilerParams(
-            dimension_semantics=("arbitrary",), vmem_limit_bytes=32 * 1024 * 1024
+            dimension_semantics=("arbitrary",), vmem_limit_bytes=52 * 1024 * 1024
         ),
         name="route",
     )(where, full, tokens, expert_pick, device_pick)
@@ -141,24 +235,30 @@
         out_shape=(
             jax.ShapeDtypeStruct((TOP, share * num_devices), jnp.float32),
             jax.ShapeDtypeStruct((1, share * num_devices), jnp.float32),
-            jax.ShapeDtypeStruct((8, share), jnp.float32),
+            jax.ShapeDtypeStruct((ROWS, LANES), jnp.float32),
         ),
         compiler_params=pltpu.CompilerParams(vmem_limit_bytes=16 * 1024 * 1024),
         name="spread",
     )(recv)
-    sums = jnp.sum(sent_to_all(sums[0:1, 0:768].reshape(6, LANES), DP), axis=0).reshape(768)
-    prob_sum = sums[0:num_experts]
-    counts = sums[256 : 256 + num_experts]
-    sent_counts = sums[512 : 512 + num_devices]
-    freq = counts * (num_experts / (TOP * total_tokens))
-    prob = prob_sum / total_tokens
-    dev_freq = jnp.mean(freq.reshape(per_device, num_devices), axis=0)
-    dev_prob = jnp.sum(prob.reshape(per_device, num_devices), axis=0)
-    sent = sent_counts * (num_devices / (DEV_TOP * total_tokens))
-    balance = jnp.stack(
-        [jnp.sum(freq * prob), jnp.sum(dev_freq * dev_prob), jnp.sum(sent * dev_prob)]
-    )
-    return (gates, device_max, balance)
+    chip = sums + lax.ppermute(sums, "dp_1", [(0, 1), (1, 0)])
+    length = lax.axis_size("dp_0")
+    others = [
+        lax.ppermute(chip, "dp_0", [(i, (i + k) % length) for i in range(length)]) for k in range(1, length)
+    ]
+    balance = pl.pallas_call(
+        functools.partial(balance_kernel, num_devices, per_device, total_tokens),
+        out_shape=jax.ShapeDtypeStruct((1, LANES), jnp.float32),
+        grid_spec=pltpu.PrefetchScalarGridSpec(
+            num_scalar_prefetch=1,
+            grid=(1,),
+            in_specs=[pl.BlockSpec((ROWS, LANES), lambda i, w: (0, 0))] * 4,
+            out_specs=pl.BlockSpec((1, LANES), lambda i, w: (0, 0)),
+            scratch_shapes=[pltpu.VMEM((4, ROWS, LANES), jnp.float32)],
+        ),
+        compiler_params=pltpu.CompilerParams(vmem_limit_bytes=1024 * 1024),
+        name="balance",
+    )(lax.axis_index("dp_0").astype(jnp.int32).reshape(1), chip, *others)
+    return (gates, device_max, balance[0, 0:3])
 
 
 def solution(mesh):

time: 101 us -> 85.5 us (0.85)
  blocking collectives: 76.6 us -> 56.5 us
  starting transfers between devices: 2.98 us -> 10.1 us
  local copies, waits for them, and re-layouts: 7.47 us -> 2.76 us
  Pallas kernels: 6.46 us -> 9.18 us
  other arithmetic: 4.15 us -> 1.52 us
  waiting for transfers between devices: 1.96 us -> 4.38 us
    all_to_all x2 -> x1, blocking collectives: 45.6 us -> 34.1 us  [sent_to_all(): lax.all_to_all(jnp.broadcast_to(x[None], (length, *x.shape)), axis, 0, 0,...]
    all_to_all x1, blocking collectives: 31.1 us -> 22.4 us  [local(): recv = lax.all_to_all(msg, EXPERT, 0, 0, tiled=True)]
    ppermute x0 -> x4, starting transfers between devices: none -> 7.17 us  [the longest x3 4.82 us: local(): lax.ppermute(chip, 'dp_0', [(i, (i + k) % length) for i in range(length)])]
    unnamed x8 -> x4, local copies, waits for them, and re-layouts: 6.02 us -> 0.89 us
    another operation x1 -> x0, other arithmetic: 2.47 us -> none  [local(): jnp.stack([jnp.sum(freq * prob), jnp.sum(dev_freq * dev_prob), jnp.sum(se...]
    ppermute x0 -> x4, waiting for transfers between devices: none -> 2.42 us  [the longest x3 1.59 us: local(): lax.ppermute(chip, 'dp_0', [(i, (i + k) % length) for i in range(length)])]
    pallas_call x1, Pallas kernels: 5.34 us -> 7.4 us  [local(): pl.pallas_call(functools.partial(route_kernel, num_devices, per_device),...]
    reduce_sum x4 -> x0, other arithmetic: 1.35 us -> none  [the longest x1 0.68 us: local(): jnp.sum(dev_freq * dev_prob)]
  transfers between devices with their start and end apart: 1 -> 5, of which waited for: 1 -> 4; matrix products, arithmetic and copies ran while one was open for 0% -> 0% of each run, Pallas kernels for 0% -> 0%
where the time goes in v2:
time: 85.5 us; the launch traced here: 85.2 us
  blocking collectives  56.5 us (66%)
  starting transfers between devices  10.1 us (12%)
  Pallas kernels  9.18 us (11%)
  waiting for transfers between devices  4.38 us (5%)
  local copies, waits for them, and re-layouts  2.76 us (3%)
  other arithmetic  1.52 us (2%)
    all_to_all x1, blocking collectives, sent_to_all(): lax.all_to_all(jnp.broadcast_to(x[None], (length, *x.shape)), axis, 0, 0,...  34.1 us
    all_to_all x1, blocking collectives, local(): recv = lax.all_to_all(msg, EXPERT, 0, 0, tiled=True)  22.4 us
    pallas_call x1, Pallas kernels, local(): pl.pallas_call(functools.partial(route_kernel, num_devices, per_device),...  7.4 us
    ppermute x3, starting transfers between devices, local(): lax.ppermute(chip, 'dp_0', [(i, (i + k) % length) for i in range(length)])  4.82 us
    ppermute x1, starting transfers between devices, local(): theirs = lax.ppermute(ours, 'dp_1', [(0, 1), (1, 0)])  2.98 us
    ppermute x1, starting transfers between devices, local(): chip = sums + lax.ppermute(sums, 'dp_1', [(0, 1), (1, 0)])  2.35 us
    ppermute x1, waiting for transfers between devices, local(): theirs = lax.ppermute(ours, 'dp_1', [(0, 1), (1, 0)])  1.96 us
  transfers between devices with their start and end apart: 5, of which 4 were waited for; matrix products, arithmetic and copies ran while one was open for 0% of the time, Pallas kernels for 0%

profile of v2, /device:TPU:1, one launch (start us, length us, event | category | flops | bytes accessed | tf_op | source)
XLA Modules:
  0.0 85.2 jit_solution(576657792341053769)
XLA Ops:
  0.6 0.0 copy-start
  0.7 0.9 %copy-done = bf16[5120,5]{0,1:T(8,128)(2,1)S(1)} copy-done((bf16[5120,5]{0,1:T(8,128)(2,1)S(1)}, bf16[5120,5]{0,1:T(8,128)(2,1)}, u32[]{:S(2)}) %copy-start) | copy-done | bytes 51224
  1.5 0.1 broadcast_in_dim.7
  1.6 0.1 broadcast_in_dim.8
  1.7 34.1 %all_to_all.10 = bf16[32,100,128]{2,1,0:T(8,128)(2,1)S(1)} all-to-all(bf16[32,100,128]{2,1,0:T(8,128)(2,1)S(1)} %broadcast_in_dim.8), channel_id=1, replica_groups=mesh['dp_0'=4,'dp_1'=2,'expert_0'=8,'expert_1'=4] {'expert_0','expert_1'}, dimensions={0} | all-to-all | bytes 1638400 | tf_op jit(solution)/shard_map/all_to_all | solution.py:26
  35.8 0.9 %reshape.20 = bf16[32,5,2560]{2,1,0:T(8,128)(2,1)S(1)} reshape(bf16[32,100,128]{2,1,0:T(8,128)(2,1)S(1)} %all_to_all.10) | data formatting | bytes 1638400 | tf_op jit(solution)/shard_map/reshape | solution.py:198
  36.7 0.3 copy.7
  37.0 3.0 %collective-permute-start = (bf16[160,2560]{1,0:T(8,128)(2,1)S(1)}, bf16[160,2560]{1,0:T(8,128)(2,1)S(1)}, u32[]{:S(2)}, u32[]{:S(2)}) collective-permute-start(bf16[160,2560]{1,0:T(8,128)(2,1)S(1)} %bitcast.11), channel_id=1, source_target_pairs={{0,32},{32,0},{1,33},{33,1},{2,34},{34,2},{3,35},{35,3},{4,36},{36... | collective-permute-start | bytes 2457608 | tf_op jit(solution)/shard_map/ppermute | solution.py:199
  40.0 2.0 %collective-permute-done = bf16[160,2560]{1,0:T(8,128)(2,1)S(1)} collective-permute-done((bf16[160,2560]{1,0:T(8,128)(2,1)S(1)}, bf16[160,2560]{1,0:T(8,128)(2,1)S(1)}, u32[]{:S(2)}, u32[]{:S(2)}) %collective-permute-start) | collective-permute-done | bytes 819232 | tf_op jit(solution)/shard_map/ppermute | solution.py:199
  41.9 0.2 broadcast_select_fusion.1
  42.1 0.0 copy-start.1
  42.1 1.4 %pad_maximum_fusion.router = bf16[160,5120]{1,0:T(8,128)(2,1)} fusion(bf16[160,2560]{1,0:T(8,128)(2,1)S(1)} %get-tuple-element.10, bf16[160,2560]{1,0:T(8,128)(2,1)S(1)} %get-tuple-element.9), kind=kLoop, calls=%fused_computation | loop fusion | flops 3276800 | bytes 3276800 | tf_op jit(solution)/shard_map/concatenate | solution.py:202
  43.5 0.0 copy-done.1
  43.5 7.4 %route.1 = s16[32,72,128]{2,1,0:T(8,128)(2,1)S(1)} custom-call(s32[1]{0:T(128)} %bitcast.where, bf16[160,5120]{1,0:T(8,128)(2,1)} %pad_maximum_fusion.router, bf16[5120,1024]{1,0:T(8,128)(2,1)} %tokens.1, s32[6,32768]{1,0:T(8,128)} %picks.1, s32[3,32768]{1,0:T(4,128)S(1)} %copy-done.1), custom_call_target="tpu_custom_call" | custom-call | tf_op jit(solution)/shard_map/route/pallas_call | solution.py:207
  50.9 22.4 %all_to_all.11.recv = s16[32,72,128]{2,1,0:T(8,128)(2,1)S(1)} all-to-all(s16[32,72,128]{2,1,0:T(8,128)(2,1)S(1)} %route.1), channel_id=1, replica_groups=mesh['dp_0'=4,'dp_1'=2,'expert_0'=8,'expert_1'=4] {'expert_0','expert_1'}, dimensions={0} | all-to-all | bytes 1179648 | tf_op jit(solution)/shard_map/all_to_all | solution.py:232
  73.3 1.6 %spread.1 = (f32[6,32768]{1,0:T(8,128)}, f32[1,32768]{1,0:T(1,128)}, f32[8,128]{1,0:T(8,128)S(1)}) custom-call(s16[32,72,128]{2,1,0:T(8,128)(2,1)S(1)} %all_to_all.11.recv), custom_call_target="tpu_custom_call" | custom-call | tf_op jit(solution)/shard_map/spread/pallas_call | solution.py:233
  74.9 2.3 %collective-permute-start.1 = (f32[8,128]{1,0:T(8,128)S(1)}, f32[8,128]{1,0:T(8,128)S(1)}, u32[]{:S(2)}, u32[]{:S(2)}) collective-permute-start(f32[8,128]{1,0:T(8,128)S(1)} %get-tuple-element.8), channel_id=1, source_target_pairs={{0,32},{32,0},{1,33},{33,1},{2,34},{34,2},{3,35},{35,3},{4,36},{36... | collective-permute-start | bytes 12296 | tf_op jit(solution)/shard_map/ppermute | solution.py:243
  77.2 0.8 collective-permute-done.1
  78.1 1.2 %collective-permute-start.2 = (f32[8,128]{1,0:T(8,128)S(1)}, f32[8,128]{1,0:T(8,128)S(1)}, u32[]{:S(2)}, u32[]{:S(2)}) collective-permute-start(f32[8,128]{1,0:T(8,128)S(1)} %add.11.own), channel_id=1, source_target_pairs={{0,64},{64,128},{128,192},{192,0},{1,65},{65,129},{129,193},{193,1... | collective-permute-start | bytes 12296 | tf_op jit(solution)/shard_map/ppermute | solution.py:246
  79.3 2.4 %collective-permute-start.3 = (f32[8,128]{1,0:T(8,128)S(1)}, f32[8,128]{1,0:T(8,128)S(1)}, u32[]{:S(2)}, u32[]{:S(2)}) collective-permute-start(f32[8,128]{1,0:T(8,128)S(1)} %add.11.own), channel_id=1, source_target_pairs={{0,128},{64,192},{128,0},{192,64},{1,129},{65,193},{129,1},{193,65... | collective-permute-start | bytes 12296 | tf_op jit(solution)/shard_map/ppermute | solution.py:246
  81.7 1.2 %collective-permute-start.4 = (f32[8,128]{1,0:T(8,128)S(1)}, f32[8,128]{1,0:T(8,128)S(1)}, u32[]{:S(2)}, u32[]{:S(2)}) collective-permute-start(f32[8,128]{1,0:T(8,128)S(1)} %add.11.own), channel_id=1, source_target_pairs={{0,192},{64,0},{128,64},{192,128},{1,193},{65,1},{129,65},{193,129... | collective-permute-start | bytes 12296 | tf_op jit(solution)/shard_map/ppermute | solution.py:246
  82.9 0.0 collective-permute-done.2.first
  82.9 0.4 collective-permute-done.3.second
  83.2 1.2 %collective-permute-done.4.third = f32[8,128]{1,0:T(8,128)S(1)} collective-permute-done((f32[8,128]{1,0:T(8,128)S(1)}, f32[8,128]{1,0:T(8,128)S(1)}, u32[]{:S(2)}, u32[]{:S(2)}) %collective-permute-start.4) | collective-permute-done | bytes 4128 | tf_op jit(solution)/shard_map/ppermute | solution.py:246
  84.5 0.2 balance.1
  84.6 0.5 slice_bitcast_fusion
  (2 shorter events, 0.0 us)
Async XLA Ops:
  0.6 0.9 %copy-start = (bf16[5120,5]{0,1:T(8,128)(2,1)S(1)}, bf16[5120,5]{0,1:T(8,128)(2,1)}, u32[]{:S(2)}) copy-start(bf16[5120,5]{0,1:T(8,128)(2,1)} %param.5) | copy-start | bytes 153604
  37.0 4.9 %collective-permute-start = (bf16[160,2560]{1,0:T(8,128)(2,1)S(1)}, bf16[160,2560]{1,0:T(8,128)(2,1)S(1)}, u32[]{:S(2)}, u32[]{:S(2)}) collective-permute-start(bf16[160,2560]{1,0:T(8,128)(2,1)S(1)} %bitcast.11), channel_id=1, source_target_pairs={{0,32},{32,0},{1,33},{33,1},{2,34},{34,2},{3,35},{35,3},{4,36},{36... | collective-permute-start | bytes 2457608 | tf_op jit(solution)/shard_map/ppermute | solution.py:199
  42.1 1.4 %copy-start.1 = (s32[3,32768]{1,0:T(4,128)S(1)}, s32[3,32768]{1,0:T(4,128)}, u32[]{:S(2)}) copy-start(s32[3,32768]{1,0:T(4,128)} %devs.1) | copy-start | bytes 1179652
  74.9 3.2 %collective-permute-start.1 = (f32[8,128]{1,0:T(8,128)S(1)}, f32[8,128]{1,0:T(8,128)S(1)}, u32[]{:S(2)}, u32[]{:S(2)}) collective-permute-start(f32[8,128]{1,0:T(8,128)S(1)} %get-tuple-element.8), channel_id=1, source_target_pairs={{0,32},{32,0},{1,33},{33,1},{2,34},{34,2},{3,35},{35,3},{4,36},{36... | collective-permute-start | bytes 12296 | tf_op jit(solution)/shard_map/ppermute | solution.py:243
  78.1 4.8 %collective-permute-start.2 = (f32[8,128]{1,0:T(8,128)S(1)}, f32[8,128]{1,0:T(8,128)S(1)}, u32[]{:S(2)}, u32[]{:S(2)}) collective-permute-start(f32[8,128]{1,0:T(8,128)S(1)} %add.11.own), channel_id=1, source_target_pairs={{0,64},{64,128},{128,192},{192,0},{1,65},{65,129},{129,193},{193,1... | collective-permute-start | bytes 12296 | tf_op jit(solution)/shard_map/ppermute | solution.py:246
  79.3 4.0 %collective-permute-start.3 = (f32[8,128]{1,0:T(8,128)S(1)}, f32[8,128]{1,0:T(8,128)S(1)}, u32[]{:S(2)}, u32[]{:S(2)}) collective-permute-start(f32[8,128]{1,0:T(8,128)S(1)} %add.11.own), channel_id=1, source_target_pairs={{0,128},{64,192},{128,0},{192,64},{1,129},{65,193},{129,1},{193,65... | collective-permute-start | bytes 12296 | tf_op jit(solution)/shard_map/ppermute | solution.py:246
  81.7 2.8 %collective-permute-start.4 = (f32[8,128]{1,0:T(8,128)S(1)}, f32[8,128]{1,0:T(8,128)S(1)}, u32[]{:S(2)}, u32[]{:S(2)}) collective-permute-start(f32[8,128]{1,0:T(8,128)S(1)} %add.11.own), channel_id=1, source_target_pairs={{0,192},{64,0},{128,64},{192,128},{1,193},{65,1},{129,65},{193,129... | collective-permute-start | bytes 12296 | tf_op jit(solution)/shard_map/ppermute | solution.py:246

commit v3 on v2

--- a/solution.py
+++ b/solution.py
@@ -64,30 +64,54 @@
     return base * (1.0 + unit(fine) * 16.0 / jnp.maximum(coarse, 1.0))
 
 
-def route_kernel(num_devices, per_device, where, router, tokens, picks, devs, out, prob_acc, count_acc, sent_acc):
+def source_device(core, place, row, half, sizes):
+    deep, wide = sizes
+    z, y = place
+    back = row % (deep // 2)
+    aside = (row // (deep // 2)) % wide
+    ahead = jnp.where(back == 0, deep // 2, back)
+    offset = jnp.where(core == half, deep - back, ahead)
+    return ((z + offset) % deep) * wide + (y + wide - aside) % wide
+
+
+def route_kernel(
+    sizes, per_device, where, own, other, tokens, picks, devs, out, router, prob_acc, count_acc, sent_acc
+):
     step = pl.program_id(0)
+    deep, wide = sizes
+    num_devices = deep * wide
     num_experts = num_devices * per_device
+    group = num_devices // 2
+    rows_half = num_experts // 2
     block = tokens.shape[1]
     tiles = block // LANES
     share = block * pl.num_programs(0)
+    core, place = where[1], (where[2], where[3])
 
     @pl.when(step == 0)
     def _():
+        router[:rows_half] = own[...]
+        router[rows_half:] = other[...]
         prob_acc[...] = jnp.zeros_like(prob_acc)
         count_acc[...] = jnp.zeros_like(count_acc)
         sent_acc[...] = jnp.zeros_like(sent_acc)
+
+    row = lax.broadcasted_iota(jnp.int32, (num_experts, LANES), 0)
+    half = row // rows_half
+    dev = source_device(core, place, row % group, half, sizes)
+    slot = (row % rows_half) // group
+    ids = dev * per_device + slot
+    ids_wide = jnp.concatenate([ids] * tiles, axis=1)
 
     scores = jnp.dot(router[...], tokens[...], preferred_element_type=jnp.float32)
     peak = jnp.max(scores, axis=0, keepdims=True)
     raised = jnp.exp(scores - peak)
     probs = raised / jnp.sum(raised, axis=0, keepdims=True)
     prob_acc[...] += lane_sum(probs)
-    rows = lax.broadcasted_iota(jnp.int32, (num_experts, block), 0)
-    ids = (rows % num_devices) * per_device + rows // num_devices
     chosen = []
     hits = jnp.zeros((num_experts, block), jnp.float32)
     for k in range(TOP):
-        mask = ids == picks[k : k + 1, :]
+        mask = ids_wide == picks[k : k + 1, :]
         chosen.append(jnp.sum(jnp.where(mask, probs, 0.0), axis=0, keepdims=True))
         hits += jnp.where(mask, 1.0, 0.0)
     count_acc[...] += lane_sum(hits)
@@ -102,37 +126,41 @@
     inverse = 1.0 / step_scale(scale)
     codes = [jnp.minimum(jnp.round(g * inverse), TOP_CODE) for g in chosen]
     lines = jnp.concatenate([*codes, scale, scale], axis=0).astype(jnp.int32) - MIDDLE
-    maxima = functools.reduce(
-        jnp.maximum, [probs[j * num_devices : (j + 1) * num_devices] for j in range(per_device)]
-    )
-    max_codes = jnp.round(jnp.sqrt(jnp.sqrt(maxima)) * TOP_CODE).astype(jnp.int32) - MIDDLE
-    max_codes = jnp.minimum(max_codes, MIDDLE - 1)
     stacked = jnp.concatenate([lines[:, j * LANES : (j + 1) * LANES] for j in range(tiles)], axis=0)
     last = lax.broadcasted_iota(jnp.int32, stacked.shape, 0) % ROWS == ROWS - 1
     here = pl.ds(pl.multiple_of(step * tiles * ROWS, tiles * ROWS), tiles * ROWS)
-    for d in range(num_devices):
-        line = jnp.concatenate(
-            [
-                jnp.broadcast_to(max_codes[d : d + 1, j * LANES : (j + 1) * LANES], (ROWS, LANES))
-                for j in range(tiles)
-            ],
-            axis=0,
-        )
-        out[d, here, :] = jnp.where(last, line, stacked).astype(jnp.int16)
+    for h in range(2):
+        slabs = [probs[h * rows_half + j * group : h * rows_half + (j + 1) * group] for j in range(per_device)]
+        maxima = functools.reduce(jnp.maximum, slabs)
+        max_codes = jnp.round(jnp.sqrt(jnp.sqrt(maxima)) * TOP_CODE).astype(jnp.int32) - MIDDLE
+        max_codes = jnp.minimum(max_codes, MIDDLE - 1)
+        for s in range(group):
+            line = jnp.concatenate(
+                [
+                    jnp.broadcast_to(max_codes[s : s + 1, j * LANES : (j + 1) * LANES], (ROWS, LANES))
+                    for j in range(tiles)
+                ],
+                axis=0,
+            )
+            target = source_device(core, place, s, h, sizes)
+            out[target, here, :] = jnp.where(last, line, stacked).astype(jnp.int16)
 
     @pl.when(step == pl.num_programs(0) - 1)
     def _():
-        def row(acc):
-            line = jnp.sum(acc[...].T, axis=0, keepdims=True)
-            missing = 2 * LANES - line.shape[1]
-            line = jnp.concatenate([line, jnp.zeros((1, missing), jnp.float32)], axis=1)
-            return line[:, :LANES], line[:, LANES:]
-
-        low, high = row(prob_acc)
+        def lined(acc, index):
+            total = jnp.sum(acc[...], axis=1, keepdims=True)
+            lanes = lax.broadcasted_iota(jnp.int32, index.shape, 1)
+            parts = [
+                jnp.sum(jnp.where(index == lanes + i * LANES, total, 0.0), axis=0, keepdims=True) for i in range(2)
+            ]
+            return parts
+
+        order = slot * num_devices + dev
+        low, high = lined(prob_acc, order)
         low_coarse, low_fine = coded_pair(low, share)
         high_coarse, high_fine = coded_pair(high, share)
-        count_low, count_high = row(count_acc)
-        sent_low, sent_high = row(sent_acc)
+        count_low, count_high = lined(count_acc, order)
+        sent_low, sent_high = lined(sent_acc, lax.broadcasted_iota(jnp.int32, (num_devices, LANES), 0))
         sums = jnp.concatenate(
             [low_coarse, high_coarse, low_fine, high_fine, count_low, count_high, sent_low, sent_high], axis=0
         )
@@ -141,22 +169,30 @@
             out[d, pl.ds(share // LANES * ROWS, ROWS), :] = sums
 
 
-def spread_kernel(recv, gates, maxima, sums):
+def decoded(codes):
+    return codes.astype(jnp.int32).astype(jnp.float32) + float(MIDDLE)
+
+
+def sums_kernel(share, recv, sums):
+    total = jnp.zeros((ROWS, LANES), jnp.float32)
+    for d in range(recv.shape[0]):
+        tile = decoded(recv[d])
+        probs = decoded_pair(tile[0:2], tile[2:4], share)
+        total += jnp.concatenate([probs, tile[4:8], jnp.zeros((2, LANES), jnp.float32)], axis=0)
+    sums[...] = total
+
+
+def spread_kernel(recv, gates, maxima):
     num, rows, _ = recv.shape
     tiles = rows // ROWS - 1
     share = tiles * LANES
-    total = jnp.zeros((ROWS, LANES), jnp.float32)
     for d in range(num):
-        codes = recv[d].astype(jnp.int32).astype(jnp.float32) + float(MIDDLE)
+        codes = decoded(recv[d, 0 : tiles * ROWS, :])
         for j in range(tiles):
             tile = codes[j * ROWS : (j + 1) * ROWS]
             cols = slice(d * share + j * LANES, d * share + (j + 1) * LANES)
             gates[:, cols] = tile[0:TOP] * step_scale(tile[TOP : TOP + 1])
             maxima[:, cols] = fourth(unit(tile[TOP + 1 : TOP + 2]))
-        tile = codes[tiles * ROWS :]
-        probs = decoded_pair(tile[0:2], tile[2:4], share)
-        total += jnp.concatenate([probs, tile[4:8], jnp.zeros((2, LANES), jnp.float32)], axis=0)
-    sums[...] = total
 
 
 def balance_kernel(num_devices, per_device, total_tokens, where, own, first, second, third, out, slots):
@@ -190,52 +226,73 @@
     num_experts = per_device * num_devices
     total_tokens = share * num_devices * lax.axis_size(DP)
     my_index = lax.axis_index(EXPERT)
-    core = lax.axis_index("dp_1")
-    half = features // 2
-
-    mine = lax.dynamic_slice_in_dim(router.T, core * half, half, 1)
-    packed = sent_to_all(mine.reshape(per_device * half // LANES, LANES), EXPERT)
-    ours = packed.reshape(num_devices, per_device, half).transpose(1, 0, 2).reshape(num_experts, half)
-    theirs = lax.ppermute(ours, "dp_1", [(0, 1), (1, 0)])
-    first = jnp.where(core == 0, ours, theirs)
-    second = jnp.where(core == 0, theirs, ours)
-    full = jnp.concatenate([first, second], axis=1)
+    core, z, y = (lax.axis_index(axis) for axis in ("dp_1", "expert_0", "expert_1"))
+    deep, wide = sizes = (lax.axis_size("expert_0"), lax.axis_size("expert_1"))
+    group = num_devices // 2
+
+    block = router.T.reshape(per_device * features // LANES, LANES)
+    pieces = [block]
+    for k in range(1, deep // 2):
+        pairs = [(i, (i + k) % deep) for i in range(deep)]
+        pairs += [(deep + i, deep + (i - k) % deep) for i in range(deep)]
+        pieces.append(lax.ppermute(block, ("dp_1", "expert_0"), pairs))
+    across = lax.ppermute(
+        block, ("dp_1", "expert_0"), [(deep + i, deep + (i + deep // 2) % deep) for i in range(deep)]
+    )
+    pieces[0] = jnp.where(core == 0, block, across)
+    column = jnp.stack(pieces)
+    plane = [column] + [
+        lax.ppermute(column, "expert_1", [(i, (i + k) % wide) for i in range(wide)]) for k in range(1, wide)
+    ]
+    own = jnp.stack(plane).reshape(group, per_device, features).transpose(1, 0, 2)
+    own = own.reshape(num_experts // 2, features)
+    other = lax.ppermute(own, "dp_1", [(0, 1), (1, 0)])
 
     steps = share // BLOCK
-    where = my_index.astype(jnp.int32).reshape(1)
+    where = jnp.stack([my_index, core, z, y]).astype(jnp.int32)
     rows = (share // LANES + 1) * ROWS
     msg = pl.pallas_call(
-        functools.partial(route_kernel, num_devices, per_device),
+        functools.partial(route_kernel, sizes, per_device),
         out_shape=jax.ShapeDtypeStruct((num_devices, rows, LANES), jnp.int16),
         grid_spec=pltpu.PrefetchScalarGridSpec(
             num_scalar_prefetch=1,
             grid=(steps,),
             in_specs=[
-                pl.BlockSpec((num_experts, features), lambda i, w: (0, 0)),
+                pl.BlockSpec((num_experts // 2, features), lambda i, w: (0, 0)),
+                pl.BlockSpec((num_experts // 2, features), lambda i, w: (0, 0)),
                 pl.BlockSpec((features, BLOCK), lambda i, w: (0, i)),
                 pl.BlockSpec((TOP, BLOCK), lambda i, w: (0, w[0] * steps + i)),
                 pl.BlockSpec((DEV_TOP, BLOCK), lambda i, w: (0, w[0] * steps + i)),
             ],
             out_specs=pl.BlockSpec((num_devices, rows, LANES), lambda i, w: (0, 0, 0)),
             scratch_shapes=[
+                pltpu.VMEM((num_experts, features), jnp.bfloat16),
                 pltpu.VMEM((num_experts, LANES), jnp.float32),
                 pltpu.VMEM((num_experts, LANES), jnp.float32),
                 pltpu.VMEM((num_devices, LANES), jnp.float32),
             ],
         ),
         compiler_params=pltpu.CompilerParams(
-            dimension_semantics=("arbitrary",), vmem_limit_bytes=52 * 1024 * 1024
+            dimension_semantics=("arbitrary",), vmem_limit_bytes=51 * 1024 * 1024
         ),
         name="route",
-    )(where, full, tokens, expert_pick, device_pick)
+    )(where, own, other, tokens, expert_pick, device_pick)
 
     recv = lax.all_to_all(msg, EXPERT, 0, 0, tiled=True)
-    gates, device_max, sums = pl.pallas_call(
+    sums = pl.pallas_call(
+        functools.partial(sums_kernel, share),
+        out_shape=jax.ShapeDtypeStruct((ROWS, LANES), jnp.float32),
+        grid=(1,),
+        in_specs=[pl.BlockSpec((num_devices, ROWS, LANES), lambda i: (0, rows // ROWS - 1, 0))],
+        out_specs=pl.BlockSpec((ROWS, LANES), lambda i: (0, 0)),
+        compiler_params=pltpu.CompilerParams(vmem_limit_bytes=2 * 1024 * 1024),
+        name="sums",
+    )(recv)
+    gates, device_max = pl.pallas_call(
         spread_kernel,
         out_shape=(
             jax.ShapeDtypeStruct((TOP, share * num_devices), jnp.float32),
             jax.ShapeDtypeStruct((1, share * num_devices), jnp.float32),
-            jax.ShapeDtypeStruct((ROWS, LANES), jnp.float32),
         ),
         compiler_params=pltpu.CompilerParams(vmem_limit_bytes=16 * 1024 * 1024),
         name="spread",

time: 85.5 us -> 79.6 us (0.931)
  blocking collectives: 56.5 us -> 24.6 us
  starting transfers between devices: 10.1 us -> 26.6 us
  waiting for transfers between devices: 4.38 us -> 13.4 us
  other arithmetic: 1.52 us -> 0.24 us
  local copies, waits for them, and re-layouts: 2.76 us -> 3.99 us
    all_to_all x1 -> x0, blocking collectives: 34.1 us -> none  [sent_to_all(): lax.all_to_all(jnp.broadcast_to(x[None], (length, *x.shape)), axis, 0, 0,...]
    ppermute x1 -> x8, starting transfers between devices: 2.98 us -> 20.6 us  [the longest x1 9.64 us: local(): lax.ppermute(block, ('dp_1', 'expert_0'), [(deep + i, deep + (i + deep //...]
    ppermute x1 -> x8, waiting for transfers between devices: 1.96 us -> 11.1 us  [the longest x3 6.95 us: local(): lax.ppermute(column, 'expert_1', [(i, (i + k) % wide) for i in range(wide)])]
    all_to_all x1, blocking collectives: 22.4 us -> 24.6 us  [local(): recv = lax.all_to_all(msg, EXPERT, 0, 0, tiled=True)]
    concatenate x1 -> x0, other arithmetic: 1.36 us -> none  [local(): full = jnp.concatenate([first, second], axis=1)]
    ppermute x3, starting transfers between devices: 4.82 us -> 3.61 us  [local(): lax.ppermute(chip, 'dp_0', [(i, (i + k) % length) for i in range(length)])]
    reshape x1 -> x2, local copies, waits for them, and re-layouts: 0.91 us -> 1.89 us  [the longest x1 0.97 us: local(): block = router.T.reshape(per_device * features // LANES, LANES)]
    pallas_call x1 -> x2, Pallas kernels: 7.4 us -> 8.12 us  [the longest x1 8.02 us: local(): pl.pallas_call(functools.partial(route_kernel, sizes, per_device), out_sh...]
  transfers between devices with their start and end apart: 5 -> 12, of which waited for: 4 -> 10; matrix products, arithmetic and copies ran while one was open for 0% -> 0% of each run, Pallas kernels for 0% -> 2%
where the time goes in v3:
time: 79.6 us; the launch traced here: 79.3 us
  starting transfers between devices  26.6 us (33%)
  blocking collectives  24.6 us (31%)
  waiting for transfers between devices  13.4 us (17%)
  Pallas kernels  9.84 us (12%)
  local copies, waits for them, and re-layouts  3.99 us (5%)
    all_to_all x1, blocking collectives, local(): recv = lax.all_to_all(msg, EXPERT, 0, 0, tiled=True)  24.6 us
    ppermute x1, starting transfers between devices, local(): lax.ppermute(block, ('dp_1', 'expert_0'), [(deep + i, deep + (i + deep //...  9.64 us
    pallas_call x1, Pallas kernels, local(): pl.pallas_call(functools.partial(route_kernel, sizes, per_device), out_sh...  8.02 us
    ppermute x3, waiting for transfers between devices, local(): lax.ppermute(column, 'expert_1', [(i, (i + k) % wide) for i in range(wide)])  6.95 us
    ppermute x3, starting transfers between devices, local(): lax.ppermute(column, 'expert_1', [(i, (i + k) % wide) for i in range(wide)])  5.68 us
    ppermute x3, starting transfers between devices, local(): pieces.append(lax.ppermute(block, ('dp_1', 'expert_0'), pairs))  4.84 us
    ppermute x3, starting transfers between devices, local(): lax.ppermute(chip, 'dp_0', [(i, (i + k) % length) for i in range(length)])  3.61 us
    ppermute x1, starting transfers between devices, local(): chip = sums + lax.ppermute(sums, 'dp_1', [(0, 1), (1, 0)])  2.42 us
  transfers between devices with their start and end apart: 12, of which 10 were waited for; matrix products, arithmetic and copies ran while one was open for 0% of the time, Pallas kernels for 2%

profile of v3, /device:TPU:1, one launch (start us, length us, event | category | flops | bytes accessed | tf_op | source)
XLA Modules:
  0.0 79.3 jit_solution(12982612464658189431)
XLA Ops:
  0.6 1.0 %reshape.18 = bf16[200,128]{1,0:T(8,128)(2,1)S(1)} reshape(bf16[5,5120]{1,0:T(8,128)(2,1)} %bitcast.28) | data formatting | bytes 102400 | tf_op jit(solution)/shard_map/reshape | solution.py:233
  1.6 9.6 %collective-permute-start = (bf16[200,128]{1,0:T(8,128)(2,1)S(1)}, bf16[200,128]{1,0:T(8,128)(2,1)S(1)}, u32[]{:S(2)}, u32[]{:S(2)}) collective-permute-start(bf16[200,128]{1,0:T(8,128)(2,1)S(1)} %reshape.18), channel_id=1, source_target_pairs={{32,48},{36,52},{40,56},{44,60},{48,32},{52,36},{56,40},{60,44},{3... | collective-permute-start | bytes 153608 | tf_op jit(solution)/shard_map/ppermute | solution.py:239
  11.2 0.1 collective-permute-start.3
  11.3 4.0 %collective-permute-start.2 = (bf16[200,128]{1,0:T(8,128)(2,1)S(1)}, bf16[200,128]{1,0:T(8,128)(2,1)S(1)}, u32[]{:S(2)}, u32[]{:S(2)}) collective-permute-start(bf16[200,128]{1,0:T(8,128)(2,1)S(1)} %reshape.18), channel_id=1, source_target_pairs={{0,8},{4,12},{8,16},{12,20},{16,24},{20,28},{24,0},{28,4},{32,56},... | collective-permute-start | bytes 153608 | tf_op jit(solution)/shard_map/ppermute | solution.py:238
  15.4 0.7 collective-permute-start.1
  16.1 0.0 collective-permute-done
  16.1 0.1 collective-permute-done.3
  16.2 0.4 collective-permute-done.2
  16.6 1.7 %collective-permute-done.1 = bf16[200,128]{1,0:T(8,128)(2,1)S(1)} collective-permute-done((bf16[200,128]{1,0:T(8,128)(2,1)S(1)}, bf16[200,128]{1,0:T(8,128)(2,1)S(1)}, u32[]{:S(2)}, u32[]{:S(2)}) %collective-permute-start.1) | collective-permute-done | bytes 51232 | tf_op jit(solution)/shard_map/ppermute | solution.py:238
  18.4 3.0 %collective-permute-start.5 = (bf16[4,200,128]{2,1,0:T(8,128)(2,1)S(1)}, bf16[4,200,128]{2,1,0:T(8,128)(2,1)S(1)}, u32[]{:S(2)}, u32[]{:S(2)}) collective-permute-start(bf16[4,200,128]{2,1,0:T(8,128)(2,1)S(1)} %get-tuple-element.8), channel_id=1, source_target_pairs={{0,2},{1,3},{2,0},{3,1},{4,6},{5,7},{6,4},{7,5},{8,10},{9,11},{10,... | collective-permute-start | bytes 614408 | tf_op jit(solution)/shard_map/ppermute | solution.py:245
  21.4 0.4 collective-permute-start.4
  21.8 2.3 %collective-permute-start.6 = (bf16[4,200,128]{2,1,0:T(8,128)(2,1)S(1)}, bf16[4,200,128]{2,1,0:T(8,128)(2,1)S(1)}, u32[]{:S(2)}, u32[]{:S(2)}) collective-permute-start(bf16[4,200,128]{2,1,0:T(8,128)(2,1)S(1)} %get-tuple-element.8), channel_id=1, source_target_pairs={{0,3},{1,0},{2,1},{3,2},{4,7},{5,4},{6,5},{7,6},{8,11},{9,8},{10,9... | collective-permute-start | bytes 614408 | tf_op jit(solution)/shard_map/ppermute | solution.py:245
  24.0 2.7 %collective-permute-done.5 = bf16[4,200,128]{2,1,0:T(8,128)(2,1)S(1)} collective-permute-done((bf16[4,200,128]{2,1,0:T(8,128)(2,1)S(1)}, bf16[4,200,128]{2,1,0:T(8,128)(2,1)S(1)}, u32[]{:S(2)}, u32[]{:S(2)}) %collective-permute-start.5) | collective-permute-done | bytes 204832 | tf_op jit(solution)/shard_map/ppermute | solution.py:245
  26.8 4.2 %collective-permute-done.4 = bf16[4,200,128]{2,1,0:T(8,128)(2,1)S(1)} collective-permute-done((bf16[4,200,128]{2,1,0:T(8,128)(2,1)S(1)}, bf16[4,200,128]{2,1,0:T(8,128)(2,1)S(1)}, u32[]{:S(2)}, u32[]{:S(2)}) %collective-permute-start.4) | collective-permute-done | bytes 204832 | tf_op jit(solution)/shard_map/ppermute | solution.py:245
  30.9 0.1 collective-permute-done.6
  31.0 0.1 pad_maximum_fusion
  31.1 0.9 %reshape.19 = bf16[16,5,5120]{2,1,0:T(8,128)(2,1)S(1)} reshape(bf16[4,4,200,128]{3,2,1,0:T(8,128)(2,1)S(1)} %pad_maximum_fusion) | data formatting | bytes 1638400 | tf_op jit(solution)/shard_map/reshape | solution.py:247
  32.0 0.5 copy.7
  32.6 0.4 collective-permute-start.7
  33.0 0.1 pad_add_fusion.where
  33.1 1.9 %collective-permute-done.7.other = bf16[80,5120]{1,0:T(8,128)(2,1)S(1)} collective-permute-done((bf16[80,5120]{1,0:T(8,128)(2,1)S(1)}, bf16[80,5120]{1,0:T(8,128)(2,1)S(1)}, u32[]{:S(2)}, u32[]{:S(2)}) %collective-permute-start.7) | collective-permute-done | bytes 819232 | tf_op jit(solution)/shard_map/ppermute | solution.py:249
  35.0 0.0 copy-start
  35.0 1.0 %copy-done = s32[3,32768]{1,0:T(4,128)S(1)} copy-done((s32[3,32768]{1,0:T(4,128)S(1)}, s32[3,32768]{1,0:T(4,128)}, u32[]{:S(2)}) %copy-start) | copy-done | bytes 393240
  36.1 8.0 %route.1 = s16[32,72,128]{2,1,0:T(8,128)(2,1)S(1)} custom-call(s32[4]{0:T(128)S(1)} %pad_add_fusion.where, bf16[80,5120]{1,0:T(8,128)(2,1)S(1)} %bitcast.23, bf16[80,5120]{1,0:T(8,128)(2,1)S(1)} %collective-permute-done.7.other, bf16[5120,1024]{1,0:T(8,128)(2,1)} %tokens.1, s32[6,32768]{1,0:T(8,128)} %picks.1, s32[3,32768]{1,0:T(4,128)S(1)} %copy-done), custom_call_target="tpu_custom_call" | custom-call | tf_op jit(solution)/shard_map/route/pallas_call | solution.py:254
  44.1 24.6 %all_to_all.5.recv = s16[32,72,128]{2,1,0:T(8,128)(2,1)S(1)} all-to-all(s16[32,72,128]{2,1,0:T(8,128)(2,1)S(1)} %route.1), channel_id=1, replica_groups=mesh['dp_0'=4,'dp_1'=2,'expert_0'=8,'expert_1'=4] {'expert_0','expert_1'}, dimensions={0} | all-to-all | bytes 1179648 | tf_op jit(solution)/shard_map/all_to_all | solution.py:281
  68.6 0.1 sums.1
  68.7 2.4 %collective-permute-start.8 = (f32[8,128]{1,0:T(8,128)S(1)}, f32[8,128]{1,0:T(8,128)S(1)}, u32[]{:S(2)}, u32[]{:S(2)}) collective-permute-start(f32[8,128]{1,0:T(8,128)S(1)} %sums.1), channel_id=1, source_target_pairs={{0,32},{32,0},{1,33},{33,1},{2,34},{34,2},{3,35},{35,3},{4,36},{36... | collective-permute-start | bytes 12296 | tf_op jit(solution)/shard_map/ppermute | solution.py:300
  71.2 0.8 %collective-permute-done.8 = f32[8,128]{1,0:T(8,128)S(1)} collective-permute-done((f32[8,128]{1,0:T(8,128)S(1)}, f32[8,128]{1,0:T(8,128)S(1)}, u32[]{:S(2)}, u32[]{:S(2)}) %collective-permute-start.8) | collective-permute-done | bytes 4128 | tf_op jit(solution)/shard_map/ppermute | solution.py:300
  72.0 2.5 %collective-permute-start.11 = (f32[8,128]{1,0:T(8,128)S(1)}, f32[8,128]{1,0:T(8,128)S(1)}, u32[]{:S(2)}, u32[]{:S(2)}) collective-permute-start(f32[8,128]{1,0:T(8,128)S(1)} %add.7.own), channel_id=1, source_target_pairs={{0,192},{64,0},{128,64},{192,128},{1,193},{65,1},{129,65},{193,129... | collective-permute-start | bytes 12296 | tf_op jit(solution)/shard_map/ppermute | solution.py:303
  74.5 0.5 collective-permute-start.10
  75.0 0.6 collective-permute-start.9
  75.6 1.5 %spread.1 = (f32[6,32768]{1,0:T(8,128)}, f32[1,32768]{1,0:T(1,128)}) custom-call(s16[32,72,128]{2,1,0:T(8,128)(2,1)S(1)} %all_to_all.5.recv), custom_call_target="tpu_custom_call" | custom-call | tf_op jit(solution)/shard_map/spread/pallas_call | solution.py:291
  77.1 0.0 collective-permute-done.11.third
  77.1 1.3 %collective-permute-done.10.second = f32[8,128]{1,0:T(8,128)S(1)} collective-permute-done((f32[8,128]{1,0:T(8,128)S(1)}, f32[8,128]{1,0:T(8,128)S(1)}, u32[]{:S(2)}, u32[]{:S(2)}) %collective-permute-start.10) | collective-permute-done | bytes 4128 | tf_op jit(solution)/shard_map/ppermute | solution.py:303
  78.4 0.2 collective-permute-done.9.first
  78.7 0.2 balance.1
  78.8 0.5 slice_bitcast_fusion
  (3 shorter events, 0.1 us)
Async XLA Ops:
  1.6 14.5 %collective-permute-start = (bf16[200,128]{1,0:T(8,128)(2,1)S(1)}, bf16[200,128]{1,0:T(8,128)(2,1)S(1)}, u32[]{:S(2)}, u32[]{:S(2)}) collective-permute-start(bf16[200,128]{1,0:T(8,128)(2,1)S(1)} %reshape.18), channel_id=1, source_target_pairs={{32,48},{36,52},{40,56},{44,60},{48,32},{52,36},{56,40},{60,44},{3... | collective-permute-start | bytes 153608 | tf_op jit(solution)/shard_map/ppermute | solution.py:239
  11.2 4.9 %collective-permute-start.3 = (bf16[200,128]{1,0:T(8,128)(2,1)S(1)}, bf16[200,128]{1,0:T(8,128)(2,1)S(1)}, u32[]{:S(2)}, u32[]{:S(2)}) collective-permute-start(bf16[200,128]{1,0:T(8,128)(2,1)S(1)} %reshape.18), channel_id=1, source_target_pairs={{0,12},{4,16},{8,20},{12,24},{16,28},{20,0},{24,4},{28,8},{32,52},... | collective-permute-start | bytes 153608 | tf_op jit(solution)/shard_map/ppermute | solution.py:238
  11.3 5.3 %collective-permute-start.2 = (bf16[200,128]{1,0:T(8,128)(2,1)S(1)}, bf16[200,128]{1,0:T(8,128)(2,1)S(1)}, u32[]{:S(2)}, u32[]{:S(2)}) collective-permute-start(bf16[200,128]{1,0:T(8,128)(2,1)S(1)} %reshape.18), channel_id=1, source_target_pairs={{0,8},{4,12},{8,16},{12,20},{16,24},{20,28},{24,0},{28,4},{32,56},... | collective-permute-start | bytes 153608 | tf_op jit(solution)/shard_map/ppermute | solution.py:238
  15.4 3.0 %collective-permute-start.1 = (bf16[200,128]{1,0:T(8,128)(2,1)S(1)}, bf16[200,128]{1,0:T(8,128)(2,1)S(1)}, u32[]{:S(2)}, u32[]{:S(2)}) collective-permute-start(bf16[200,128]{1,0:T(8,128)(2,1)S(1)} %reshape.18), channel_id=1, source_target_pairs={{0,4},{4,8},{8,12},{12,16},{16,20},{20,24},{24,28},{28,0},{32,60},... | collective-permute-start | bytes 153608 | tf_op jit(solution)/shard_map/ppermute | solution.py:238
  18.4 8.4 %collective-permute-start.5 = (bf16[4,200,128]{2,1,0:T(8,128)(2,1)S(1)}, bf16[4,200,128]{2,1,0:T(8,128)(2,1)S(1)}, u32[]{:S(2)}, u32[]{:S(2)}) collective-permute-start(bf16[4,200,128]{2,1,0:T(8,128)(2,1)S(1)} %get-tuple-element.8), channel_id=1, source_target_pairs={{0,2},{1,3},{2,0},{3,1},{4,6},{5,7},{6,4},{7,5},{8,10},{9,11},{10,... | collective-permute-start | bytes 614408 | tf_op jit(solution)/shard_map/ppermute | solution.py:245
  21.4 9.6 %collective-permute-start.4 = (bf16[4,200,128]{2,1,0:T(8,128)(2,1)S(1)}, bf16[4,200,128]{2,1,0:T(8,128)(2,1)S(1)}, u32[]{:S(2)}, u32[]{:S(2)}) collective-permute-start(bf16[4,200,128]{2,1,0:T(8,128)(2,1)S(1)} %get-tuple-element.8), channel_id=1, source_target_pairs={{0,1},{1,2},{2,3},{3,0},{4,5},{5,6},{6,7},{7,4},{8,9},{9,10},{10,1... | collective-permute-start | bytes 614408 | tf_op jit(solution)/shard_map/ppermute | solution.py:245
  21.8 9.2 %collective-permute-start.6 = (bf16[4,200,128]{2,1,0:T(8,128)(2,1)S(1)}, bf16[4,200,128]{2,1,0:T(8,128)(2,1)S(1)}, u32[]{:S(2)}, u32[]{:S(2)}) collective-permute-start(bf16[4,200,128]{2,1,0:T(8,128)(2,1)S(1)} %get-tuple-element.8), channel_id=1, source_target_pairs={{0,3},{1,0},{2,1},{3,2},{4,7},{5,4},{6,5},{7,6},{8,11},{9,8},{10,9... | collective-permute-start | bytes 614408 | tf_op jit(solution)/shard_map/ppermute | solution.py:245
  32.6 2.4 %collective-permute-start.7 = (bf16[80,5120]{1,0:T(8,128)(2,1)S(1)}, bf16[80,5120]{1,0:T(8,128)(2,1)S(1)}, u32[]{:S(2)}, u32[]{:S(2)}) collective-permute-start(bf16[80,5120]{1,0:T(8,128)(2,1)S(1)} %bitcast.22), channel_id=1, source_target_pairs={{0,32},{32,0},{1,33},{33,1},{2,34},{34,2},{3,35},{35,3},{4,36},{36... | collective-permute-start | bytes 2457608 | tf_op jit(solution)/shard_map/ppermute | solution.py:249
  35.0 1.0 %copy-start = (s32[3,32768]{1,0:T(4,128)S(1)}, s32[3,32768]{1,0:T(4,128)}, u32[]{:S(2)}) copy-start(s32[3,32768]{1,0:T(4,128)} %devs.1) | copy-start | bytes 1179652
  68.7 3.2 %collective-permute-start.8 = (f32[8,128]{1,0:T(8,128)S(1)}, f32[8,128]{1,0:T(8,128)S(1)}, u32[]{:S(2)}, u32[]{:S(2)}) collective-permute-start(f32[8,128]{1,0:T(8,128)S(1)} %sums.1), channel_id=1, source_target_pairs={{0,32},{32,0},{1,33},{33,1},{2,34},{34,2},{3,35},{35,3},{4,36},{36... | collective-permute-start | bytes 12296 | tf_op jit(solution)/shard_map/ppermute | solution.py:300
  72.0 5.2 %collective-permute-start.11 = (f32[8,128]{1,0:T(8,128)S(1)}, f32[8,128]{1,0:T(8,128)S(1)}, u32[]{:S(2)}, u32[]{:S(2)}) collective-permute-start(f32[8,128]{1,0:T(8,128)S(1)} %add.7.own), channel_id=1, source_target_pairs={{0,192},{64,0},{128,64},{192,128},{1,193},{65,1},{129,65},{193,129... | collective-permute-start | bytes 12296 | tf_op jit(solution)/shard_map/ppermute | solution.py:303
  74.5 4.0 %collective-permute-start.10 = (f32[8,128]{1,0:T(8,128)S(1)}, f32[8,128]{1,0:T(8,128)S(1)}, u32[]{:S(2)}, u32[]{:S(2)}) collective-permute-start(f32[8,128]{1,0:T(8,128)S(1)} %add.7.own), channel_id=1, source_target_pairs={{0,128},{64,192},{128,0},{192,64},{1,129},{65,193},{129,1},{193,65... | collective-permute-start | bytes 12296 | tf_op jit(solution)/shard_map/ppermute | solution.py:303
  75.0 3.7 %collective-permute-start.9 = (f32[8,128]{1,0:T(8,128)S(1)}, f32[8,128]{1,0:T(8,128)S(1)}, u32[]{:S(2)}, u32[]{:S(2)}) collective-permute-start(f32[8,128]{1,0:T(8,128)S(1)} %add.7.own), channel_id=1, source_target_pairs={{0,64},{64,128},{128,192},{192,0},{1,65},{65,129},{129,193},{193,1... | collective-permute-start | bytes 12296 | tf_op jit(solution)/shard_map/ppermute | solution.py:303

commit v4 on v3

--- a/solution.py
+++ b/solution.py
@@ -51,19 +51,6 @@
     return jnp.maximum(eighth(unit(code)), TINY) * (1.0 / TOP_CODE)
 
 
-def coded_pair(x, limit):
-    coarse = jnp.minimum(jnp.floor(eighth_root(x * (1.0 / limit)) * TOP_CODE), TOP_CODE)
-    base = eighth(unit(coarse)) * limit
-    rest = jnp.where(base > 0.0, (x - base) / jnp.maximum(base, TINY), 0.0)
-    fine = jnp.round(jnp.clip(rest * coarse * (1.0 / 16.0), 0.0, 1.0) * TOP_CODE)
-    return coarse, fine
-
-
-def decoded_pair(coarse, fine, limit):
-    base = eighth(unit(coarse)) * limit
-    return base * (1.0 + unit(fine) * 16.0 / jnp.maximum(coarse, 1.0))
-
-
 def source_device(core, place, row, half, sizes):
     deep, wide = sizes
     z, y = place
@@ -75,7 +62,7 @@
 
 
 def route_kernel(
-    sizes, per_device, where, own, other, tokens, picks, devs, out, router, prob_acc, count_acc, sent_acc
+    sizes, per_device, where, own, other, tokens, picks, devs, out, sums, router, prob_acc, count_acc, sent_acc
 ):
     step = pl.program_id(0)
     deep, wide = sizes
@@ -85,8 +72,7 @@
     rows_half = num_experts // 2
     block = tokens.shape[1]
     tiles = block // LANES
-    share = block * pl.num_programs(0)
-    core, place = where[1], (where[2], where[3])
+    core, place = where[0], (where[1], where[2])
 
     @pl.when(step == 0)
     def _():
@@ -156,35 +142,18 @@
             return parts
 
         order = slot * num_devices + dev
-        low, high = lined(prob_acc, order)
-        low_coarse, low_fine = coded_pair(low, share)
-        high_coarse, high_fine = coded_pair(high, share)
-        count_low, count_high = lined(count_acc, order)
-        sent_low, sent_high = lined(sent_acc, lax.broadcasted_iota(jnp.int32, (num_devices, LANES), 0))
-        sums = jnp.concatenate(
-            [low_coarse, high_coarse, low_fine, high_fine, count_low, count_high, sent_low, sent_high], axis=0
-        )
-        sums = (sums.astype(jnp.int32) - MIDDLE).astype(jnp.int16)
-        for d in range(num_devices):
-            out[d, pl.ds(share // LANES * ROWS, ROWS), :] = sums
+        device_rows = lax.broadcasted_iota(jnp.int32, (num_devices, LANES), 0)
+        parts = [*lined(prob_acc, order), *lined(count_acc, order), *lined(sent_acc, device_rows)]
+        sums[...] = jnp.concatenate([*parts, jnp.zeros((ROWS - len(parts), LANES), jnp.float32)], axis=0)
 
 
 def decoded(codes):
     return codes.astype(jnp.int32).astype(jnp.float32) + float(MIDDLE)
 
 
-def sums_kernel(share, recv, sums):
-    total = jnp.zeros((ROWS, LANES), jnp.float32)
-    for d in range(recv.shape[0]):
-        tile = decoded(recv[d])
-        probs = decoded_pair(tile[0:2], tile[2:4], share)
-        total += jnp.concatenate([probs, tile[4:8], jnp.zeros((2, LANES), jnp.float32)], axis=0)
-    sums[...] = total
-
-
 def spread_kernel(recv, gates, maxima):
     num, rows, _ = recv.shape
-    tiles = rows // ROWS - 1
+    tiles = rows // ROWS
     share = tiles * LANES
     for d in range(num):
         codes = decoded(recv[d, 0 : tiles * ROWS, :])
@@ -195,11 +164,24 @@
             maxima[:, cols] = fourth(unit(tile[TOP + 1 : TOP + 2]))
 
 
-def balance_kernel(num_devices, per_device, total_tokens, where, own, first, second, third, out, slots):
+def ring_sum_kernel(where, own, first, second, third, out, slots):
     place = where[0]
     for k, part in enumerate((own, first, second, third)):
         slots[(place + 4 - k) % 4] = part[...]
-    total = (slots[0] + slots[1]) + (slots[2] + slots[3])
+    out[...] = (slots[0] + slots[1]) + (slots[2] + slots[3])
+
+
+def ring_slots_kernel(where, own, first, second, third, across, out):
+    core, z = where[0], where[1]
+    out[...] = jnp.zeros_like(out)
+    for k, part in enumerate((first, second, third), 1):
+        out[(z + jnp.where(core == 0, 8 - k, k)) % 8] = part[...]
+    near = jnp.where(core == 0, own[...], across[...])
+    out[(z + jnp.where(core == 0, 0, 4)) % 8] = near
+
+
+def balance_kernel(num_devices, per_device, total_tokens, mine, others, out):
+    total = functools.reduce(jnp.add, [mine[i] + others[i] for i in range(8)])
     num_experts = num_devices * per_device
     prob = jnp.concatenate([total[0:1], total[1:2]], axis=1)[:, :num_experts] / total_tokens
     freq = jnp.concatenate([total[2:3], total[3:4]], axis=1)[:, :num_experts] * (
@@ -217,6 +199,17 @@
     losses = [jnp.sum(a * b, axis=1, keepdims=True) for a, b in ((freq, prob), (dev_freq, dev_prob), (sent, dev_prob))]
     lane = lax.broadcasted_iota(jnp.int32, (1, LANES), 1)
     out[...] = jnp.where(lane == 0, losses[0], jnp.where(lane == 1, losses[1], losses[2]))
+
+
+def along_z(x, deep):
+    axes = ("dp_1", "expert_0")
+    parts = []
+    for k in range(1, deep // 2):
+        pairs = [(i, (i + k) % deep) for i in range(deep)]
+        pairs += [(deep + i, deep + (i - k) % deep) for i in range(deep)]
+        parts.append(lax.ppermute(x, axes, pairs))
+    far = [(deep + i, deep + (i + deep // 2) % deep) for i in range(deep)]
+    return (*parts, lax.ppermute(x, axes, far))
 
 
 def local(tokens, router, device_pick, expert_pick):
@@ -231,15 +224,8 @@
     group = num_devices // 2
 
     block = router.T.reshape(per_device * features // LANES, LANES)
-    pieces = [block]
-    for k in range(1, deep // 2):
-        pairs = [(i, (i + k) % deep) for i in range(deep)]
-        pairs += [(deep + i, deep + (i - k) % deep) for i in range(deep)]
-        pieces.append(lax.ppermute(block, ("dp_1", "expert_0"), pairs))
-    across = lax.ppermute(
-        block, ("dp_1", "expert_0"), [(deep + i, deep + (i + deep // 2) % deep) for i in range(deep)]
-    )
-    pieces[0] = jnp.where(core == 0, block, across)
+    *pieces, across = along_z(block, deep)
+    pieces = [jnp.where(core == 0, block, across), *pieces]
     column = jnp.stack(pieces)
     plane = [column] + [
         lax.ppermute(column, "expert_1", [(i, (i + k) % wide) for i in range(wide)]) for k in range(1, wide)
@@ -249,11 +235,16 @@
     other = lax.ppermute(own, "dp_1", [(0, 1), (1, 0)])
 
     steps = share // BLOCK
-    where = jnp.stack([my_index, core, z, y]).astype(jnp.int32)
-    rows = (share // LANES + 1) * ROWS
-    msg = pl.pallas_call(
+    where = jnp.stack([core, z, y]).astype(jnp.int32)
+    rows = share // LANES * ROWS
+    experts_here = lax.dynamic_slice_in_dim(expert_pick, my_index * share, share, 1)
+    devices_here = lax.dynamic_slice_in_dim(device_pick, my_index * share, share, 1)
+    msg, sums = pl.pallas_call(
         functools.partial(route_kernel, sizes, per_device),
-        out_shape=jax.ShapeDtypeStruct((num_devices, rows, LANES), jnp.int16),
+        out_shape=(
+            jax.ShapeDtypeStruct((num_devices, rows, LANES), jnp.int16),
+            jax.ShapeDtypeStruct((ROWS, LANES), jnp.float32),
+        ),
         grid_spec=pltpu.PrefetchScalarGridSpec(
             num_scalar_prefetch=1,
             grid=(steps,),
@@ -261,10 +252,13 @@
                 pl.BlockSpec((num_experts // 2, features), lambda i, w: (0, 0)),
                 pl.BlockSpec((num_experts // 2, features), lambda i, w: (0, 0)),
                 pl.BlockSpec((features, BLOCK), lambda i, w: (0, i)),
-                pl.BlockSpec((TOP, BLOCK), lambda i, w: (0, w[0] * steps + i)),
-                pl.BlockSpec((DEV_TOP, BLOCK), lambda i, w: (0, w[0] * steps + i)),
+                pl.BlockSpec((TOP, BLOCK), lambda i, w: (0, i)),
+                pl.BlockSpec((DEV_TOP, BLOCK), lambda i, w: (0, i)),
             ],
-            out_specs=pl.BlockSpec((num_devices, rows, LANES), lambda i, w: (0, 0, 0)),
+            out_specs=(
+                pl.BlockSpec((num_devices, rows, LANES), lambda i, w: (0, 0, 0)),
+                pl.BlockSpec((ROWS, LANES), lambda i, w: (0, 0)),
+            ),
             scratch_shapes=[
                 pltpu.VMEM((num_experts, features), jnp.bfloat16),
                 pltpu.VMEM((num_experts, LANES), jnp.float32),
@@ -276,18 +270,9 @@
             dimension_semantics=("arbitrary",), vmem_limit_bytes=51 * 1024 * 1024
         ),
         name="route",
-    )(where, own, other, tokens, expert_pick, device_pick)
+    )(where, own, other, tokens, experts_here, devices_here)
 
     recv = lax.all_to_all(msg, EXPERT, 0, 0, tiled=True)
-    sums = pl.pallas_call(
-        functools.partial(sums_kernel, share),
-        out_shape=jax.ShapeDtypeStruct((ROWS, LANES), jnp.float32),
-        grid=(1,),
-        in_specs=[pl.BlockSpec((num_devices, ROWS, LANES), lambda i: (0, rows // ROWS - 1, 0))],
-        out_specs=pl.BlockSpec((ROWS, LANES), lambda i: (0, 0)),
-        compiler_params=pltpu.CompilerParams(vmem_limit_bytes=2 * 1024 * 1024),
-        name="sums",
-    )(recv)
     gates, device_max = pl.pallas_call(
         spread_kernel,
         out_shape=(
@@ -297,24 +282,48 @@
         compiler_params=pltpu.CompilerParams(vmem_limit_bytes=16 * 1024 * 1024),
         name="spread",
     )(recv)
-    chip = sums + lax.ppermute(sums, "dp_1", [(0, 1), (1, 0)])
-    length = lax.axis_size("dp_0")
-    others = [
-        lax.ppermute(chip, "dp_0", [(i, (i + k) % length) for i in range(length)]) for k in range(1, length)
-    ]
+
+    small = pltpu.CompilerParams(vmem_limit_bytes=1024 * 1024)
+    tile = pl.BlockSpec((ROWS, LANES), lambda i, w: (0, 0))
+    scalar = lambda *values: jnp.stack(values).astype(jnp.int32)
+
+    def summed(x, axis):
+        length = lax.axis_size(axis)
+        others = [lax.ppermute(x, axis, [(i, (i + k) % length) for i in range(length)]) for k in range(1, length)]
+        return pl.pallas_call(
+            ring_sum_kernel,
+            out_shape=jax.ShapeDtypeStruct((ROWS, LANES), jnp.float32),
+            grid_spec=pltpu.PrefetchScalarGridSpec(
+                num_scalar_prefetch=1,
+                grid=(1,),
+                in_specs=[tile] * length,
+                out_specs=tile,
+                scratch_shapes=[pltpu.VMEM((length, ROWS, LANES), jnp.float32)],
+            ),
+            compiler_params=small,
+            name="ring_sum",
+        )(scalar(lax.axis_index(axis)), x, *others)
+
+    sums = sums + lax.ppermute(sums, "dp_1", [(0, 1), (1, 0)])
+    sums = summed(summed(sums, "dp_0"), "expert_1")
+    mine = pl.pallas_call(
+        ring_slots_kernel,
+        out_shape=jax.ShapeDtypeStruct((deep, ROWS, LANES), jnp.float32),
+        grid_spec=pltpu.PrefetchScalarGridSpec(
+            num_scalar_prefetch=1,
+            grid=(1,),
+            in_specs=[tile] * 5,
+            out_specs=pl.BlockSpec((deep, ROWS, LANES), lambda i, w: (0, 0, 0)),
+        ),
+        compiler_params=small,
+        name="ring_slots",
+    )(scalar(core, z), sums, *along_z(sums, deep))
     balance = pl.pallas_call(
         functools.partial(balance_kernel, num_devices, per_device, total_tokens),
         out_shape=jax.ShapeDtypeStruct((1, LANES), jnp.float32),
-        grid_spec=pltpu.PrefetchScalarGridSpec(
-            num_scalar_prefetch=1,
-            grid=(1,),
-            in_specs=[pl.BlockSpec((ROWS, LANES), lambda i, w: (0, 0))] * 4,
-            out_specs=pl.BlockSpec((1, LANES), lambda i, w: (0, 0)),
-            scratch_shapes=[pltpu.VMEM((4, ROWS, LANES), jnp.float32)],
-        ),
-        compiler_params=pltpu.CompilerParams(vmem_limit_bytes=1024 * 1024),
+        compiler_params=small,
         name="balance",
-    )(lax.axis_index("dp_0").astype(jnp.int32).reshape(1), chip, *others)
+    )(mine, lax.ppermute(mine, "dp_1", [(0, 1), (1, 0)]))
     return (gates, device_max, balance[0, 0:3])
 
 

time: 79.6 us -> 85.7 us (1.077)
  blocking collectives: 24.6 us -> 0 us
  starting transfers between devices: 26.6 us -> 49.2 us
  waiting for transfers between devices: 13.4 us -> 20.2 us
  Pallas kernels: 9.84 us -> 11.1 us
    all_to_all x1 -> x0, blocking collectives: 24.6 us -> none  [local(): recv = lax.all_to_all(msg, EXPERT, 0, 0, tiled=True)]
    ppermute x8 -> x16, starting transfers between devices: 20.5 us -> 36 us  [the longest x2 16.3 us: along_z(): return (*parts, lax.ppermute(x, axes, far))]
    ppermute x8 -> x16, waiting for transfers between devices: 4.55 us -> 12.1 us  [the longest x6 6.76 us: summed(): lax.ppermute(x, axis, [(i, (i + k) % length) for i in range(length)])]
    all_to_all x0 -> x1, starting transfers between devices: none -> 7.1 us  [local(): recv = lax.all_to_all(msg, EXPERT, 0, 0, tiled=True)]
    unnamed x2, local copies, waits for them, and re-layouts: 1.04 us -> 0.01 us
  transfers between devices with their start and end apart: 12 -> 21, of which waited for: 10 -> 14; matrix products, arithmetic and copies ran while one was open for 0% -> 2% of each run, Pallas kernels for 2% -> 1%
where the time goes in v4:
time: 85.7 us; the launch traced here: 85.3 us
  starting transfers between devices  49.2 us (57%)
  waiting for transfers between devices  20.2 us (24%)
  Pallas kernels  11.1 us (13%)
  local copies, waits for them, and re-layouts  3.77 us (4%)
    ppermute x2, starting transfers between devices, along_z(): return (*parts, lax.ppermute(x, axes, far))  16.3 us
    ppermute x6, starting transfers between devices, along_z(): parts.append(lax.ppermute(x, axes, pairs))  9.11 us
    pallas_call x1, Pallas kernels, local(): pl.pallas_call(functools.partial(route_kernel, sizes, per_device), out_sh...  8.76 us
    ppermute x6, starting transfers between devices, summed(): lax.ppermute(x, axis, [(i, (i + k) % length) for i in range(length)])  7.56 us
    all_to_all x1, starting transfers between devices, local(): recv = lax.all_to_all(msg, EXPERT, 0, 0, tiled=True)  7.1 us
    ppermute x3, waiting for transfers between devices, local(): lax.ppermute(column, 'expert_1', [(i, (i + k) % wide) for i in range(wide)])  6.95 us
    ppermute x6, waiting for transfers between devices, summed(): lax.ppermute(x, axis, [(i, (i + k) % length) for i in range(length)])  6.76 us
    ppermute x3, starting transfers between devices, local(): lax.ppermute(column, 'expert_1', [(i, (i + k) % wide) for i in range(wide)])  5.68 us
  transfers between devices with their start and end apart: 21, of which 14 were waited for; matrix products, arithmetic and copies ran while one was open for 2% of the time, Pallas kernels for 1%

profile of v4, /device:TPU:1, one launch (start us, length us, event | category | flops | bytes accessed | tf_op | source)
XLA Modules:
  0.0 85.3 jit_solution(12336402463926034869)
XLA Ops:
  0.6 0.0 copy-start
  0.6 1.1 %reshape.15 = bf16[200,128]{1,0:T(8,128)(2,1)S(1)} reshape(bf16[5,5120]{1,0:T(8,128)(2,1)} %bitcast.27) | data formatting | bytes 102400 | tf_op jit(solution)/shard_map/reshape | solution.py:226
  1.7 9.6 %collective-permute-start = (bf16[200,128]{1,0:T(8,128)(2,1)S(1)}, bf16[200,128]{1,0:T(8,128)(2,1)S(1)}, u32[]{:S(2)}, u32[]{:S(2)}) collective-permute-start(bf16[200,128]{1,0:T(8,128)(2,1)S(1)} %reshape.15), channel_id=1, source_target_pairs={{32,48},{36,52},{40,56},{44,60},{48,32},{52,36},{56,40},{60,44},{3... | collective-permute-start | bytes 153608 | tf_op jit(solution)/shard_map/ppermute | solution.py:212
  11.3 0.1 collective-permute-start.3
  11.4 4.0 %collective-permute-start.2 = (bf16[200,128]{1,0:T(8,128)(2,1)S(1)}, bf16[200,128]{1,0:T(8,128)(2,1)S(1)}, u32[]{:S(2)}, u32[]{:S(2)}) collective-permute-start(bf16[200,128]{1,0:T(8,128)(2,1)S(1)} %reshape.15), channel_id=1, source_target_pairs={{0,8},{4,12},{8,16},{12,20},{16,24},{20,28},{24,0},{28,4},{32,56},... | collective-permute-start | bytes 153608 | tf_op jit(solution)/shard_map/ppermute | solution.py:210
  15.5 0.7 collective-permute-start.1
  16.2 0.1 collective-permute-done.3
  16.3 0.4 collective-permute-done.2
  16.7 1.7 %collective-permute-done.1 = bf16[200,128]{1,0:T(8,128)(2,1)S(1)} collective-permute-done((bf16[200,128]{1,0:T(8,128)(2,1)S(1)}, bf16[200,128]{1,0:T(8,128)(2,1)S(1)}, u32[]{:S(2)}, u32[]{:S(2)}) %collective-permute-start.1) | collective-permute-done | bytes 51232 | tf_op jit(solution)/shard_map/ppermute | solution.py:210
  18.5 3.0 %collective-permute-start.5 = (bf16[4,200,128]{2,1,0:T(8,128)(2,1)S(1)}, bf16[4,200,128]{2,1,0:T(8,128)(2,1)S(1)}, u32[]{:S(2)}, u32[]{:S(2)}) collective-permute-start(bf16[4,200,128]{2,1,0:T(8,128)(2,1)S(1)} %get-tuple-element.12), channel_id=1, source_target_pairs={{0,2},{1,3},{2,0},{3,1},{4,6},{5,7},{6,4},{7,5},{8,10},{9,11},{10,... | collective-permute-start | bytes 614408 | tf_op jit(solution)/shard_map/ppermute | solution.py:231
  21.5 0.4 collective-permute-start.4
  21.9 2.3 %collective-permute-start.6 = (bf16[4,200,128]{2,1,0:T(8,128)(2,1)S(1)}, bf16[4,200,128]{2,1,0:T(8,128)(2,1)S(1)}, u32[]{:S(2)}, u32[]{:S(2)}) collective-permute-start(bf16[4,200,128]{2,1,0:T(8,128)(2,1)S(1)} %get-tuple-element.12), channel_id=1, source_target_pairs={{0,3},{1,0},{2,1},{3,2},{4,7},{5,4},{6,5},{7,6},{8,11},{9,8},{10,9... | collective-permute-start | bytes 614408 | tf_op jit(solution)/shard_map/ppermute | solution.py:231
  24.2 2.7 %collective-permute-done.5 = bf16[4,200,128]{2,1,0:T(8,128)(2,1)S(1)} collective-permute-done((bf16[4,200,128]{2,1,0:T(8,128)(2,1)S(1)}, bf16[4,200,128]{2,1,0:T(8,128)(2,1)S(1)}, u32[]{:S(2)}, u32[]{:S(2)}) %collective-permute-start.5) | collective-permute-done | bytes 204832 | tf_op jit(solution)/shard_map/ppermute | solution.py:231
  26.9 4.2 %collective-permute-done.4 = bf16[4,200,128]{2,1,0:T(8,128)(2,1)S(1)} collective-permute-done((bf16[4,200,128]{2,1,0:T(8,128)(2,1)S(1)}, bf16[4,200,128]{2,1,0:T(8,128)(2,1)S(1)}, u32[]{:S(2)}, u32[]{:S(2)}) %collective-permute-start.4) | collective-permute-done | bytes 204832 | tf_op jit(solution)/shard_map/ppermute | solution.py:231
  31.0 0.1 collective-permute-done.6
  31.1 0.1 pad_maximum_fusion
  31.2 0.9 %reshape.16 = bf16[16,5,5120]{2,1,0:T(8,128)(2,1)S(1)} reshape(bf16[4,4,200,128]{3,2,1,0:T(8,128)(2,1)S(1)} %pad_maximum_fusion) | data formatting | bytes 1638400 | tf_op jit(solution)/shard_map/reshape | solution.py:233
  32.1 0.5 copy.7
  32.7 0.4 collective-permute-start.7
  33.1 0.1 pad_add_fusion.where
  33.2 0.7 constant_dynamic-slice_fusion.devs
  33.9 1.2 %collective-permute-done.7.other = bf16[80,5120]{1,0:T(8,128)(2,1)S(1)} collective-permute-done((bf16[80,5120]{1,0:T(8,128)(2,1)S(1)}, bf16[80,5120]{1,0:T(8,128)(2,1)S(1)}, u32[]{:S(2)}, u32[]{:S(2)}) %collective-permute-start.7) | collective-permute-done | bytes 819232 | tf_op jit(solution)/shard_map/ppermute | solution.py:235
  35.1 8.8 %route.1 = (s16[32,64,128]{2,1,0:T(8,128)(2,1)}, f32[8,128]{1,0:T(8,128)S(1)}) custom-call(s32[3]{0:T(128)S(1)} %pad_add_fusion.where, bf16[80,5120]{1,0:T(8,128)(2,1)S(1)} %bitcast.22, bf16[80,5120]{1,0:T(8,128)(2,1)S(1)} %collective-permute-done.7.other, bf16[5120,1024]{1,0:T(8,128)(2,1)} %tokens.1, s32[6,1024]{1,0:T(8,128)S(1)} %constant_dynamic-slice_fusion.1.picks, ...), custom_call_target="tpu_custom_call" | custom-call | tf_op jit(solution)/shard_map/route/pallas_call | solution.py:242
  43.9 7.1 %all-to-all-start = ((s16[32,64,128]{2,1,0:T(8,128)(2,1)}), s16[32,64,128]{2,1,0:T(8,128)(2,1)S(1)}, u32[]{:S(2)}, u32[]{:S(2)}) async-start(s16[32,64,128]{2,1,0:T(8,128)(2,1)} %get-tuple-element.7), calls=%async_computation | async-start | bytes 1048576 | tf_op jit(solution)/shard_map/all_to_all | solution.py:275
  51.0 0.7 collective-permute-start.8
  51.7 0.8 collective-permute-done.8
  52.5 2.5 %collective-permute-start.11 = (f32[8,128]{1,0:T(8,128)S(1)}, f32[8,128]{1,0:T(8,128)S(1)}, u32[]{:S(2)}, u32[]{:S(2)}) collective-permute-start(f32[8,128]{1,0:T(8,128)S(1)} %add.12.own), channel_id=1, source_target_pairs={{0,192},{64,0},{128,64},{192,128},{1,193},{65,1},{129,65},{193,129... | collective-permute-start | bytes 12296 | tf_op jit(solution)/shard_map/ppermute | solution.py:292
  55.0 0.5 collective-permute-start.10
  55.5 0.6 collective-permute-start.9
  56.2 3.1 %collective-permute-done.10.second = f32[8,128]{1,0:T(8,128)S(1)} collective-permute-done((f32[8,128]{1,0:T(8,128)S(1)}, f32[8,128]{1,0:T(8,128)S(1)}, u32[]{:S(2)}, u32[]{:S(2)}) %collective-permute-start.10) | collective-permute-done | bytes 4128 | tf_op jit(solution)/shard_map/ppermute | solution.py:292
  59.3 0.2 collective-permute-done.9.first
  59.5 2.8 %collective-permute-start.14 = (f32[8,128]{1,0:T(8,128)S(1)}, f32[8,128]{1,0:T(8,128)S(1)}, u32[]{:S(2)}, u32[]{:S(2)}) collective-permute-start(f32[8,128]{1,0:T(8,128)S(1)} %ring_sum.2.own), channel_id=1, source_target_pairs={{0,3},{1,0},{2,1},{3,2},{4,7},{5,4},{6,5},{7,6},{8,11},{9,8},{10,9... | collective-permute-start | bytes 12296 | tf_op jit(solution)/shard_map/ppermute | solution.py:292
  62.3 0.6 collective-permute-start.13
  62.9 0.6 collective-permute-start.12
  63.5 3.1 %collective-permute-done.13.second = f32[8,128]{1,0:T(8,128)S(1)} collective-permute-done((f32[8,128]{1,0:T(8,128)S(1)}, f32[8,128]{1,0:T(8,128)S(1)}, u32[]{:S(2)}, u32[]{:S(2)}) %collective-permute-start.13) | collective-permute-done | bytes 4128 | tf_op jit(solution)/shard_map/ppermute | solution.py:292
  66.6 0.3 collective-permute-done.12.first
  66.9 6.7 %collective-permute-start.18 = (f32[8,128]{1,0:T(8,128)S(1)}, f32[8,128]{1,0:T(8,128)S(1)}, u32[]{:S(2)}, u32[]{:S(2)}) collective-permute-start(f32[8,128]{1,0:T(8,128)S(1)} %ring_sum.3.own), channel_id=1, source_target_pairs={{32,48},{36,52},{40,56},{44,60},{48,32},{52,36},{56,40},{60,44},{3... | collective-permute-start | bytes 12296 | tf_op jit(solution)/shard_map/ppermute | solution.py:212
  73.6 0.8 collective-permute-start.17
  74.4 2.4 %collective-permute-start.16 = (f32[8,128]{1,0:T(8,128)S(1)}, f32[8,128]{1,0:T(8,128)S(1)}, u32[]{:S(2)}, u32[]{:S(2)}) collective-permute-start(f32[8,128]{1,0:T(8,128)S(1)} %ring_sum.3.own), channel_id=1, source_target_pairs={{0,8},{4,12},{8,16},{12,20},{16,24},{20,28},{24,0},{28,4},{32,56},... | collective-permute-start | bytes 12296 | tf_op jit(solution)/shard_map/ppermute | solution.py:210
  76.7 1.1 %collective-permute-start.15 = (f32[8,128]{1,0:T(8,128)S(1)}, f32[8,128]{1,0:T(8,128)S(1)}, u32[]{:S(2)}, u32[]{:S(2)}) collective-permute-start(f32[8,128]{1,0:T(8,128)S(1)} %ring_sum.3.own), channel_id=1, source_target_pairs={{0,4},{4,8},{8,12},{12,16},{16,20},{20,24},{24,28},{28,0},{32,60},... | collective-permute-start | bytes 12296 | tf_op jit(solution)/shard_map/ppermute | solution.py:210
  77.9 0.1 pad_add_fusion.1.where
  78.0 1.4 %collective-permute-done.15.first = f32[8,128]{1,0:T(8,128)S(1)} collective-permute-done((f32[8,128]{1,0:T(8,128)S(1)}, f32[8,128]{1,0:T(8,128)S(1)}, u32[]{:S(2)}, u32[]{:S(2)}) %collective-permute-start.15) | collective-permute-done | bytes 4128 | tf_op jit(solution)/shard_map/ppermute | solution.py:210
  79.4 0.6 ring_slots.1.mine
  80.0 2.3 %collective-permute-start.19 = (f32[8,8,128]{2,1,0:T(8,128)S(1)}, f32[8,8,128]{2,1,0:T(8,128)S(1)}, u32[]{:S(2)}, u32[]{:S(2)}) collective-permute-start(f32[8,8,128]{2,1,0:T(8,128)S(1)} %ring_slots.1.mine), channel_id=1, source_target_pairs={{0,32},{32,0},{1,33},{33,1},{2,34},{34,2},{3,35},{35,3},{4,36},{36... | collective-permute-start | bytes 98312 | tf_op jit(solution)/shard_map/ppermute | solution.py:326
  82.2 0.9 %collective-permute-done.19.others = f32[8,8,128]{2,1,0:T(8,128)S(1)} collective-permute-done((f32[8,8,128]{2,1,0:T(8,128)S(1)}, f32[8,8,128]{2,1,0:T(8,128)S(1)}, u32[]{:S(2)}, u32[]{:S(2)}) %collective-permute-start.19) | collective-permute-done | bytes 32800 | tf_op jit(solution)/shard_map/ppermute | solution.py:326
  83.1 0.2 balance.1
  83.3 0.5 slice_bitcast_fusion
  83.8 1.6 %spread.1 = (f32[6,32768]{1,0:T(8,128)}, f32[1,32768]{1,0:T(1,128)}) custom-call(s16[32,64,128]{2,1,0:T(8,128)(2,1)S(1)} %all-to-all-done.recv), custom_call_target="tpu_custom_call" | custom-call | tf_op jit(solution)/shard_map/spread/pallas_call | solution.py:276
  (14 shorter events, 0.1 us)
Async XLA Ops:
  0.6 33.3 %copy-start = (s32[6,32768]{1,0:T(8,128)S(1)}, s32[6,32768]{1,0:T(8,128)}, u32[]{:S(2)}) copy-start(s32[6,32768]{1,0:T(8,128)} %param.7) | copy-start | bytes 2359300
  1.7 14.5 %collective-permute-start = (bf16[200,128]{1,0:T(8,128)(2,1)S(1)}, bf16[200,128]{1,0:T(8,128)(2,1)S(1)}, u32[]{:S(2)}, u32[]{:S(2)}) collective-permute-start(bf16[200,128]{1,0:T(8,128)(2,1)S(1)} %reshape.15), channel_id=1, source_target_pairs={{32,48},{36,52},{40,56},{44,60},{48,32},{52,36},{56,40},{60,44},{3... | collective-permute-start | bytes 153608 | tf_op jit(solution)/shard_map/ppermute | solution.py:212
  11.3 4.9 %collective-permute-start.3 = (bf16[200,128]{1,0:T(8,128)(2,1)S(1)}, bf16[200,128]{1,0:T(8,128)(2,1)S(1)}, u32[]{:S(2)}, u32[]{:S(2)}) collective-permute-start(bf16[200,128]{1,0:T(8,128)(2,1)S(1)} %reshape.15), channel_id=1, source_target_pairs={{0,12},{4,16},{8,20},{12,24},{16,28},{20,0},{24,4},{28,8},{32,52},... | collective-permute-start | bytes 153608 | tf_op jit(solution)/shard_map/ppermute | solution.py:210
  11.4 5.3 %collective-permute-start.2 = (bf16[200,128]{1,0:T(8,128)(2,1)S(1)}, bf16[200,128]{1,0:T(8,128)(2,1)S(1)}, u32[]{:S(2)}, u32[]{:S(2)}) collective-permute-start(bf16[200,128]{1,0:T(8,128)(2,1)S(1)} %reshape.15), channel_id=1, source_target_pairs={{0,8},{4,12},{8,16},{12,20},{16,24},{20,28},{24,0},{28,4},{32,56},... | collective-permute-start | bytes 153608 | tf_op jit(solution)/shard_map/ppermute | solution.py:210
  15.5 3.0 %collective-permute-start.1 = (bf16[200,128]{1,0:T(8,128)(2,1)S(1)}, bf16[200,128]{1,0:T(8,128)(2,1)S(1)}, u32[]{:S(2)}, u32[]{:S(2)}) collective-permute-start(bf16[200,128]{1,0:T(8,128)(2,1)S(1)} %reshape.15), channel_id=1, source_target_pairs={{0,4},{4,8},{8,12},{12,16},{16,20},{20,24},{24,28},{28,0},{32,60},... | collective-permute-start | bytes 153608 | tf_op jit(solution)/shard_map/ppermute | solution.py:210
  18.5 8.4 %collective-permute-start.5 = (bf16[4,200,128]{2,1,0:T(8,128)(2,1)S(1)}, bf16[4,200,128]{2,1,0:T(8,128)(2,1)S(1)}, u32[]{:S(2)}, u32[]{:S(2)}) collective-permute-start(bf16[4,200,128]{2,1,0:T(8,128)(2,1)S(1)} %get-tuple-element.12), channel_id=1, source_target_pairs={{0,2},{1,3},{2,0},{3,1},{4,6},{5,7},{6,4},{7,5},{8,10},{9,11},{10,... | collective-permute-start | bytes 614408 | tf_op jit(solution)/shard_map/ppermute | solution.py:231
  21.5 9.6 %collective-permute-start.4 = (bf16[4,200,128]{2,1,0:T(8,128)(2,1)S(1)}, bf16[4,200,128]{2,1,0:T(8,128)(2,1)S(1)}, u32[]{:S(2)}, u32[]{:S(2)}) collective-permute-start(bf16[4,200,128]{2,1,0:T(8,128)(2,1)S(1)} %get-tuple-element.12), channel_id=1, source_target_pairs={{0,1},{1,2},{2,3},{3,0},{4,5},{5,6},{6,7},{7,4},{8,9},{9,10},{10,1... | collective-permute-start | bytes 614408 | tf_op jit(solution)/shard_map/ppermute | solution.py:231
  21.9 9.2 %collective-permute-start.6 = (bf16[4,200,128]{2,1,0:T(8,128)(2,1)S(1)}, bf16[4,200,128]{2,1,0:T(8,128)(2,1)S(1)}, u32[]{:S(2)}, u32[]{:S(2)}) collective-permute-start(bf16[4,200,128]{2,1,0:T(8,128)(2,1)S(1)} %get-tuple-element.12), channel_id=1, source_target_pairs={{0,3},{1,0},{2,1},{3,2},{4,7},{5,4},{6,5},{7,6},{8,11},{9,8},{10,9... | collective-permute-start | bytes 614408 | tf_op jit(solution)/shard_map/ppermute | solution.py:231
  32.7 2.4 %collective-permute-start.7 = (bf16[80,5120]{1,0:T(8,128)(2,1)S(1)}, bf16[80,5120]{1,0:T(8,128)(2,1)S(1)}, u32[]{:S(2)}, u32[]{:S(2)}) collective-permute-start(bf16[80,5120]{1,0:T(8,128)(2,1)S(1)} %bitcast.21), channel_id=1, source_target_pairs={{0,32},{32,0},{1,33},{33,1},{2,34},{34,2},{3,35},{35,3},{4,36},{36... | collective-permute-start | bytes 2457608 | tf_op jit(solution)/shard_map/ppermute | solution.py:235
  43.9 39.9 %all-to-all-start = ((s16[32,64,128]{2,1,0:T(8,128)(2,1)}), s16[32,64,128]{2,1,0:T(8,128)(2,1)S(1)}, u32[]{:S(2)}, u32[]{:S(2)}) async-start(s16[32,64,128]{2,1,0:T(8,128)(2,1)} %get-tuple-element.7), calls=%async_computation | async-start | bytes 1048576 | tf_op jit(solution)/shard_map/all_to_all | solution.py:275
  51.0 1.6 %collective-permute-start.8 = (f32[8,128]{1,0:T(8,128)S(1)}, f32[8,128]{1,0:T(8,128)S(1)}, u32[]{:S(2)}, u32[]{:S(2)}) collective-permute-start(f32[8,128]{1,0:T(8,128)S(1)} %get-tuple-element.10), channel_id=1, source_target_pairs={{0,32},{32,0},{1,33},{33,1},{2,34},{34,2},{3,35},{35,3},{4,36},{36... | collective-permute-start | bytes 12296 | tf_op jit(solution)/shard_map/ppermute | solution.py:307
  52.5 3.6 %collective-permute-start.11 = (f32[8,128]{1,0:T(8,128)S(1)}, f32[8,128]{1,0:T(8,128)S(1)}, u32[]{:S(2)}, u32[]{:S(2)}) collective-permute-start(f32[8,128]{1,0:T(8,128)S(1)} %add.12.own), channel_id=1, source_target_pairs={{0,192},{64,0},{128,64},{192,128},{1,193},{65,1},{129,65},{193,129... | collective-permute-start | bytes 12296 | tf_op jit(solution)/shard_map/ppermute | solution.py:292
  55.0 4.3 %collective-permute-start.10 = (f32[8,128]{1,0:T(8,128)S(1)}, f32[8,128]{1,0:T(8,128)S(1)}, u32[]{:S(2)}, u32[]{:S(2)}) collective-permute-start(f32[8,128]{1,0:T(8,128)S(1)} %add.12.own), channel_id=1, source_target_pairs={{0,128},{64,192},{128,0},{192,64},{1,129},{65,193},{129,1},{193,65... | collective-permute-start | bytes 12296 | tf_op jit(solution)/shard_map/ppermute | solution.py:292
  55.5 4.0 %collective-permute-start.9 = (f32[8,128]{1,0:T(8,128)S(1)}, f32[8,128]{1,0:T(8,128)S(1)}, u32[]{:S(2)}, u32[]{:S(2)}) collective-permute-start(f32[8,128]{1,0:T(8,128)S(1)} %add.12.own), channel_id=1, source_target_pairs={{0,64},{64,128},{128,192},{192,0},{1,65},{65,129},{129,193},{193,1... | collective-permute-start | bytes 12296 | tf_op jit(solution)/shard_map/ppermute | solution.py:292
  59.5 4.0 %collective-permute-start.14 = (f32[8,128]{1,0:T(8,128)S(1)}, f32[8,128]{1,0:T(8,128)S(1)}, u32[]{:S(2)}, u32[]{:S(2)}) collective-permute-start(f32[8,128]{1,0:T(8,128)S(1)} %ring_sum.2.own), channel_id=1, source_target_pairs={{0,3},{1,0},{2,1},{3,2},{4,7},{5,4},{6,5},{7,6},{8,11},{9,8},{10,9... | collective-permute-start | bytes 12296 | tf_op jit(solution)/shard_map/ppermute | solution.py:292
  62.3 4.3 %collective-permute-start.13 = (f32[8,128]{1,0:T(8,128)S(1)}, f32[8,128]{1,0:T(8,128)S(1)}, u32[]{:S(2)}, u32[]{:S(2)}) collective-permute-start(f32[8,128]{1,0:T(8,128)S(1)} %ring_sum.2.own), channel_id=1, source_target_pairs={{0,2},{1,3},{2,0},{3,1},{4,6},{5,7},{6,4},{7,5},{8,10},{9,11},{10,... | collective-permute-start | bytes 12296 | tf_op jit(solution)/shard_map/ppermute | solution.py:292
  62.9 4.0 %collective-permute-start.12 = (f32[8,128]{1,0:T(8,128)S(1)}, f32[8,128]{1,0:T(8,128)S(1)}, u32[]{:S(2)}, u32[]{:S(2)}) collective-permute-start(f32[8,128]{1,0:T(8,128)S(1)} %ring_sum.2.own), channel_id=1, source_target_pairs={{0,1},{1,2},{2,3},{3,0},{4,5},{5,6},{6,7},{7,4},{8,9},{9,10},{10,1... | collective-permute-start | bytes 12296 | tf_op jit(solution)/shard_map/ppermute | solution.py:292
  66.9 11.0 %collective-permute-start.18 = (f32[8,128]{1,0:T(8,128)S(1)}, f32[8,128]{1,0:T(8,128)S(1)}, u32[]{:S(2)}, u32[]{:S(2)}) collective-permute-start(f32[8,128]{1,0:T(8,128)S(1)} %ring_sum.3.own), channel_id=1, source_target_pairs={{32,48},{36,52},{40,56},{44,60},{48,32},{52,36},{56,40},{60,44},{3... | collective-permute-start | bytes 12296 | tf_op jit(solution)/shard_map/ppermute | solution.py:212
  73.6 4.4 %collective-permute-start.17 = (f32[8,128]{1,0:T(8,128)S(1)}, f32[8,128]{1,0:T(8,128)S(1)}, u32[]{:S(2)}, u32[]{:S(2)}) collective-permute-start(f32[8,128]{1,0:T(8,128)S(1)} %ring_sum.3.own), channel_id=1, source_target_pairs={{0,12},{4,16},{8,20},{12,24},{16,28},{20,0},{24,4},{28,8},{32,52},... | collective-permute-start | bytes 12296 | tf_op jit(solution)/shard_map/ppermute | solution.py:210
  74.4 3.6 %collective-permute-start.16 = (f32[8,128]{1,0:T(8,128)S(1)}, f32[8,128]{1,0:T(8,128)S(1)}, u32[]{:S(2)}, u32[]{:S(2)}) collective-permute-start(f32[8,128]{1,0:T(8,128)S(1)} %ring_sum.3.own), channel_id=1, source_target_pairs={{0,8},{4,12},{8,16},{12,20},{16,24},{20,28},{24,0},{28,4},{32,56},... | collective-permute-start | bytes 12296 | tf_op jit(solution)/shard_map/ppermute | solution.py:210
  76.7 2.6 %collective-permute-start.15 = (f32[8,128]{1,0:T(8,128)S(1)}, f32[8,128]{1,0:T(8,128)S(1)}, u32[]{:S(2)}, u32[]{:S(2)}) collective-permute-start(f32[8,128]{1,0:T(8,128)S(1)} %ring_sum.3.own), channel_id=1, source_target_pairs={{0,4},{4,8},{8,12},{12,16},{16,20},{20,24},{24,28},{28,0},{32,60},... | collective-permute-start | bytes 12296 | tf_op jit(solution)/shard_map/ppermute | solution.py:210
  80.0 3.1 %collective-permute-start.19 = (f32[8,8,128]{2,1,0:T(8,128)S(1)}, f32[8,8,128]{2,1,0:T(8,128)S(1)}, u32[]{:S(2)}, u32[]{:S(2)}) collective-permute-start(f32[8,8,128]{2,1,0:T(8,128)S(1)} %ring_slots.1.mine), channel_id=1, source_target_pairs={{0,32},{32,0},{1,33},{33,1},{2,34},{34,2},{3,35},{35,3},{4,36},{36... | collective-permute-start | bytes 98312 | tf_op jit(solution)/shard_map/ppermute | solution.py:326

commit v5 on v3

--- a/solution.py
+++ b/solution.py
@@ -14,6 +14,7 @@
 DP = ("dp_0", "dp_1")
 DP_EXPERT = ("dp_0", "dp_1", "expert_0", "expert_1")
 BLOCK = 256
+PIECES = 1
 LANES = 128
 ROWS = 8
 TOP_CODE = 65535.0
@@ -64,62 +65,93 @@
     return base * (1.0 + unit(fine) * 16.0 / jnp.maximum(coarse, 1.0))
 
 
-def source_device(core, place, row, half, sizes):
+def source_devices(core, place, sizes):
     deep, wide = sizes
     z, y = place
+    row = jnp.arange(deep * wide, dtype=jnp.int32)
     back = row % (deep // 2)
     aside = (row // (deep // 2)) % wide
+    half = row // (deep * wide // 2)
     ahead = jnp.where(back == 0, deep // 2, back)
     offset = jnp.where(core == half, deep - back, ahead)
     return ((z + offset) % deep) * wide + (y + wide - aside) % wide
 
 
+def lined(total, index):
+    lanes = lax.broadcasted_iota(jnp.int32, index.shape, 1)
+    return [
+        jnp.sum(jnp.where(index == lanes + i * LANES, total, 0.0), axis=0, keepdims=True) for i in range(2)
+    ]
+
+
+def count_kernel(num_devices, per_device, picks, devs, out):
+    num_experts = num_devices * per_device
+    share = picks.shape[1]
+    counts, sent = [], []
+    for j in range(per_device):
+        ids = lax.broadcasted_iota(jnp.int32, (num_devices, LANES), 0) * per_device + j
+        total = jnp.zeros((num_devices, LANES), jnp.float32)
+        for c in range(0, share, LANES):
+            for k in range(TOP):
+                total += jnp.where(ids == picks[k : k + 1, c : c + LANES], 1.0, 0.0)
+        counts.append(jnp.sum(total, axis=1, keepdims=True))
+    ids = lax.broadcasted_iota(jnp.int32, (num_devices, LANES), 0)
+    total = jnp.zeros((num_devices, LANES), jnp.float32)
+    for c in range(0, share, LANES):
+        for k in range(DEV_TOP):
+            total += jnp.where(ids == devs[k : k + 1, c : c + LANES], 1.0, 0.0)
+    rows = lax.broadcasted_iota(jnp.int32, (num_experts, LANES), 0)
+    low, high = lined(jnp.concatenate(counts, axis=0), rows)
+    sent_low, sent_high = lined(jnp.sum(total, axis=1, keepdims=True), ids)
+    none = jnp.zeros((ROWS - 4, LANES), jnp.float32)
+    out[...] = jnp.concatenate([low, high, sent_low, sent_high, none], axis=0)
+
+
 def route_kernel(
-    sizes, per_device, where, own, other, tokens, picks, devs, out, router, prob_acc, count_acc, sent_acc
+    num_devices, per_device, where, own, other, tokens, picks, counts, out, router, ids, blocks, arrived, prob_acc
 ):
     step = pl.program_id(0)
-    deep, wide = sizes
-    num_devices = deep * wide
     num_experts = num_devices * per_device
     group = num_devices // 2
     rows_half = num_experts // 2
-    block = tokens.shape[1]
+    steps, features, block = blocks.shape
     tiles = block // LANES
-    share = block * pl.num_programs(0)
-    core, place = where[1], (where[2], where[3])
+    share = block * steps
+    depth = features // PIECES
+
+    def piece(i, p):
+        rows = pl.ds(p * depth, depth)
+        cols = pl.ds(i * block, block)
+        return pltpu.make_async_copy(tokens.at[rows, cols], blocks.at[i, rows, :], arrived.at[i, p])
 
     @pl.when(step == 0)
     def _():
+        for i in range(steps):
+            for p in range(PIECES):
+                piece(i, p).start()
         router[:rows_half] = own[...]
         router[rows_half:] = other[...]
         prob_acc[...] = jnp.zeros_like(prob_acc)
-        count_acc[...] = jnp.zeros_like(count_acc)
-        sent_acc[...] = jnp.zeros_like(sent_acc)
-
-    row = lax.broadcasted_iota(jnp.int32, (num_experts, LANES), 0)
-    half = row // rows_half
-    dev = source_device(core, place, row % group, half, sizes)
-    slot = (row % rows_half) // group
-    ids = dev * per_device + slot
-    ids_wide = jnp.concatenate([ids] * tiles, axis=1)
-
-    scores = jnp.dot(router[...], tokens[...], preferred_element_type=jnp.float32)
+        row = lax.broadcasted_iota(jnp.int32, (group, LANES), 0)
+        for h in range(2):
+            dev = jnp.zeros((group, LANES), jnp.int32)
+            for s in range(group):
+                dev = jnp.where(row == s, where[h * group + s], dev)
+            for j in range(per_device):
+                ids[pl.ds(h * rows_half + j * group, group), :] = dev * per_device + j
+
+    for p in range(PIECES):
+        piece(step, p).wait()
+    scores = jnp.dot(router[...], blocks[step], preferred_element_type=jnp.float32)
     peak = jnp.max(scores, axis=0, keepdims=True)
     raised = jnp.exp(scores - peak)
-    probs = raised / jnp.sum(raised, axis=0, keepdims=True)
+    probs = raised * (1.0 / jnp.sum(raised, axis=0, keepdims=True))
     prob_acc[...] += lane_sum(probs)
-    chosen = []
-    hits = jnp.zeros((num_experts, block), jnp.float32)
-    for k in range(TOP):
-        mask = ids_wide == picks[k : k + 1, :]
-        chosen.append(jnp.sum(jnp.where(mask, probs, 0.0), axis=0, keepdims=True))
-        hits += jnp.where(mask, 1.0, 0.0)
-    count_acc[...] += lane_sum(hits)
-    dev_ids = lax.broadcasted_iota(jnp.int32, (num_devices, block), 0)
-    sent = jnp.zeros((num_devices, block), jnp.float32)
-    for k in range(DEV_TOP):
-        sent += jnp.where(dev_ids == devs[k : k + 1, :], 1.0, 0.0)
-    sent_acc[...] += lane_sum(sent)
+    ids_wide = jnp.concatenate([ids[...]] * tiles, axis=1)
+    chosen = [
+        jnp.sum(jnp.where(ids_wide == picks[k : k + 1, :], probs, 0.0), axis=0, keepdims=True)
+        for k in range(TOP)
+    ]
 
     largest = functools.reduce(jnp.maximum, chosen)
     scale = jnp.minimum(jnp.floor(eighth_root(largest) * TOP_CODE) + 1.0, TOP_CODE)
@@ -127,7 +159,7 @@
     codes = [jnp.minimum(jnp.round(g * inverse), TOP_CODE) for g in chosen]
     lines = jnp.concatenate([*codes, scale, scale], axis=0).astype(jnp.int32) - MIDDLE
     stacked = jnp.concatenate([lines[:, j * LANES : (j + 1) * LANES] for j in range(tiles)], axis=0)
-    last = lax.broadcasted_iota(jnp.int32, stacked.shape, 0) % ROWS == ROWS - 1
+    last = (lax.broadcasted_iota(jnp.int32, stacked.shape, 0) & (ROWS - 1)) == ROWS - 1
     here = pl.ds(pl.multiple_of(step * tiles * ROWS, tiles * ROWS), tiles * ROWS)
     for h in range(2):
         slabs = [probs[h * rows_half + j * group : h * rows_half + (j + 1) * group] for j in range(per_device)]
@@ -142,31 +174,56 @@
                 ],
                 axis=0,
             )
-            target = source_device(core, place, s, h, sizes)
-            out[target, here, :] = jnp.where(last, line, stacked).astype(jnp.int16)
-
-    @pl.when(step == pl.num_programs(0) - 1)
+            out[where[h * group + s], here, :] = jnp.where(last, line, stacked).astype(jnp.int16)
+
+    @pl.when(step == steps - 1)
     def _():
-        def lined(acc, index):
-            total = jnp.sum(acc[...], axis=1, keepdims=True)
-            lanes = lax.broadcasted_iota(jnp.int32, index.shape, 1)
-            parts = [
-                jnp.sum(jnp.where(index == lanes + i * LANES, total, 0.0), axis=0, keepdims=True) for i in range(2)
-            ]
-            return parts
-
-        order = slot * num_devices + dev
-        low, high = lined(prob_acc, order)
+        expert = ids[...]
+        dev = jnp.zeros_like(expert)
+        for d in range(1, num_devices):
+            dev += jnp.where(expert >= d * per_device, 1, 0)
+        order = (expert - dev * per_device) * num_devices + dev
+        low, high = lined(jnp.sum(prob_acc[...], axis=1, keepdims=True), order)
         low_coarse, low_fine = coded_pair(low, share)
         high_coarse, high_fine = coded_pair(high, share)
-        count_low, count_high = lined(count_acc, order)
-        sent_low, sent_high = lined(sent_acc, lax.broadcasted_iota(jnp.int32, (num_devices, LANES), 0))
-        sums = jnp.concatenate(
-            [low_coarse, high_coarse, low_fine, high_fine, count_low, count_high, sent_low, sent_high], axis=0
-        )
+        sums = jnp.concatenate([low_coarse, high_coarse, low_fine, high_fine, counts[0:4, :]], axis=0)
         sums = (sums.astype(jnp.int32) - MIDDLE).astype(jnp.int16)
         for d in range(num_devices):
             out[d, pl.ds(share // LANES * ROWS, ROWS), :] = sums
+
+
+def route(num_devices, per_device, where, own, other, tokens, picks, counts):
+    features, share = tokens.shape
+    num_experts = num_devices * per_device
+    rows = (share // LANES + 1) * ROWS
+    steps = share // BLOCK
+    return pl.pallas_call(
+        functools.partial(route_kernel, num_devices, per_device),
+        out_shape=jax.ShapeDtypeStruct((num_devices, rows, LANES), jnp.int16),
+        grid_spec=pltpu.PrefetchScalarGridSpec(
+            num_scalar_prefetch=1,
+            grid=(steps,),
+            in_specs=[
+                pl.BlockSpec((num_experts // 2, features), lambda i, w: (0, 0)),
+                pl.BlockSpec((num_experts // 2, features), lambda i, w: (0, 0)),
+                pl.BlockSpec(memory_space=pl.ANY),
+                pl.BlockSpec((TOP, BLOCK), lambda i, w: (0, i)),
+                pl.BlockSpec((ROWS, LANES), lambda i, w: (0, 0)),
+            ],
+            out_specs=pl.BlockSpec((num_devices, rows, LANES), lambda i, w: (0, 0, 0)),
+            scratch_shapes=[
+                pltpu.VMEM((num_experts, features), jnp.bfloat16),
+                pltpu.VMEM((num_experts, LANES), jnp.int32),
+                pltpu.VMEM((steps, features, BLOCK), jnp.bfloat16),
+                pltpu.SemaphoreType.DMA((steps, PIECES)),
+                pltpu.VMEM((num_experts, LANES), jnp.float32),
+            ],
+        ),
+        compiler_params=pltpu.CompilerParams(
+            dimension_semantics=("arbitrary",), vmem_limit_bytes=51 * 1024 * 1024
+        ),
+        name="route",
+    )(where, own, other, tokens, picks, counts)
 
 
 def decoded(codes):
@@ -248,35 +305,17 @@
     own = own.reshape(num_experts // 2, features)
     other = lax.ppermute(own, "dp_1", [(0, 1), (1, 0)])
 
-    steps = share // BLOCK
-    where = jnp.stack([my_index, core, z, y]).astype(jnp.int32)
+    where = source_devices(core, (z, y), sizes)
     rows = (share // LANES + 1) * ROWS
-    msg = pl.pallas_call(
-        functools.partial(route_kernel, sizes, per_device),
-        out_shape=jax.ShapeDtypeStruct((num_devices, rows, LANES), jnp.int16),
-        grid_spec=pltpu.PrefetchScalarGridSpec(
-            num_scalar_prefetch=1,
-            grid=(steps,),
-            in_specs=[
-                pl.BlockSpec((num_experts // 2, features), lambda i, w: (0, 0)),
-                pl.BlockSpec((num_experts // 2, features), lambda i, w: (0, 0)),
-                pl.BlockSpec((features, BLOCK), lambda i, w: (0, i)),
-                pl.BlockSpec((TOP, BLOCK), lambda i, w: (0, w[0] * steps + i)),
-                pl.BlockSpec((DEV_TOP, BLOCK), lambda i, w: (0, w[0] * steps + i)),
-            ],
-            out_specs=pl.BlockSpec((num_devices, rows, LANES), lambda i, w: (0, 0, 0)),
-            scratch_shapes=[
-                pltpu.VMEM((num_experts, features), jnp.bfloat16),
-                pltpu.VMEM((num_experts, LANES), jnp.float32),
-                pltpu.VMEM((num_experts, LANES), jnp.float32),
-                pltpu.VMEM((num_devices, LANES), jnp.float32),
-            ],
-        ),
-        compiler_params=pltpu.CompilerParams(
-            dimension_semantics=("arbitrary",), vmem_limit_bytes=51 * 1024 * 1024
-        ),
-        name="route",
-    )(where, own, other, tokens, expert_pick, device_pick)
+    experts_here = lax.dynamic_slice_in_dim(expert_pick, my_index * share, share, 1)
+    devices_here = lax.dynamic_slice_in_dim(device_pick, my_index * share, share, 1)
+    counts = pl.pallas_call(
+        functools.partial(count_kernel, num_devices, per_device),
+        out_shape=jax.ShapeDtypeStruct((ROWS, LANES), jnp.float32),
+        compiler_params=pltpu.CompilerParams(vmem_limit_bytes=2 * 1024 * 1024),
+        name="count",
+    )(experts_here, devices_here)
+    msg = route(num_devices, per_device, where, own, other, tokens, experts_here, counts)
 
     recv = lax.all_to_all(msg, EXPERT, 0, 0, tiled=True)
     sums = pl.pallas_call(

time: 79.6 us -> 77 us (0.967)
  waiting for transfers between devices: 13.4 us -> 12.1 us
  Pallas kernels: 9.84 us -> 8.84 us
    ppermute x1, waiting for transfers between devices: 1.92 us -> 0.61 us  [local(): other = lax.ppermute(own, 'dp_1', [(0, 1), (1, 0)])]
    unnamed x2, local copies, waits for them, and re-layouts: 1.04 us -> 0.01 us
    pallas_call x1 -> x2, Pallas kernels: 8.02 us -> 7.02 us  [the longest x1 6.38 us: route(): pl.pallas_call(functools.partial(route_kernel, num_devices, per_device),...]
  transfers between devices with their start and end apart: 12 -> 12, of which waited for: 10 -> 10; matrix products, arithmetic and copies ran while one was open for 0% -> 1% of each run, Pallas kernels for 2% -> 3%
where the time goes in v5:
time: 77 us; the launch traced here: 76.8 us
  starting transfers between devices  26.6 us (35%)
  blocking collectives  24.6 us (32%)
  waiting for transfers between devices  12.1 us (16%)
  Pallas kernels  8.84 us (11%)
  local copies, waits for them, and re-layouts  3.77 us (5%)
    all_to_all x1, blocking collectives, local(): recv = lax.all_to_all(msg, EXPERT, 0, 0, tiled=True)  24.6 us
    ppermute x1, starting transfers between devices, local(): lax.ppermute(block, ('dp_1', 'expert_0'), [(deep + i, deep + (i + deep //...  9.64 us
    ppermute x3, waiting for transfers between devices, local(): lax.ppermute(column, 'expert_1', [(i, (i + k) % wide) for i in range(wide)])  6.95 us
    pallas_call x1, Pallas kernels, route(): pl.pallas_call(functools.partial(route_kernel, num_devices, per_device),...  6.38 us
    ppermute x3, starting transfers between devices, local(): lax.ppermute(column, 'expert_1', [(i, (i + k) % wide) for i in range(wide)])  5.68 us
    ppermute x3, starting transfers between devices, local(): pieces.append(lax.ppermute(block, ('dp_1', 'expert_0'), pairs))  4.84 us
    ppermute x3, starting transfers between devices, local(): lax.ppermute(chip, 'dp_0', [(i, (i + k) % length) for i in range(length)])  3.6 us
    ppermute x1, starting transfers between devices, local(): chip = sums + lax.ppermute(sums, 'dp_1', [(0, 1), (1, 0)])  2.42 us
  transfers between devices with their start and end apart: 12, of which 10 were waited for; matrix products, arithmetic and copies ran while one was open for 1% of the time, Pallas kernels for 3%

profile of v5, /device:TPU:1, one launch (start us, length us, event | category | flops | bytes accessed | tf_op | source)
XLA Modules:
  0.0 76.8 jit_solution(15274272396217677323)
XLA Ops:
  0.6 0.0 copy-start
  0.6 1.1 %reshape.18 = bf16[200,128]{1,0:T(8,128)(2,1)S(1)} reshape(bf16[5,5120]{1,0:T(8,128)(2,1)} %bitcast.24) | data formatting | bytes 102400 | tf_op jit(solution)/shard_map/reshape | solution.py:290
  1.7 9.6 %collective-permute-start = (bf16[200,128]{1,0:T(8,128)(2,1)S(1)}, bf16[200,128]{1,0:T(8,128)(2,1)S(1)}, u32[]{:S(2)}, u32[]{:S(2)}) collective-permute-start(bf16[200,128]{1,0:T(8,128)(2,1)S(1)} %reshape.18), channel_id=1, source_target_pairs={{32,48},{36,52},{40,56},{44,60},{48,32},{52,36},{56,40},{60,44},{3... | collective-permute-start | bytes 153608 | tf_op jit(solution)/shard_map/ppermute | solution.py:296
  11.3 0.1 collective-permute-start.3
  11.4 4.0 %collective-permute-start.2 = (bf16[200,128]{1,0:T(8,128)(2,1)S(1)}, bf16[200,128]{1,0:T(8,128)(2,1)S(1)}, u32[]{:S(2)}, u32[]{:S(2)}) collective-permute-start(bf16[200,128]{1,0:T(8,128)(2,1)S(1)} %reshape.18), channel_id=1, source_target_pairs={{0,8},{4,12},{8,16},{12,20},{16,24},{20,28},{24,0},{28,4},{32,56},... | collective-permute-start | bytes 153608 | tf_op jit(solution)/shard_map/ppermute | solution.py:295
  15.5 0.7 collective-permute-start.1
  16.2 0.0 collective-permute-done
  16.2 0.1 collective-permute-done.3
  16.3 0.4 collective-permute-done.2
  16.7 1.7 %collective-permute-done.1 = bf16[200,128]{1,0:T(8,128)(2,1)S(1)} collective-permute-done((bf16[200,128]{1,0:T(8,128)(2,1)S(1)}, bf16[200,128]{1,0:T(8,128)(2,1)S(1)}, u32[]{:S(2)}, u32[]{:S(2)}) %collective-permute-start.1) | collective-permute-done | bytes 51232 | tf_op jit(solution)/shard_map/ppermute | solution.py:295
  18.5 3.0 %collective-permute-start.5 = (bf16[4,200,128]{2,1,0:T(8,128)(2,1)S(1)}, bf16[4,200,128]{2,1,0:T(8,128)(2,1)S(1)}, u32[]{:S(2)}, u32[]{:S(2)}) collective-permute-start(bf16[4,200,128]{2,1,0:T(8,128)(2,1)S(1)} %get-tuple-element.8), channel_id=1, source_target_pairs={{0,2},{1,3},{2,0},{3,1},{4,6},{5,7},{6,4},{7,5},{8,10},{9,11},{10,... | collective-permute-start | bytes 614408 | tf_op jit(solution)/shard_map/ppermute | solution.py:302
  21.5 0.4 collective-permute-start.4
  21.9 2.3 %collective-permute-start.6 = (bf16[4,200,128]{2,1,0:T(8,128)(2,1)S(1)}, bf16[4,200,128]{2,1,0:T(8,128)(2,1)S(1)}, u32[]{:S(2)}, u32[]{:S(2)}) collective-permute-start(bf16[4,200,128]{2,1,0:T(8,128)(2,1)S(1)} %get-tuple-element.8), channel_id=1, source_target_pairs={{0,3},{1,0},{2,1},{3,2},{4,7},{5,4},{6,5},{7,6},{8,11},{9,8},{10,9... | collective-permute-start | bytes 614408 | tf_op jit(solution)/shard_map/ppermute | solution.py:302
  24.2 2.7 %collective-permute-done.5 = bf16[4,200,128]{2,1,0:T(8,128)(2,1)S(1)} collective-permute-done((bf16[4,200,128]{2,1,0:T(8,128)(2,1)S(1)}, bf16[4,200,128]{2,1,0:T(8,128)(2,1)S(1)}, u32[]{:S(2)}, u32[]{:S(2)}) %collective-permute-start.5) | collective-permute-done | bytes 204832 | tf_op jit(solution)/shard_map/ppermute | solution.py:302
  26.9 4.2 %collective-permute-done.4 = bf16[4,200,128]{2,1,0:T(8,128)(2,1)S(1)} collective-permute-done((bf16[4,200,128]{2,1,0:T(8,128)(2,1)S(1)}, bf16[4,200,128]{2,1,0:T(8,128)(2,1)S(1)}, u32[]{:S(2)}, u32[]{:S(2)}) %collective-permute-start.4) | collective-permute-done | bytes 204832 | tf_op jit(solution)/shard_map/ppermute | solution.py:302
  31.0 0.1 collective-permute-done.6
  31.1 0.1 pad_maximum_fusion
  31.2 0.9 %reshape.19 = bf16[16,5,5120]{2,1,0:T(8,128)(2,1)S(1)} reshape(bf16[4,4,200,128]{3,2,1,0:T(8,128)(2,1)S(1)} %pad_maximum_fusion) | data formatting | bytes 1638400 | tf_op jit(solution)/shard_map/reshape | solution.py:304
  32.1 0.5 copy.7
  32.7 0.4 collective-permute-start.7
  33.1 0.7 constant_dynamic-slice_fusion.devs
  33.8 0.0 copy-done
  33.8 0.6 count.1.counts
  34.5 0.6 collective-permute-done.7.other
  35.1 6.4 %route.1 = s16[32,72,128]{2,1,0:T(8,128)(2,1)S(1)} custom-call(s32[32]{0:T(128)S(1)} %fusion.where, bf16[80,5120]{1,0:T(8,128)(2,1)S(1)} %bitcast.19, bf16[80,5120]{1,0:T(8,128)(2,1)S(1)} %collective-permute-done.7.other, bf16[5120,1024]{1,0:T(8,128)(2,1)} %tokens.1, s32[6,1024]{1,0:T(8,128)S(1)} %constant_dynamic-slice_fusion.1.picks, f32[8,128]{1,0:T(8,128)S(1)} %count.1.counts), custom_call_target="tpu_custom_call" | custom-call | tf_op jit(solution)/shard_map/route/pallas_call | solution.py:200
  41.5 24.6 %all_to_all.5.recv = s16[32,72,128]{2,1,0:T(8,128)(2,1)S(1)} all-to-all(s16[32,72,128]{2,1,0:T(8,128)(2,1)S(1)} %route.1), channel_id=1, replica_groups=mesh['dp_0'=4,'dp_1'=2,'expert_0'=8,'expert_1'=4] {'expert_0','expert_1'}, dimensions={0} | all-to-all | bytes 1179648 | tf_op jit(solution)/shard_map/all_to_all | solution.py:320
  66.1 0.1 sums.1
  66.2 2.4 %collective-permute-start.8 = (f32[8,128]{1,0:T(8,128)S(1)}, f32[8,128]{1,0:T(8,128)S(1)}, u32[]{:S(2)}, u32[]{:S(2)}) collective-permute-start(f32[8,128]{1,0:T(8,128)S(1)} %sums.1), channel_id=1, source_target_pairs={{0,32},{32,0},{1,33},{33,1},{2,34},{34,2},{3,35},{35,3},{4,36},{36... | collective-permute-start | bytes 12296 | tf_op jit(solution)/shard_map/ppermute | solution.py:339
  68.6 0.8 %collective-permute-done.8 = f32[8,128]{1,0:T(8,128)S(1)} collective-permute-done((f32[8,128]{1,0:T(8,128)S(1)}, f32[8,128]{1,0:T(8,128)S(1)}, u32[]{:S(2)}, u32[]{:S(2)}) %collective-permute-start.8) | collective-permute-done | bytes 4128 | tf_op jit(solution)/shard_map/ppermute | solution.py:339
  69.4 2.5 %collective-permute-start.11 = (f32[8,128]{1,0:T(8,128)S(1)}, f32[8,128]{1,0:T(8,128)S(1)}, u32[]{:S(2)}, u32[]{:S(2)}) collective-permute-start(f32[8,128]{1,0:T(8,128)S(1)} %add.54.own), channel_id=1, source_target_pairs={{0,192},{64,0},{128,64},{192,128},{1,193},{65,1},{129,65},{193,129... | collective-permute-start | bytes 12296 | tf_op jit(solution)/shard_map/ppermute | solution.py:342
  71.9 0.5 collective-permute-start.10
  72.4 0.6 collective-permute-start.9
  73.0 1.5 %spread.1 = (f32[6,32768]{1,0:T(8,128)}, f32[1,32768]{1,0:T(1,128)}) custom-call(s16[32,72,128]{2,1,0:T(8,128)(2,1)S(1)} %all_to_all.5.recv), custom_call_target="tpu_custom_call" | custom-call | tf_op jit(solution)/shard_map/spread/pallas_call | solution.py:330
  74.6 0.0 collective-permute-done.11.third
  74.6 1.3 %collective-permute-done.10.second = f32[8,128]{1,0:T(8,128)S(1)} collective-permute-done((f32[8,128]{1,0:T(8,128)S(1)}, f32[8,128]{1,0:T(8,128)S(1)}, u32[]{:S(2)}, u32[]{:S(2)}) %collective-permute-start.10) | collective-permute-done | bytes 4128 | tf_op jit(solution)/shard_map/ppermute | solution.py:342
  75.9 0.2 collective-permute-done.9.first
  76.1 0.2 balance.1
  76.3 0.5 slice_bitcast_fusion
  (5 shorter events, 0.1 us)
Async XLA Ops:
  0.6 33.2 %copy-start = (s32[6,32768]{1,0:T(8,128)S(1)}, s32[6,32768]{1,0:T(8,128)}, u32[]{:S(2)}) copy-start(s32[6,32768]{1,0:T(8,128)} %param.7) | copy-start | bytes 2359300
  1.7 14.5 %collective-permute-start = (bf16[200,128]{1,0:T(8,128)(2,1)S(1)}, bf16[200,128]{1,0:T(8,128)(2,1)S(1)}, u32[]{:S(2)}, u32[]{:S(2)}) collective-permute-start(bf16[200,128]{1,0:T(8,128)(2,1)S(1)} %reshape.18), channel_id=1, source_target_pairs={{32,48},{36,52},{40,56},{44,60},{48,32},{52,36},{56,40},{60,44},{3... | collective-permute-start | bytes 153608 | tf_op jit(solution)/shard_map/ppermute | solution.py:296
  11.3 4.9 %collective-permute-start.3 = (bf16[200,128]{1,0:T(8,128)(2,1)S(1)}, bf16[200,128]{1,0:T(8,128)(2,1)S(1)}, u32[]{:S(2)}, u32[]{:S(2)}) collective-permute-start(bf16[200,128]{1,0:T(8,128)(2,1)S(1)} %reshape.18), channel_id=1, source_target_pairs={{0,12},{4,16},{8,20},{12,24},{16,28},{20,0},{24,4},{28,8},{32,52},... | collective-permute-start | bytes 153608 | tf_op jit(solution)/shard_map/ppermute | solution.py:295
  11.4 5.3 %collective-permute-start.2 = (bf16[200,128]{1,0:T(8,128)(2,1)S(1)}, bf16[200,128]{1,0:T(8,128)(2,1)S(1)}, u32[]{:S(2)}, u32[]{:S(2)}) collective-permute-start(bf16[200,128]{1,0:T(8,128)(2,1)S(1)} %reshape.18), channel_id=1, source_target_pairs={{0,8},{4,12},{8,16},{12,20},{16,24},{20,28},{24,0},{28,4},{32,56},... | collective-permute-start | bytes 153608 | tf_op jit(solution)/shard_map/ppermute | solution.py:295
  15.5 3.0 %collective-permute-start.1 = (bf16[200,128]{1,0:T(8,128)(2,1)S(1)}, bf16[200,128]{1,0:T(8,128)(2,1)S(1)}, u32[]{:S(2)}, u32[]{:S(2)}) collective-permute-start(bf16[200,128]{1,0:T(8,128)(2,1)S(1)} %reshape.18), channel_id=1, source_target_pairs={{0,4},{4,8},{8,12},{12,16},{16,20},{20,24},{24,28},{28,0},{32,60},... | collective-permute-start | bytes 153608 | tf_op jit(solution)/shard_map/ppermute | solution.py:295
  18.5 8.4 %collective-permute-start.5 = (bf16[4,200,128]{2,1,0:T(8,128)(2,1)S(1)}, bf16[4,200,128]{2,1,0:T(8,128)(2,1)S(1)}, u32[]{:S(2)}, u32[]{:S(2)}) collective-permute-start(bf16[4,200,128]{2,1,0:T(8,128)(2,1)S(1)} %get-tuple-element.8), channel_id=1, source_target_pairs={{0,2},{1,3},{2,0},{3,1},{4,6},{5,7},{6,4},{7,5},{8,10},{9,11},{10,... | collective-permute-start | bytes 614408 | tf_op jit(solution)/shard_map/ppermute | solution.py:302
  21.5 9.6 %collective-permute-start.4 = (bf16[4,200,128]{2,1,0:T(8,128)(2,1)S(1)}, bf16[4,200,128]{2,1,0:T(8,128)(2,1)S(1)}, u32[]{:S(2)}, u32[]{:S(2)}) collective-permute-start(bf16[4,200,128]{2,1,0:T(8,128)(2,1)S(1)} %get-tuple-element.8), channel_id=1, source_target_pairs={{0,1},{1,2},{2,3},{3,0},{4,5},{5,6},{6,7},{7,4},{8,9},{9,10},{10,1... | collective-permute-start | bytes 614408 | tf_op jit(solution)/shard_map/ppermute | solution.py:302
  21.9 9.2 %collective-permute-start.6 = (bf16[4,200,128]{2,1,0:T(8,128)(2,1)S(1)}, bf16[4,200,128]{2,1,0:T(8,128)(2,1)S(1)}, u32[]{:S(2)}, u32[]{:S(2)}) collective-permute-start(bf16[4,200,128]{2,1,0:T(8,128)(2,1)S(1)} %get-tuple-element.8), channel_id=1, source_target_pairs={{0,3},{1,0},{2,1},{3,2},{4,7},{5,4},{6,5},{7,6},{8,11},{9,8},{10,9... | collective-permute-start | bytes 614408 | tf_op jit(solution)/shard_map/ppermute | solution.py:302
  32.7 2.4 %collective-permute-start.7 = (bf16[80,5120]{1,0:T(8,128)(2,1)S(1)}, bf16[80,5120]{1,0:T(8,128)(2,1)S(1)}, u32[]{:S(2)}, u32[]{:S(2)}) collective-permute-start(bf16[80,5120]{1,0:T(8,128)(2,1)S(1)} %bitcast.18), channel_id=1, source_target_pairs={{0,32},{32,0},{1,33},{33,1},{2,34},{34,2},{3,35},{35,3},{4,36},{36... | collective-permute-start | bytes 2457608 | tf_op jit(solution)/shard_map/ppermute | solution.py:306
  66.2 3.2 %collective-permute-start.8 = (f32[8,128]{1,0:T(8,128)S(1)}, f32[8,128]{1,0:T(8,128)S(1)}, u32[]{:S(2)}, u32[]{:S(2)}) collective-permute-start(f32[8,128]{1,0:T(8,128)S(1)} %sums.1), channel_id=1, source_target_pairs={{0,32},{32,0},{1,33},{33,1},{2,34},{34,2},{3,35},{35,3},{4,36},{36... | collective-permute-start | bytes 12296 | tf_op jit(solution)/shard_map/ppermute | solution.py:339
  69.4 5.2 %collective-permute-start.11 = (f32[8,128]{1,0:T(8,128)S(1)}, f32[8,128]{1,0:T(8,128)S(1)}, u32[]{:S(2)}, u32[]{:S(2)}) collective-permute-start(f32[8,128]{1,0:T(8,128)S(1)} %add.54.own), channel_id=1, source_target_pairs={{0,192},{64,0},{128,64},{192,128},{1,193},{65,1},{129,65},{193,129... | collective-permute-start | bytes 12296 | tf_op jit(solution)/shard_map/ppermute | solution.py:342
  71.9 4.0 %collective-permute-start.10 = (f32[8,128]{1,0:T(8,128)S(1)}, f32[8,128]{1,0:T(8,128)S(1)}, u32[]{:S(2)}, u32[]{:S(2)}) collective-permute-start(f32[8,128]{1,0:T(8,128)S(1)} %add.54.own), channel_id=1, source_target_pairs={{0,128},{64,192},{128,0},{192,64},{1,129},{65,193},{129,1},{193,65... | collective-permute-start | bytes 12296 | tf_op jit(solution)/shard_map/ppermute | solution.py:342
  72.4 3.7 %collective-permute-start.9 = (f32[8,128]{1,0:T(8,128)S(1)}, f32[8,128]{1,0:T(8,128)S(1)}, u32[]{:S(2)}, u32[]{:S(2)}) collective-permute-start(f32[8,128]{1,0:T(8,128)S(1)} %add.54.own), channel_id=1, source_target_pairs={{0,64},{64,128},{128,192},{192,0},{1,65},{65,129},{129,193},{193,1... | collective-permute-start | bytes 12296 | tf_op jit(solution)/shard_map/ppermute | solution.py:342

commit v6 on v5

--- a/solution.py
+++ b/solution.py
@@ -252,10 +252,12 @@
             maxima[:, cols] = fourth(unit(tile[TOP + 1 : TOP + 2]))
 
 
-def balance_kernel(num_devices, per_device, total_tokens, where, own, first, second, third, out, slots):
-    place = where[0]
-    for k, part in enumerate((own, first, second, third)):
-        slots[(place + 4 - k) % 4] = part[...]
+def balance_kernel(num_devices, per_device, total_tokens, where, own, near, far, swapped, out, slots):
+    place, core = where[0], where[1]
+    slots[place] = own[...]
+    slots[(place + jnp.where(core == 0, 3, 1)) % 4] = near[...]
+    slots[(place + 2) % 4] = far[...]
+    slots[(place + jnp.where(core == 0, 1, 3)) % 4] = swapped[...]
     total = (slots[0] + slots[1]) + (slots[2] + slots[3])
     num_experts = num_devices * per_device
     prob = jnp.concatenate([total[0:1], total[1:2]], axis=1)[:, :num_experts] / total_tokens
@@ -301,7 +303,8 @@
     plane = [column] + [
         lax.ppermute(column, "expert_1", [(i, (i + k) % wide) for i in range(wide)]) for k in range(1, wide)
     ]
-    own = jnp.stack(plane).reshape(group, per_device, features).transpose(1, 0, 2)
+    tall = features // LANES
+    own = jnp.stack(plane).reshape(group, per_device, tall, LANES).transpose(1, 0, 2, 3)
     own = own.reshape(num_experts // 2, features)
     other = lax.ppermute(own, "dp_1", [(0, 1), (1, 0)])
 
@@ -336,11 +339,14 @@
         compiler_params=pltpu.CompilerParams(vmem_limit_bytes=16 * 1024 * 1024),
         name="spread",
     )(recv)
-    chip = sums + lax.ppermute(sums, "dp_1", [(0, 1), (1, 0)])
+    swap = [(0, 1), (1, 0)]
+    chip = sums + lax.ppermute(sums, "dp_1", swap)
     length = lax.axis_size("dp_0")
-    others = [
-        lax.ppermute(chip, "dp_0", [(i, (i + k) % length) for i in range(length)]) for k in range(1, length)
-    ]
+    around = [(2 * i, (2 * i + 2) % (2 * length)) for i in range(length)]
+    around += [(2 * i + 1, (2 * i - 1) % (2 * length)) for i in range(length)]
+    near = lax.ppermute(chip, ("dp_0", "dp_1"), around)
+    far = lax.ppermute(chip, "dp_0", [(i, (i + length // 2) % length) for i in range(length)])
+    swapped = lax.ppermute(near, "dp_1", swap)
     balance = pl.pallas_call(
         functools.partial(balance_kernel, num_devices, per_device, total_tokens),
         out_shape=jax.ShapeDtypeStruct((1, LANES), jnp.float32),
@@ -353,7 +359,7 @@
         ),
         compiler_params=pltpu.CompilerParams(vmem_limit_bytes=1024 * 1024),
         name="balance",
-    )(lax.axis_index("dp_0").astype(jnp.int32).reshape(1), chip, *others)
+    )(jnp.stack([lax.axis_index("dp_0"), core]).astype(jnp.int32), chip, near, far, swapped)
     return (gates, device_max, balance[0, 0:3])
 
 

time: 77 us -> 76.4 us (level)
  waiting for transfers between devices: 12.1 us -> 10.8 us
  starting transfers between devices: 26.6 us -> 27.9 us
  local copies, waits for them, and re-layouts: 3.77 us -> 2.51 us
    ppermute x4, starting transfers between devices: 6.02 us -> 7.35 us  [the longest x1 2.48 us: local(): near = lax.ppermute(chip, ('dp_0', 'dp_1'), around)]
    ppermute x4, waiting for transfers between devices: 2.34 us -> 1.06 us  [the longest x1 0.82 us: local(): chip = sums + lax.ppermute(sums, 'dp_1', swap)]
    reshape x1 -> x0, local copies, waits for them, and re-layouts: 0.92 us -> none  [local(): jnp.stack(plane).reshape(group, per_device, features).transpose(1, 0, 2)]
  transfers between devices with their start and end apart: 12 -> 12, of which waited for: 10 -> 9; matrix products, arithmetic and copies ran while one was open for 1% -> 1% of each run, Pallas kernels for 3% -> 3%
where the time goes in v6:
time: 76.4 us; the launch traced here: 76.2 us
  starting transfers between devices  27.9 us (37%)
  blocking collectives  24.6 us (32%)
  waiting for transfers between devices  10.8 us (14%)
  Pallas kernels  9.4 us (12%)
  local copies, waits for them, and re-layouts  2.51 us (3%)
    all_to_all x1, blocking collectives, local(): recv = lax.all_to_all(msg, EXPERT, 0, 0, tiled=True)  24.6 us
    ppermute x1, starting transfers between devices, local(): lax.ppermute(block, ('dp_1', 'expert_0'), [(deep + i, deep + (i + deep //...  9.64 us
    ppermute x3, waiting for transfers between devices, local(): lax.ppermute(column, 'expert_1', [(i, (i + k) % wide) for i in range(wide)])  6.95 us
    pallas_call x1, Pallas kernels, route(): pl.pallas_call(functools.partial(route_kernel, num_devices, per_device),...  6.39 us
    ppermute x3, starting transfers between devices, local(): lax.ppermute(column, 'expert_1', [(i, (i + k) % wide) for i in range(wide)])  5.68 us
    ppermute x3, starting transfers between devices, local(): pieces.append(lax.ppermute(block, ('dp_1', 'expert_0'), pairs))  4.84 us
    ppermute x1, starting transfers between devices, local(): near = lax.ppermute(chip, ('dp_0', 'dp_1'), around)  2.48 us
    ppermute x1, starting transfers between devices, local(): chip = sums + lax.ppermute(sums, 'dp_1', swap)  2.42 us
  transfers between devices with their start and end apart: 12, of which 9 were waited for; matrix products, arithmetic and copies ran while one was open for 1% of the time, Pallas kernels for 3%

profile of v6, /device:TPU:1, one launch (start us, length us, event | category | flops | bytes accessed | tf_op | source)
XLA Modules:
  0.0 76.2 jit_solution(15903719767418774252)
XLA Ops:
  0.6 0.0 copy-start
  0.6 1.1 %reshape.15 = bf16[200,128]{1,0:T(8,128)(2,1)S(1)} reshape(bf16[5,5120]{1,0:T(8,128)(2,1)} %bitcast.30) | data formatting | bytes 102400 | tf_op jit(solution)/shard_map/reshape | solution.py:292
  1.7 9.6 %collective-permute-start = (bf16[200,128]{1,0:T(8,128)(2,1)S(1)}, bf16[200,128]{1,0:T(8,128)(2,1)S(1)}, u32[]{:S(2)}, u32[]{:S(2)}) collective-permute-start(bf16[200,128]{1,0:T(8,128)(2,1)S(1)} %reshape.15), channel_id=1, source_target_pairs={{32,48},{36,52},{40,56},{44,60},{48,32},{52,36},{56,40},{60,44},{3... | collective-permute-start | bytes 153608 | tf_op jit(solution)/shard_map/ppermute | solution.py:298
  11.3 0.1 collective-permute-start.3
  11.4 4.0 %collective-permute-start.2 = (bf16[200,128]{1,0:T(8,128)(2,1)S(1)}, bf16[200,128]{1,0:T(8,128)(2,1)S(1)}, u32[]{:S(2)}, u32[]{:S(2)}) collective-permute-start(bf16[200,128]{1,0:T(8,128)(2,1)S(1)} %reshape.15), channel_id=1, source_target_pairs={{0,8},{4,12},{8,16},{12,20},{16,24},{20,28},{24,0},{28,4},{32,56},... | collective-permute-start | bytes 153608 | tf_op jit(solution)/shard_map/ppermute | solution.py:297
  15.5 0.7 collective-permute-start.1
  16.2 0.0 collective-permute-done
  16.2 0.1 collective-permute-done.3
  16.3 0.4 collective-permute-done.2
  16.7 1.7 %collective-permute-done.1 = bf16[200,128]{1,0:T(8,128)(2,1)S(1)} collective-permute-done((bf16[200,128]{1,0:T(8,128)(2,1)S(1)}, bf16[200,128]{1,0:T(8,128)(2,1)S(1)}, u32[]{:S(2)}, u32[]{:S(2)}) %collective-permute-start.1) | collective-permute-done | bytes 51232 | tf_op jit(solution)/shard_map/ppermute | solution.py:297
  18.5 3.0 %collective-permute-start.5 = (bf16[4,200,128]{2,1,0:T(8,128)(2,1)S(1)}, bf16[4,200,128]{2,1,0:T(8,128)(2,1)S(1)}, u32[]{:S(2)}, u32[]{:S(2)}) collective-permute-start(bf16[4,200,128]{2,1,0:T(8,128)(2,1)S(1)} %get-tuple-element.8), channel_id=1, source_target_pairs={{0,2},{1,3},{2,0},{3,1},{4,6},{5,7},{6,4},{7,5},{8,10},{9,11},{10,... | collective-permute-start | bytes 614408 | tf_op jit(solution)/shard_map/ppermute | solution.py:304
  21.5 0.4 collective-permute-start.4
  21.9 2.3 %collective-permute-start.6 = (bf16[4,200,128]{2,1,0:T(8,128)(2,1)S(1)}, bf16[4,200,128]{2,1,0:T(8,128)(2,1)S(1)}, u32[]{:S(2)}, u32[]{:S(2)}) collective-permute-start(bf16[4,200,128]{2,1,0:T(8,128)(2,1)S(1)} %get-tuple-element.8), channel_id=1, source_target_pairs={{0,3},{1,0},{2,1},{3,2},{4,7},{5,4},{6,5},{7,6},{8,11},{9,8},{10,9... | collective-permute-start | bytes 614408 | tf_op jit(solution)/shard_map/ppermute | solution.py:304
  24.2 2.7 %collective-permute-done.5 = bf16[4,200,128]{2,1,0:T(8,128)(2,1)S(1)} collective-permute-done((bf16[4,200,128]{2,1,0:T(8,128)(2,1)S(1)}, bf16[4,200,128]{2,1,0:T(8,128)(2,1)S(1)}, u32[]{:S(2)}, u32[]{:S(2)}) %collective-permute-start.5) | collective-permute-done | bytes 204832 | tf_op jit(solution)/shard_map/ppermute | solution.py:304
  26.9 4.2 %collective-permute-done.4 = bf16[4,200,128]{2,1,0:T(8,128)(2,1)S(1)} collective-permute-done((bf16[4,200,128]{2,1,0:T(8,128)(2,1)S(1)}, bf16[4,200,128]{2,1,0:T(8,128)(2,1)S(1)}, u32[]{:S(2)}, u32[]{:S(2)}) %collective-permute-start.4) | collective-permute-done | bytes 204832 | tf_op jit(solution)/shard_map/ppermute | solution.py:304
  31.0 0.1 collective-permute-done.6
  31.1 0.1 pad_maximum_fusion
  31.2 0.1 copy.7
  31.3 0.1 copy.10
  31.4 0.4 collective-permute-start.7
  31.9 0.7 constant_dynamic-slice_fusion.devs
  32.6 0.0 copy-done
  32.6 0.6 count.1.counts
  33.2 0.6 collective-permute-done.7.other
  33.9 6.4 %route.1 = s16[32,72,128]{2,1,0:T(8,128)(2,1)S(1)} custom-call(s32[32]{0:T(128)S(1)} %fusion.where, bf16[80,5120]{1,0:T(8,128)(2,1)S(1)} %bitcast.24, bf16[80,5120]{1,0:T(8,128)(2,1)S(1)} %collective-permute-done.7.other, bf16[5120,1024]{1,0:T(8,128)(2,1)} %tokens.1, s32[6,1024]{1,0:T(8,128)S(1)} %constant_dynamic-slice_fusion.1.picks, f32[8,128]{1,0:T(8,128)S(1)} %count.1.counts), custom_call_target="tpu_custom_call" | custom-call | tf_op jit(solution)/shard_map/route/pallas_call | solution.py:200
  40.2 24.6 %all_to_all.5.recv = s16[32,72,128]{2,1,0:T(8,128)(2,1)S(1)} all-to-all(s16[32,72,128]{2,1,0:T(8,128)(2,1)S(1)} %route.1), channel_id=1, replica_groups=mesh['dp_0'=4,'dp_1'=2,'expert_0'=8,'expert_1'=4] {'expert_0','expert_1'}, dimensions={0} | all-to-all | bytes 1179648 | tf_op jit(solution)/shard_map/all_to_all | solution.py:323
  64.8 0.1 sums.1
  64.9 2.4 %collective-permute-start.8 = (f32[8,128]{1,0:T(8,128)S(1)}, f32[8,128]{1,0:T(8,128)S(1)}, u32[]{:S(2)}, u32[]{:S(2)}) collective-permute-start(f32[8,128]{1,0:T(8,128)S(1)} %sums.1), channel_id=1, source_target_pairs={{0,32},{32,0},{1,33},{33,1},{2,34},{34,2},{3,35},{35,3},{4,36},{36... | collective-permute-start | bytes 12296 | tf_op jit(solution)/shard_map/ppermute | solution.py:343
  67.3 0.8 %collective-permute-done.8 = f32[8,128]{1,0:T(8,128)S(1)} collective-permute-done((f32[8,128]{1,0:T(8,128)S(1)}, f32[8,128]{1,0:T(8,128)S(1)}, u32[]{:S(2)}, u32[]{:S(2)}) %collective-permute-start.8) | collective-permute-done | bytes 4128 | tf_op jit(solution)/shard_map/ppermute | solution.py:343
  68.2 2.5 %collective-permute-start.9 = (f32[8,128]{1,0:T(8,128)S(1)}, f32[8,128]{1,0:T(8,128)S(1)}, u32[]{:S(2)}, u32[]{:S(2)}) collective-permute-start(f32[8,128]{1,0:T(8,128)S(1)} %add.54.own), channel_id=1, source_target_pairs={{0,64},{64,128},{128,192},{192,0},{32,224},{96,32},{160,96},{224,1... | collective-permute-start | bytes 12296 | tf_op jit(solution)/shard_map/ppermute | solution.py:347
  70.6 0.5 collective-permute-start.10
  71.2 0.2 collective-permute-done.9.near
  71.4 1.9 %collective-permute-start.11 = (f32[8,128]{1,0:T(8,128)S(1)}, f32[8,128]{1,0:T(8,128)S(1)}, u32[]{:S(2)}, u32[]{:S(2)}) collective-permute-start(f32[8,128]{1,0:T(8,128)S(1)} %collective-permute-done.9.near), channel_id=1, source_target_pairs={{0,32},{32,0},{1,33},{33,1},{2,34},{34,2},{3,35},{35,3},{4,36},{36... | collective-permute-start | bytes 12296 | tf_op jit(solution)/shard_map/ppermute | solution.py:349
  73.3 0.1 pad_add_fusion.where
  73.4 1.5 %spread.1 = (f32[6,32768]{1,0:T(8,128)}, f32[1,32768]{1,0:T(1,128)}) custom-call(s16[32,72,128]{2,1,0:T(8,128)(2,1)S(1)} %all_to_all.5.recv), custom_call_target="tpu_custom_call" | custom-call | tf_op jit(solution)/shard_map/spread/pallas_call | solution.py:333
  74.9 0.0 collective-permute-done.10.far
  74.9 0.0 collective-permute-done.11.swapped
  74.9 0.7 balance.1
  75.7 0.5 slice_bitcast_fusion
  (5 shorter events, 0.1 us)
Async XLA Ops:
  0.6 32.0 %copy-start = (s32[6,32768]{1,0:T(8,128)S(1)}, s32[6,32768]{1,0:T(8,128)}, u32[]{:S(2)}) copy-start(s32[6,32768]{1,0:T(8,128)} %param.7) | copy-start | bytes 2359300
  1.7 14.5 %collective-permute-start = (bf16[200,128]{1,0:T(8,128)(2,1)S(1)}, bf16[200,128]{1,0:T(8,128)(2,1)S(1)}, u32[]{:S(2)}, u32[]{:S(2)}) collective-permute-start(bf16[200,128]{1,0:T(8,128)(2,1)S(1)} %reshape.15), channel_id=1, source_target_pairs={{32,48},{36,52},{40,56},{44,60},{48,32},{52,36},{56,40},{60,44},{3... | collective-permute-start | bytes 153608 | tf_op jit(solution)/shard_map/ppermute | solution.py:298
  11.3 4.9 %collective-permute-start.3 = (bf16[200,128]{1,0:T(8,128)(2,1)S(1)}, bf16[200,128]{1,0:T(8,128)(2,1)S(1)}, u32[]{:S(2)}, u32[]{:S(2)}) collective-permute-start(bf16[200,128]{1,0:T(8,128)(2,1)S(1)} %reshape.15), channel_id=1, source_target_pairs={{0,12},{4,16},{8,20},{12,24},{16,28},{20,0},{24,4},{28,8},{32,52},... | collective-permute-start | bytes 153608 | tf_op jit(solution)/shard_map/ppermute | solution.py:297
  11.4 5.3 %collective-permute-start.2 = (bf16[200,128]{1,0:T(8,128)(2,1)S(1)}, bf16[200,128]{1,0:T(8,128)(2,1)S(1)}, u32[]{:S(2)}, u32[]{:S(2)}) collective-permute-start(bf16[200,128]{1,0:T(8,128)(2,1)S(1)} %reshape.15), channel_id=1, source_target_pairs={{0,8},{4,12},{8,16},{12,20},{16,24},{20,28},{24,0},{28,4},{32,56},... | collective-permute-start | bytes 153608 | tf_op jit(solution)/shard_map/ppermute | solution.py:297
  15.5 3.0 %collective-permute-start.1 = (bf16[200,128]{1,0:T(8,128)(2,1)S(1)}, bf16[200,128]{1,0:T(8,128)(2,1)S(1)}, u32[]{:S(2)}, u32[]{:S(2)}) collective-permute-start(bf16[200,128]{1,0:T(8,128)(2,1)S(1)} %reshape.15), channel_id=1, source_target_pairs={{0,4},{4,8},{8,12},{12,16},{16,20},{20,24},{24,28},{28,0},{32,60},... | collective-permute-start | bytes 153608 | tf_op jit(solution)/shard_map/ppermute | solution.py:297
  18.5 8.4 %collective-permute-start.5 = (bf16[4,200,128]{2,1,0:T(8,128)(2,1)S(1)}, bf16[4,200,128]{2,1,0:T(8,128)(2,1)S(1)}, u32[]{:S(2)}, u32[]{:S(2)}) collective-permute-start(bf16[4,200,128]{2,1,0:T(8,128)(2,1)S(1)} %get-tuple-element.8), channel_id=1, source_target_pairs={{0,2},{1,3},{2,0},{3,1},{4,6},{5,7},{6,4},{7,5},{8,10},{9,11},{10,... | collective-permute-start | bytes 614408 | tf_op jit(solution)/shard_map/ppermute | solution.py:304
  21.5 9.6 %collective-permute-start.4 = (bf16[4,200,128]{2,1,0:T(8,128)(2,1)S(1)}, bf16[4,200,128]{2,1,0:T(8,128)(2,1)S(1)}, u32[]{:S(2)}, u32[]{:S(2)}) collective-permute-start(bf16[4,200,128]{2,1,0:T(8,128)(2,1)S(1)} %get-tuple-element.8), channel_id=1, source_target_pairs={{0,1},{1,2},{2,3},{3,0},{4,5},{5,6},{6,7},{7,4},{8,9},{9,10},{10,1... | collective-permute-start | bytes 614408 | tf_op jit(solution)/shard_map/ppermute | solution.py:304
  21.9 9.2 %collective-permute-start.6 = (bf16[4,200,128]{2,1,0:T(8,128)(2,1)S(1)}, bf16[4,200,128]{2,1,0:T(8,128)(2,1)S(1)}, u32[]{:S(2)}, u32[]{:S(2)}) collective-permute-start(bf16[4,200,128]{2,1,0:T(8,128)(2,1)S(1)} %get-tuple-element.8), channel_id=1, source_target_pairs={{0,3},{1,0},{2,1},{3,2},{4,7},{5,4},{6,5},{7,6},{8,11},{9,8},{10,9... | collective-permute-start | bytes 614408 | tf_op jit(solution)/shard_map/ppermute | solution.py:304
  31.4 2.4 %collective-permute-start.7 = (bf16[80,5120]{1,0:T(8,128)(2,1)S(1)}, bf16[80,5120]{1,0:T(8,128)(2,1)S(1)}, u32[]{:S(2)}, u32[]{:S(2)}) collective-permute-start(bf16[80,5120]{1,0:T(8,128)(2,1)S(1)} %bitcast.23), channel_id=1, source_target_pairs={{0,32},{32,0},{1,33},{33,1},{2,34},{34,2},{3,35},{35,3},{4,36},{36... | collective-permute-start | bytes 2457608 | tf_op jit(solution)/shard_map/ppermute | solution.py:309
  64.9 3.2 %collective-permute-start.8 = (f32[8,128]{1,0:T(8,128)S(1)}, f32[8,128]{1,0:T(8,128)S(1)}, u32[]{:S(2)}, u32[]{:S(2)}) collective-permute-start(f32[8,128]{1,0:T(8,128)S(1)} %sums.1), channel_id=1, source_target_pairs={{0,32},{32,0},{1,33},{33,1},{2,34},{34,2},{3,35},{35,3},{4,36},{36... | collective-permute-start | bytes 12296 | tf_op jit(solution)/shard_map/ppermute | solution.py:343
  68.2 3.2 %collective-permute-start.9 = (f32[8,128]{1,0:T(8,128)S(1)}, f32[8,128]{1,0:T(8,128)S(1)}, u32[]{:S(2)}, u32[]{:S(2)}) collective-permute-start(f32[8,128]{1,0:T(8,128)S(1)} %add.54.own), channel_id=1, source_target_pairs={{0,64},{64,128},{128,192},{192,0},{32,224},{96,32},{160,96},{224,1... | collective-permute-start | bytes 12296 | tf_op jit(solution)/shard_map/ppermute | solution.py:347
  70.6 4.3 %collective-permute-start.10 = (f32[8,128]{1,0:T(8,128)S(1)}, f32[8,128]{1,0:T(8,128)S(1)}, u32[]{:S(2)}, u32[]{:S(2)}) collective-permute-start(f32[8,128]{1,0:T(8,128)S(1)} %add.54.own), channel_id=1, source_target_pairs={{0,128},{64,192},{128,0},{192,64},{1,129},{65,193},{129,1},{193,65... | collective-permute-start | bytes 12296 | tf_op jit(solution)/shard_map/ppermute | solution.py:348
  71.4 3.6 %collective-permute-start.11 = (f32[8,128]{1,0:T(8,128)S(1)}, f32[8,128]{1,0:T(8,128)S(1)}, u32[]{:S(2)}, u32[]{:S(2)}) collective-permute-start(f32[8,128]{1,0:T(8,128)S(1)} %collective-permute-done.9.near), channel_id=1, source_target_pairs={{0,32},{32,0},{1,33},{33,1},{2,34},{34,2},{3,35},{35,3},{4,36},{36... | collective-permute-start | bytes 12296 | tf_op jit(solution)/shard_map/ppermute | solution.py:349

commit v7 on v6

--- a/solution.py
+++ b/solution.py
@@ -8,23 +8,18 @@
 from jax.sharding import Mesh
 from jax.sharding import PartitionSpec as P
 
+
 TOP = 6
 DEV_TOP = 3
 EXPERT = ("expert_0", "expert_1")
 DP = ("dp_0", "dp_1")
 DP_EXPERT = ("dp_0", "dp_1", "expert_0", "expert_1")
 BLOCK = 256
-PIECES = 1
 LANES = 128
 ROWS = 8
 TOP_CODE = 65535.0
 MIDDLE = 32768
 TINY = 1e-30
-
-
-def sent_to_all(x, axis):
-    length = lax.axis_size(axis)
-    return lax.all_to_all(jnp.broadcast_to(x[None], (length, *x.shape)), axis, 0, 0, tiled=True)
 
 
 def lane_sum(x):
@@ -87,7 +82,7 @@
 def count_kernel(num_devices, per_device, picks, devs, out):
     num_experts = num_devices * per_device
     share = picks.shape[1]
-    counts, sent = [], []
+    counts = []
     for j in range(per_device):
         ids = lax.broadcasted_iota(jnp.int32, (num_devices, LANES), 0) * per_device + j
         total = jnp.zeros((num_devices, LANES), jnp.float32)
@@ -107,30 +102,60 @@
     out[...] = jnp.concatenate([low, high, sent_low, sent_high, none], axis=0)
 
 
+def block_copy(tokens, blocks, arrived, first, i):
+    _, depth, block = blocks.shape
+    source = tokens.at[pl.ds(first, depth), pl.ds(i * block, block)]
+    return pltpu.make_async_copy(source, blocks.at[i], arrived.at[i])
+
+
+def load(own, other, tokens, router, blocks, arrived, first):
+    half = own.shape[0]
+    for i in range(blocks.shape[0]):
+        block_copy(tokens, blocks, arrived, first, i).start()
+    router[:half] = own[...]
+    router[half:] = other[...]
+
+
+def partial_kernel(own, other, tokens, out, router, blocks, arrived):
+    step = pl.program_id(0)
+
+    @pl.when(step == 0)
+    def _():
+        load(own, other, tokens, router, blocks, arrived, 0)
+
+    block_copy(tokens, blocks, arrived, 0, step).wait()
+    out[...] = jnp.dot(router[...], blocks[step], preferred_element_type=jnp.float32)
+
+
 def route_kernel(
-    num_devices, per_device, where, own, other, tokens, picks, counts, out, router, ids, blocks, arrived, prob_acc
+    num_devices,
+    per_device,
+    where,
+    own,
+    other,
+    tokens,
+    partial,
+    picks,
+    counts,
+    out,
+    router,
+    ids,
+    blocks,
+    arrived,
+    prob_acc,
 ):
     step = pl.program_id(0)
     num_experts = num_devices * per_device
     group = num_devices // 2
     rows_half = num_experts // 2
-    steps, features, block = blocks.shape
+    steps, depth, block = blocks.shape
+    first = tokens.shape[0] - depth
     tiles = block // LANES
     share = block * steps
-    depth = features // PIECES
-
-    def piece(i, p):
-        rows = pl.ds(p * depth, depth)
-        cols = pl.ds(i * block, block)
-        return pltpu.make_async_copy(tokens.at[rows, cols], blocks.at[i, rows, :], arrived.at[i, p])
 
     @pl.when(step == 0)
     def _():
-        for i in range(steps):
-            for p in range(PIECES):
-                piece(i, p).start()
-        router[:rows_half] = own[...]
-        router[rows_half:] = other[...]
+        load(own, other, tokens, router, blocks, arrived, first)
         prob_acc[...] = jnp.zeros_like(prob_acc)
         row = lax.broadcasted_iota(jnp.int32, (group, LANES), 0)
         for h in range(2):
@@ -140,9 +165,8 @@
             for j in range(per_device):
                 ids[pl.ds(h * rows_half + j * group, group), :] = dev * per_device + j
 
-    for p in range(PIECES):
-        piece(step, p).wait()
-    scores = jnp.dot(router[...], blocks[step], preferred_element_type=jnp.float32)
+    block_copy(tokens, blocks, arrived, first, step).wait()
+    scores = partial[...] + jnp.dot(router[...], blocks[step], preferred_element_type=jnp.float32)
     peak = jnp.max(scores, axis=0, keepdims=True)
     raised = jnp.exp(scores - peak)
     probs = raised * (1.0 / jnp.sum(raised, axis=0, keepdims=True))
@@ -192,8 +216,35 @@
             out[d, pl.ds(share // LANES * ROWS, ROWS), :] = sums
 
 
-def route(num_devices, per_device, where, own, other, tokens, picks, counts):
-    features, share = tokens.shape
+def partial_scores(own, other, tokens):
+    half, depth = own.shape
+    share = tokens.shape[1]
+    steps = share // BLOCK
+    return pl.pallas_call(
+        partial_kernel,
+        out_shape=jax.ShapeDtypeStruct((2 * half, share), jnp.float32),
+        grid=(steps,),
+        in_specs=[
+            pl.BlockSpec((half, depth), lambda i: (0, 0)),
+            pl.BlockSpec((half, depth), lambda i: (0, 0)),
+            pl.BlockSpec(memory_space=pl.ANY),
+        ],
+        out_specs=pl.BlockSpec((2 * half, BLOCK), lambda i: (0, i)),
+        scratch_shapes=[
+            pltpu.VMEM((2 * half, depth), jnp.bfloat16),
+            pltpu.VMEM((steps, depth, BLOCK), jnp.bfloat16),
+            pltpu.SemaphoreType.DMA((steps,)),
+        ],
+        compiler_params=pltpu.CompilerParams(
+            dimension_semantics=("arbitrary",), vmem_limit_bytes=51 * 1024 * 1024
+        ),
+        name="partial",
+    )(own, other, tokens)
+
+
+def route(num_devices, per_device, where, own, other, tokens, partial, picks, counts):
+    half, depth = own.shape
+    share = tokens.shape[1]
     num_experts = num_devices * per_device
     rows = (share // LANES + 1) * ROWS
     steps = share // BLOCK
@@ -204,18 +255,19 @@
             num_scalar_prefetch=1,
             grid=(steps,),
             in_specs=[
-                pl.BlockSpec((num_experts // 2, features), lambda i, w: (0, 0)),
-                pl.BlockSpec((num_experts // 2, features), lambda i, w: (0, 0)),
+                pl.BlockSpec((half, depth), lambda i, w: (0, 0)),
+                pl.BlockSpec((half, depth), lambda i, w: (0, 0)),
                 pl.BlockSpec(memory_space=pl.ANY),
+                pl.BlockSpec((num_experts, BLOCK), lambda i, w: (0, i)),
                 pl.BlockSpec((TOP, BLOCK), lambda i, w: (0, i)),
                 pl.BlockSpec((ROWS, LANES), lambda i, w: (0, 0)),
             ],
             out_specs=pl.BlockSpec((num_devices, rows, LANES), lambda i, w: (0, 0, 0)),
             scratch_shapes=[
-                pltpu.VMEM((num_experts, features), jnp.bfloat16),
+                pltpu.VMEM((num_experts, depth), jnp.bfloat16),
                 pltpu.VMEM((num_experts, LANES), jnp.int32),
-                pltpu.VMEM((steps, features, BLOCK), jnp.bfloat16),
-                pltpu.SemaphoreType.DMA((steps, PIECES)),
+                pltpu.VMEM((steps, depth, BLOCK), jnp.bfloat16),
+                pltpu.SemaphoreType.DMA((steps,)),
                 pltpu.VMEM((num_experts, LANES), jnp.float32),
             ],
         ),
@@ -223,7 +275,7 @@
             dimension_semantics=("arbitrary",), vmem_limit_bytes=51 * 1024 * 1024
         ),
         name="route",
-    )(where, own, other, tokens, picks, counts)
+    )(where, own, other, tokens, partial, picks, counts)
 
 
 def decoded(codes):
@@ -289,7 +341,12 @@
     deep, wide = sizes = (lax.axis_size("expert_0"), lax.axis_size("expert_1"))
     group = num_devices // 2
 
-    block = router.T.reshape(per_device * features // LANES, LANES)
+    tall = features // LANES
+    early = tall * 3 // 5 // ROWS * ROWS
+    columns = router.T.reshape(per_device, tall, LANES)
+    block = jnp.concatenate(
+        [part.reshape(-1, LANES) for part in (columns[:, :early], columns[:, early:])], axis=0
+    )
     pieces = [block]
     for k in range(1, deep // 2):
         pairs = [(i, (i + k) % deep) for i in range(deep)]
@@ -300,25 +357,33 @@
     )
     pieces[0] = jnp.where(core == 0, block, across)
     column = jnp.stack(pieces)
-    plane = [column] + [
-        lax.ppermute(column, "expert_1", [(i, (i + k) % wide) for i in range(wide)]) for k in range(1, wide)
-    ]
-    tall = features // LANES
-    own = jnp.stack(plane).reshape(group, per_device, tall, LANES).transpose(1, 0, 2, 3)
-    own = own.reshape(num_experts // 2, features)
-    other = lax.ppermute(own, "dp_1", [(0, 1), (1, 0)])
+
+    def along_y(part):
+        plane = [part]
+        for k in range(1, wide):
+            plane.append(lax.ppermute(part, "expert_1", [(i, (i + k) % wide) for i in range(wide)]))
+        plane = jnp.stack(plane).reshape(group, per_device, -1, LANES).transpose(1, 0, 2, 3)
+        return plane.reshape(num_experts // 2, -1)
+
+    swap = [(0, 1), (1, 0)]
+    cut = early * per_device
+    own_first, own_last = along_y(column[:, :cut]), along_y(column[:, cut:])
+    other_first = lax.ppermute(own_first, "dp_1", swap)
+    partial = partial_scores(own_first, other_first, tokens)
+    other_last = lax.ppermute(own_last, "dp_1", swap)
 
     where = source_devices(core, (z, y), sizes)
     rows = (share // LANES + 1) * ROWS
     experts_here = lax.dynamic_slice_in_dim(expert_pick, my_index * share, share, 1)
     devices_here = lax.dynamic_slice_in_dim(device_pick, my_index * share, share, 1)
-    counts = pl.pallas_call(
+    tally = pl.pallas_call(
         functools.partial(count_kernel, num_devices, per_device),
         out_shape=jax.ShapeDtypeStruct((ROWS, LANES), jnp.float32),
         compiler_params=pltpu.CompilerParams(vmem_limit_bytes=2 * 1024 * 1024),
         name="count",
-    )(experts_here, devices_here)
-    msg = route(num_devices, per_device, where, own, other, tokens, experts_here, counts)
+    )
+    counts = tally(experts_here, devices_here)
+    msg = route(num_devices, per_device, where, own_last, other_last, tokens, partial, experts_here, counts)
 
     recv = lax.all_to_all(msg, EXPERT, 0, 0, tiled=True)
     sums = pl.pallas_call(
@@ -339,7 +404,6 @@
         compiler_params=pltpu.CompilerParams(vmem_limit_bytes=16 * 1024 * 1024),
         name="spread",
     )(recv)
-    swap = [(0, 1), (1, 0)]
     chip = sums + lax.ppermute(sums, "dp_1", swap)
     length = lax.axis_size("dp_0")
     around = [(2 * i, (2 * i + 2) % (2 * length)) for i in range(length)]

time: 76.4 us -> 78.4 us (1.026)
  waiting for transfers between devices: 10.8 us -> 7.24 us
  starting transfers between devices: 27.9 us -> 30.7 us
  Pallas kernels: 9.4 us -> 11.3 us
    pallas_call x1 -> x2, Pallas kernels: 0.64 us -> 4.02 us  [the longest x1 3.38 us: partial_scores(): pl.pallas_call(partial_kernel, out_shape=jax.ShapeDtypeStruct((2 * half,...]
    ppermute x4 -> x8, starting transfers between devices: 6.1 us -> 9.12 us  [the longest x6 8.06 us: along_y(): lax.ppermute(part, 'expert_1', [(i, (i + k) % wide) for i in range(wide)])]
    ppermute x4 -> x8, waiting for transfers between devices: 7.56 us -> 5 us  [the longest x6 4.99 us: along_y(): lax.ppermute(part, 'expert_1', [(i, (i + k) % wide) for i in range(wide)])]
    pallas_call x1, Pallas kernels: 6.39 us -> 4.95 us  [route(): pl.pallas_call(functools.partial(route_kernel, num_devices, per_device),...]
    reshape x1 -> x0, local copies, waits for them, and re-layouts: 1.06 us -> none  [local(): block = router.T.reshape(per_device * features // LANES, LANES)]
    ppermute x3, waiting for transfers between devices: 2.21 us -> 1.16 us  [local(): pieces.append(lax.ppermute(block, ('dp_1', 'expert_0'), pairs))]
    unnamed x3 -> x5, local copies, waits for them, and re-layouts: 0.14 us -> 1.16 us
  transfers between devices with their start and end apart: 12 -> 16, of which waited for: 9 -> 7; matrix products, arithmetic and copies ran while one was open for 1% -> 2% of each run, Pallas kernels for 3% -> 7%
where the time goes in v7:
time: 78.4 us; the launch traced here: 78.1 us
  starting transfers between devices  30.7 us (39%)
  blocking collectives  25.3 us (32%)
  Pallas kernels  11.3 us (14%)
  waiting for transfers between devices  7.24 us (9%)
  local copies, waits for them, and re-layouts  2.48 us (3%)
  between operations  0.82 us (1%)
    all_to_all x1, blocking collectives, local(): recv = lax.all_to_all(msg, EXPERT, 0, 0, tiled=True)  25.3 us
    ppermute x1, starting transfers between devices, local(): lax.ppermute(block, ('dp_1', 'expert_0'), [(deep + i, deep + (i + deep //...  9.64 us
    ppermute x6, starting transfers between devices, along_y(): lax.ppermute(part, 'expert_1', [(i, (i + k) % wide) for i in range(wide)])  8.06 us
    ppermute x6, waiting for transfers between devices, along_y(): lax.ppermute(part, 'expert_1', [(i, (i + k) % wide) for i in range(wide)])  4.99 us
    pallas_call x1, Pallas kernels, route(): pl.pallas_call(functools.partial(route_kernel, num_devices, per_device),...  4.95 us
    ppermute x3, starting transfers between devices, local(): pieces.append(lax.ppermute(block, ('dp_1', 'expert_0'), pairs))  4.83 us
    pallas_call x1, Pallas kernels, partial_scores(): pl.pallas_call(partial_kernel, out_shape=jax.ShapeDtypeStruct((2 * half,...  3.38 us
    ppermute x1, starting transfers between devices, local(): near = lax.ppermute(chip, ('dp_0', 'dp_1'), around)  2.49 us
  transfers between devices with their start and end apart: 16, of which 7 were waited for; matrix products, arithmetic and copies ran while one was open for 2% of the time, Pallas kernels for 7%

profile of v7, /device:TPU:1, one launch (start us, length us, event | category | flops | bytes accessed | tf_op | source)
XLA Modules:
  0.0 78.1 jit_solution(9937655513981342698)
XLA Ops:
  0.6 0.0 copy-start
  0.6 1.0 %copy.17 = bf16[1,5,40,128]{3,2,1,0:T(8,128)(2,1)S(1)} copy(bf16[1,5,40,128]{3,1,2,0:T(8,128)(2,1)} %bitcast.74) | data formatting | bytes 102400
  1.7 9.6 %collective-permute-start = (bf16[200,128]{1,0:T(8,128)(2,1)S(1)}, bf16[200,128]{1,0:T(8,128)(2,1)S(1)}, u32[]{:S(2)}, u32[]{:S(2)}) collective-permute-start(bf16[200,128]{1,0:T(8,128)(2,1)S(1)} %pad_maximum_fusion.6), channel_id=1, source_target_pairs={{32,48},{36,52},{40,56},{44,60},{48,32},{52,36},{56,40},{60,44},{3... | collective-permute-start | bytes 153608 | tf_op jit(solution)/shard_map/ppermute | solution.py:355
  11.3 0.1 collective-permute-start.1
  11.4 0.1 collective-permute-start.2
  11.5 4.7 %collective-permute-start.3 = (bf16[200,128]{1,0:T(8,128)(2,1)S(1)}, bf16[200,128]{1,0:T(8,128)(2,1)S(1)}, u32[]{:S(2)}, u32[]{:S(2)}) collective-permute-start(bf16[200,128]{1,0:T(8,128)(2,1)S(1)} %pad_maximum_fusion.6), channel_id=1, source_target_pairs={{0,12},{4,16},{8,20},{12,24},{16,28},{20,0},{24,4},{28,8},{32,52},... | collective-permute-start | bytes 153608 | tf_op jit(solution)/shard_map/ppermute | solution.py:354
  16.2 0.0 collective-permute-done
  16.2 0.0 collective-permute-done.1
  16.2 0.0 collective-permute-done.2
  16.2 1.2 %collective-permute-done.3 = bf16[200,128]{1,0:T(8,128)(2,1)S(1)} collective-permute-done((bf16[200,128]{1,0:T(8,128)(2,1)S(1)}, bf16[200,128]{1,0:T(8,128)(2,1)S(1)}, u32[]{:S(2)}, u32[]{:S(2)}) %collective-permute-start.3) | collective-permute-done | bytes 51232 | tf_op jit(solution)/shard_map/ppermute | solution.py:354
  17.4 1.4 %collective-permute-start.8 = (bf16[4,120,128]{2,1,0:T(8,128)(2,1)S(1)}, bf16[4,120,128]{2,1,0:T(8,128)(2,1)S(1)}, u32[]{:S(2)}, u32[]{:S(2)}) collective-permute-start(bf16[4,120,128]{2,1,0:T(8,128)(2,1)S(1)} %pad_maximum_fusion.2), channel_id=1, source_target_pairs={{0,1},{1,2},{2,3},{3,0},{4,5},{5,6},{6,7},{7,4},{8,9},{9,10},{10,1... | collective-permute-start | bytes 368648 | tf_op jit(solution)/shard_map/ppermute | solution.py:364
  18.7 2.6 %collective-permute-start.9 = (bf16[4,120,128]{2,1,0:T(8,128)(2,1)S(1)}, bf16[4,120,128]{2,1,0:T(8,128)(2,1)S(1)}, u32[]{:S(2)}, u32[]{:S(2)}) collective-permute-start(bf16[4,120,128]{2,1,0:T(8,128)(2,1)S(1)} %pad_maximum_fusion.2), channel_id=1, source_target_pairs={{0,2},{1,3},{2,0},{3,1},{4,6},{5,7},{6,4},{7,5},{8,10},{9,11},{10,... | collective-permute-start | bytes 368648 | tf_op jit(solution)/shard_map/ppermute | solution.py:364
  21.4 1.1 %collective-permute-start.10 = (bf16[4,120,128]{2,1,0:T(8,128)(2,1)S(1)}, bf16[4,120,128]{2,1,0:T(8,128)(2,1)S(1)}, u32[]{:S(2)}, u32[]{:S(2)}) collective-permute-start(bf16[4,120,128]{2,1,0:T(8,128)(2,1)S(1)} %pad_maximum_fusion.2), channel_id=1, source_target_pairs={{0,3},{1,0},{2,1},{3,2},{4,7},{5,4},{6,5},{7,6},{8,11},{9,8},{10,9... | collective-permute-start | bytes 368648 | tf_op jit(solution)/shard_map/ppermute | solution.py:364
  22.4 0.1 collective-permute-start.6
  22.5 1.4 %collective-permute-start.4 = (bf16[4,80,128]{2,1,0:T(8,128)(2,1)S(1)}, bf16[4,80,128]{2,1,0:T(8,128)(2,1)S(1)}, u32[]{:S(2)}, u32[]{:S(2)}) collective-permute-start(bf16[4,80,128]{2,1,0:T(8,128)(2,1)S(1)} %pad_maximum_fusion.5), channel_id=1, source_target_pairs={{0,1},{1,2},{2,3},{3,0},{4,5},{5,6},{6,7},{7,4},{8,9},{9,10},{10,1... | collective-permute-start | bytes 245768 | tf_op jit(solution)/shard_map/ppermute | solution.py:364
  23.9 0.0 collective-permute-done.8
  23.9 1.5 %collective-permute-start.5 = (bf16[4,80,128]{2,1,0:T(8,128)(2,1)S(1)}, bf16[4,80,128]{2,1,0:T(8,128)(2,1)S(1)}, u32[]{:S(2)}, u32[]{:S(2)}) collective-permute-start(bf16[4,80,128]{2,1,0:T(8,128)(2,1)S(1)} %pad_maximum_fusion.5), channel_id=1, source_target_pairs={{0,2},{1,3},{2,0},{3,1},{4,6},{5,7},{6,4},{7,5},{8,10},{9,11},{10,... | collective-permute-start | bytes 245768 | tf_op jit(solution)/shard_map/ppermute | solution.py:364
  25.5 2.2 %collective-permute-done.9 = bf16[4,120,128]{2,1,0:T(8,128)(2,1)S(1)} collective-permute-done((bf16[4,120,128]{2,1,0:T(8,128)(2,1)S(1)}, bf16[4,120,128]{2,1,0:T(8,128)(2,1)S(1)}, u32[]{:S(2)}, u32[]{:S(2)}) %collective-permute-start.9) | collective-permute-done | bytes 122912 | tf_op jit(solution)/shard_map/ppermute | solution.py:364
  27.6 0.0 collective-permute-done.10
  27.6 0.1 pad_maximum_fusion
  27.7 0.1 copy.8
  27.8 0.1 copy.15
  27.9 0.6 collective-permute-start.11
  28.4 0.7 collective-permute-done.6
  29.1 0.3 collective-permute-done.4
  29.4 1.8 %collective-permute-done.5 = bf16[4,80,128]{2,1,0:T(8,128)(2,1)S(1)} collective-permute-done((bf16[4,80,128]{2,1,0:T(8,128)(2,1)S(1)}, bf16[4,80,128]{2,1,0:T(8,128)(2,1)S(1)}, u32[]{:S(2)}, u32[]{:S(2)}) %collective-permute-start.5) | collective-permute-done | bytes 81952 | tf_op jit(solution)/shard_map/ppermute | solution.py:364
  31.3 0.1 copy.16
  31.4 0.5 collective-permute-start.7
  31.9 0.7 constant_dynamic-slice_fusion.devs
  32.7 0.6 count.1.counts
  33.3 0.0 collective-permute-done.11.other
  33.3 3.4 %partial.1 = f32[160,1024]{1,0:T(8,128)S(1)} custom-call(bf16[80,3072]{1,0:T(8,128)(2,1)S(1)} %bitcast.43, bf16[80,3072]{1,0:T(8,128)(2,1)S(1)} %collective-permute-done.11.other, bf16[5120,1024]{1,0:T(8,128)(2,1)} %tokens.3), custom_call_target="tpu_custom_call" | custom-call | tf_op jit(solution)/shard_map/partial/pallas_call | solution.py:223
  36.7 0.0 collective-permute-done.7.other
  36.7 4.9 %route.1 = s16[32,72,128]{2,1,0:T(8,128)(2,1)S(1)} custom-call(s32[32]{0:T(128)S(1)} %fusion.where, bf16[80,2048]{1,0:T(8,128)(2,1)S(1)} %bitcast.45, bf16[80,2048]{1,0:T(8,128)(2,1)S(1)} %collective-permute-done.7.other, bf16[5120,1024]{1,0:T(8,128)(2,1)} %tokens.3, f32[160,1024]{1,0:T(8,128)S(1)} %partial.1, ...), custom_call_target="tpu_custom_call" | custom-call | tf_op jit(solution)/shard_map/route/pallas_call | solution.py:251
  41.7 25.3 %all_to_all.5.recv = s16[32,72,128]{2,1,0:T(8,128)(2,1)S(1)} all-to-all(s16[32,72,128]{2,1,0:T(8,128)(2,1)S(1)} %route.1), channel_id=1, replica_groups=mesh['dp_0'=4,'dp_1'=2,'expert_0'=8,'expert_1'=4] {'expert_0','expert_1'}, dimensions={0} | all-to-all | bytes 1179648 | tf_op jit(solution)/shard_map/all_to_all | solution.py:388
  67.0 0.1 sums.1
  67.1 2.2 %collective-permute-start.12 = (f32[8,128]{1,0:T(8,128)S(1)}, f32[8,128]{1,0:T(8,128)S(1)}, u32[]{:S(2)}, u32[]{:S(2)}) collective-permute-start(f32[8,128]{1,0:T(8,128)S(1)} %sums.1), channel_id=1, source_target_pairs={{0,32},{32,0},{1,33},{33,1},{2,34},{34,2},{3,35},{35,3},{4,36},{36... | collective-permute-start | bytes 12296 | tf_op jit(solution)/shard_map/ppermute | solution.py:407
  69.3 0.8 %collective-permute-done.12 = f32[8,128]{1,0:T(8,128)S(1)} collective-permute-done((f32[8,128]{1,0:T(8,128)S(1)}, f32[8,128]{1,0:T(8,128)S(1)}, u32[]{:S(2)}, u32[]{:S(2)}) %collective-permute-start.12) | collective-permute-done | bytes 4128 | tf_op jit(solution)/shard_map/ppermute | solution.py:407
  70.1 2.5 %collective-permute-start.13 = (f32[8,128]{1,0:T(8,128)S(1)}, f32[8,128]{1,0:T(8,128)S(1)}, u32[]{:S(2)}, u32[]{:S(2)}) collective-permute-start(f32[8,128]{1,0:T(8,128)S(1)} %add.54.own), channel_id=1, source_target_pairs={{0,64},{64,128},{128,192},{192,0},{32,224},{96,32},{160,96},{224,1... | collective-permute-start | bytes 12296 | tf_op jit(solution)/shard_map/ppermute | solution.py:411
  72.6 0.5 collective-permute-start.14
  73.1 0.2 collective-permute-done.13.near
  73.4 1.9 %collective-permute-start.15 = (f32[8,128]{1,0:T(8,128)S(1)}, f32[8,128]{1,0:T(8,128)S(1)}, u32[]{:S(2)}, u32[]{:S(2)}) collective-permute-start(f32[8,128]{1,0:T(8,128)S(1)} %collective-permute-done.13.near), channel_id=1, source_target_pairs={{0,32},{32,0},{1,33},{33,1},{2,34},{34,2},{3,35},{35,3},{4,36},{36... | collective-permute-start | bytes 12296 | tf_op jit(solution)/shard_map/ppermute | solution.py:413
  75.3 0.1 pad_add_fusion.where
  75.3 1.5 %spread.1 = (f32[6,32768]{1,0:T(8,128)}, f32[1,32768]{1,0:T(1,128)}) custom-call(s16[32,72,128]{2,1,0:T(8,128)(2,1)S(1)} %all_to_all.5.recv), custom_call_target="tpu_custom_call" | custom-call | tf_op jit(solution)/shard_map/spread/pallas_call | solution.py:398
  76.9 0.0 collective-permute-done.14.far
  76.9 0.0 collective-permute-done.15.swapped
  76.9 0.7 balance.1
  77.6 0.5 slice_bitcast_fusion
  (14 shorter events, 0.2 us)
Async XLA Ops:
  0.6 32.0 %copy-start = (s32[6,32768]{1,0:T(8,128)S(1)}, s32[6,32768]{1,0:T(8,128)}, u32[]{:S(2)}) copy-start(s32[6,32768]{1,0:T(8,128)} %param.7) | copy-start | bytes 2359300
  1.7 14.5 %collective-permute-start = (bf16[200,128]{1,0:T(8,128)(2,1)S(1)}, bf16[200,128]{1,0:T(8,128)(2,1)S(1)}, u32[]{:S(2)}, u32[]{:S(2)}) collective-permute-start(bf16[200,128]{1,0:T(8,128)(2,1)S(1)} %pad_maximum_fusion.6), channel_id=1, source_target_pairs={{32,48},{36,52},{40,56},{44,60},{48,32},{52,36},{56,40},{60,44},{3... | collective-permute-start | bytes 153608 | tf_op jit(solution)/shard_map/ppermute | solution.py:355
  11.3 4.9 %collective-permute-start.1 = (bf16[200,128]{1,0:T(8,128)(2,1)S(1)}, bf16[200,128]{1,0:T(8,128)(2,1)S(1)}, u32[]{:S(2)}, u32[]{:S(2)}) collective-permute-start(bf16[200,128]{1,0:T(8,128)(2,1)S(1)} %pad_maximum_fusion.6), channel_id=1, source_target_pairs={{0,4},{4,8},{8,12},{12,16},{16,20},{20,24},{24,28},{28,0},{32,60},... | collective-permute-start | bytes 153608 | tf_op jit(solution)/shard_map/ppermute | solution.py:354
  11.4 4.8 %collective-permute-start.2 = (bf16[200,128]{1,0:T(8,128)(2,1)S(1)}, bf16[200,128]{1,0:T(8,128)(2,1)S(1)}, u32[]{:S(2)}, u32[]{:S(2)}) collective-permute-start(bf16[200,128]{1,0:T(8,128)(2,1)S(1)} %pad_maximum_fusion.6), channel_id=1, source_target_pairs={{0,8},{4,12},{8,16},{12,20},{16,24},{20,28},{24,0},{28,4},{32,56},... | collective-permute-start | bytes 153608 | tf_op jit(solution)/shard_map/ppermute | solution.py:354
  11.5 5.9 %collective-permute-start.3 = (bf16[200,128]{1,0:T(8,128)(2,1)S(1)}, bf16[200,128]{1,0:T(8,128)(2,1)S(1)}, u32[]{:S(2)}, u32[]{:S(2)}) collective-permute-start(bf16[200,128]{1,0:T(8,128)(2,1)S(1)} %pad_maximum_fusion.6), channel_id=1, source_target_pairs={{0,12},{4,16},{8,20},{12,24},{16,28},{20,0},{24,4},{28,8},{32,52},... | collective-permute-start | bytes 153608 | tf_op jit(solution)/shard_map/ppermute | solution.py:354
  17.4 6.6 %collective-permute-start.8 = (bf16[4,120,128]{2,1,0:T(8,128)(2,1)S(1)}, bf16[4,120,128]{2,1,0:T(8,128)(2,1)S(1)}, u32[]{:S(2)}, u32[]{:S(2)}) collective-permute-start(bf16[4,120,128]{2,1,0:T(8,128)(2,1)S(1)} %pad_maximum_fusion.2), channel_id=1, source_target_pairs={{0,1},{1,2},{2,3},{3,0},{4,5},{5,6},{6,7},{7,4},{8,9},{9,10},{10,1... | collective-permute-start | bytes 368648 | tf_op jit(solution)/shard_map/ppermute | solution.py:364
  18.7 8.9 %collective-permute-start.9 = (bf16[4,120,128]{2,1,0:T(8,128)(2,1)S(1)}, bf16[4,120,128]{2,1,0:T(8,128)(2,1)S(1)}, u32[]{:S(2)}, u32[]{:S(2)}) collective-permute-start(bf16[4,120,128]{2,1,0:T(8,128)(2,1)S(1)} %pad_maximum_fusion.2), channel_id=1, source_target_pairs={{0,2},{1,3},{2,0},{3,1},{4,6},{5,7},{6,4},{7,5},{8,10},{9,11},{10,... | collective-permute-start | bytes 368648 | tf_op jit(solution)/shard_map/ppermute | solution.py:364
  21.4 6.3 %collective-permute-start.10 = (bf16[4,120,128]{2,1,0:T(8,128)(2,1)S(1)}, bf16[4,120,128]{2,1,0:T(8,128)(2,1)S(1)}, u32[]{:S(2)}, u32[]{:S(2)}) collective-permute-start(bf16[4,120,128]{2,1,0:T(8,128)(2,1)S(1)} %pad_maximum_fusion.2), channel_id=1, source_target_pairs={{0,3},{1,0},{2,1},{3,2},{4,7},{5,4},{6,5},{7,6},{8,11},{9,8},{10,9... | collective-permute-start | bytes 368648 | tf_op jit(solution)/shard_map/ppermute | solution.py:364
  22.4 6.7 %collective-permute-start.6 = (bf16[4,80,128]{2,1,0:T(8,128)(2,1)S(1)}, bf16[4,80,128]{2,1,0:T(8,128)(2,1)S(1)}, u32[]{:S(2)}, u32[]{:S(2)}) collective-permute-start(bf16[4,80,128]{2,1,0:T(8,128)(2,1)S(1)} %pad_maximum_fusion.5), channel_id=1, source_target_pairs={{0,3},{1,0},{2,1},{3,2},{4,7},{5,4},{6,5},{7,6},{8,11},{9,8},{10,9... | collective-permute-start | bytes 245768 | tf_op jit(solution)/shard_map/ppermute | solution.py:364
  22.5 6.9 %collective-permute-start.4 = (bf16[4,80,128]{2,1,0:T(8,128)(2,1)S(1)}, bf16[4,80,128]{2,1,0:T(8,128)(2,1)S(1)}, u32[]{:S(2)}, u32[]{:S(2)}) collective-permute-start(bf16[4,80,128]{2,1,0:T(8,128)(2,1)S(1)} %pad_maximum_fusion.5), channel_id=1, source_target_pairs={{0,1},{1,2},{2,3},{3,0},{4,5},{5,6},{6,7},{7,4},{8,9},{9,10},{10,1... | collective-permute-start | bytes 245768 | tf_op jit(solution)/shard_map/ppermute | solution.py:364
  23.9 7.3 %collective-permute-start.5 = (bf16[4,80,128]{2,1,0:T(8,128)(2,1)S(1)}, bf16[4,80,128]{2,1,0:T(8,128)(2,1)S(1)}, u32[]{:S(2)}, u32[]{:S(2)}) collective-permute-start(bf16[4,80,128]{2,1,0:T(8,128)(2,1)S(1)} %pad_maximum_fusion.5), channel_id=1, source_target_pairs={{0,2},{1,3},{2,0},{3,1},{4,6},{5,7},{6,4},{7,5},{8,10},{9,11},{10,... | collective-permute-start | bytes 245768 | tf_op jit(solution)/shard_map/ppermute | solution.py:364
  27.9 5.5 %collective-permute-start.11 = (bf16[80,3072]{1,0:T(8,128)(2,1)S(1)}, bf16[80,3072]{1,0:T(8,128)(2,1)S(1)}, u32[]{:S(2)}, u32[]{:S(2)}) collective-permute-start(bf16[80,3072]{1,0:T(8,128)(2,1)S(1)} %bitcast.42), channel_id=1, source_target_pairs={{0,32},{32,0},{1,33},{33,1},{2,34},{34,2},{3,35},{35,3},{4,36},{36... | collective-permute-start | bytes 1474568 | tf_op jit(solution)/shard_map/ppermute | solution.py:371
  31.4 5.3 %collective-permute-start.7 = (bf16[80,2048]{1,0:T(8,128)(2,1)S(1)}, bf16[80,2048]{1,0:T(8,128)(2,1)S(1)}, u32[]{:S(2)}, u32[]{:S(2)}) collective-permute-start(bf16[80,2048]{1,0:T(8,128)(2,1)S(1)} %bitcast.44), channel_id=1, source_target_pairs={{0,32},{32,0},{1,33},{33,1},{2,34},{34,2},{3,35},{35,3},{4,36},{36... | collective-permute-start | bytes 983048 | tf_op jit(solution)/shard_map/ppermute | solution.py:373
  67.1 3.0 %collective-permute-start.12 = (f32[8,128]{1,0:T(8,128)S(1)}, f32[8,128]{1,0:T(8,128)S(1)}, u32[]{:S(2)}, u32[]{:S(2)}) collective-permute-start(f32[8,128]{1,0:T(8,128)S(1)} %sums.1), channel_id=1, source_target_pairs={{0,32},{32,0},{1,33},{33,1},{2,34},{34,2},{3,35},{35,3},{4,36},{36... | collective-permute-start | bytes 12296 | tf_op jit(solution)/shard_map/ppermute | solution.py:407
  70.1 3.2 %collective-permute-start.13 = (f32[8,128]{1,0:T(8,128)S(1)}, f32[8,128]{1,0:T(8,128)S(1)}, u32[]{:S(2)}, u32[]{:S(2)}) collective-permute-start(f32[8,128]{1,0:T(8,128)S(1)} %add.54.own), channel_id=1, source_target_pairs={{0,64},{64,128},{128,192},{192,0},{32,224},{96,32},{160,96},{224,1... | collective-permute-start | bytes 12296 | tf_op jit(solution)/shard_map/ppermute | solution.py:411
  72.6 4.3 %collective-permute-start.14 = (f32[8,128]{1,0:T(8,128)S(1)}, f32[8,128]{1,0:T(8,128)S(1)}, u32[]{:S(2)}, u32[]{:S(2)}) collective-permute-start(f32[8,128]{1,0:T(8,128)S(1)} %add.54.own), channel_id=1, source_target_pairs={{0,128},{64,192},{128,0},{192,64},{1,129},{65,193},{129,1},{193,65... | collective-permute-start | bytes 12296 | tf_op jit(solution)/shard_map/ppermute | solution.py:412
  73.4 3.5 %collective-permute-start.15 = (f32[8,128]{1,0:T(8,128)S(1)}, f32[8,128]{1,0:T(8,128)S(1)}, u32[]{:S(2)}, u32[]{:S(2)}) collective-permute-start(f32[8,128]{1,0:T(8,128)S(1)} %collective-permute-done.13.near), channel_id=1, source_target_pairs={{0,32},{32,0},{1,33},{33,1},{2,34},{34,2},{3,35},{35,3},{4,36},{36... | collective-permute-start | bytes 12296 | tf_op jit(solution)/shard_map/ppermute | solution.py:413

commit v8 on v6

--- a/solution.py
+++ b/solution.py
@@ -65,15 +65,11 @@
     return base * (1.0 + unit(fine) * 16.0 / jnp.maximum(coarse, 1.0))
 
 
-def source_devices(core, place, sizes):
+def source_device(index, row, sizes):
     deep, wide = sizes
-    z, y = place
-    row = jnp.arange(deep * wide, dtype=jnp.int32)
-    back = row % (deep // 2)
-    aside = (row // (deep // 2)) % wide
-    half = row // (deep * wide // 2)
-    ahead = jnp.where(back == 0, deep // 2, back)
-    offset = jnp.where(core == half, deep - back, ahead)
+    core, z, y = index // (deep * wide), (index // wide) % deep, index % wide
+    half, aside, back = row // (deep * wide // 2), (row // (deep // 2)) % wide, row % (deep // 2)
+    offset = jnp.where(core == half, deep - back, back or deep // 2)
     return ((z + offset) % deep) * wide + (y + wide - aside) % wide
 
 
@@ -108,9 +104,24 @@
 
 
 def route_kernel(
-    num_devices, per_device, where, own, other, tokens, picks, counts, out, router, ids, blocks, arrived, prob_acc
+    sizes,
+    per_device,
+    where,
+    own,
+    other,
+    tokens,
+    picks,
+    counts,
+    out,
+    router,
+    ids,
+    targets,
+    blocks,
+    arrived,
+    prob_acc,
 ):
     step = pl.program_id(0)
+    num_devices = sizes[0] * sizes[1]
     num_experts = num_devices * per_device
     group = num_devices // 2
     rows_half = num_experts // 2
@@ -136,7 +147,9 @@
         for h in range(2):
             dev = jnp.zeros((group, LANES), jnp.int32)
             for s in range(group):
-                dev = jnp.where(row == s, where[h * group + s], dev)
+                target = source_device(where[0], h * group + s, sizes)
+                targets[h * group + s] = target
+                dev = jnp.where(row == s, target, dev)
             for j in range(per_device):
                 ids[pl.ds(h * rows_half + j * group, group), :] = dev * per_device + j
 
@@ -174,7 +187,7 @@
                 ],
                 axis=0,
             )
-            out[where[h * group + s], here, :] = jnp.where(last, line, stacked).astype(jnp.int16)
+            out[targets[h * group + s], here, :] = jnp.where(last, line, stacked).astype(jnp.int16)
 
     @pl.when(step == steps - 1)
     def _():
@@ -192,13 +205,14 @@
             out[d, pl.ds(share // LANES * ROWS, ROWS), :] = sums
 
 
-def route(num_devices, per_device, where, own, other, tokens, picks, counts):
+def route(sizes, per_device, where, own, other, tokens, picks, counts):
     features, share = tokens.shape
+    num_devices = sizes[0] * sizes[1]
     num_experts = num_devices * per_device
     rows = (share // LANES + 1) * ROWS
     steps = share // BLOCK
     return pl.pallas_call(
-        functools.partial(route_kernel, num_devices, per_device),
+        functools.partial(route_kernel, sizes, per_device),
         out_shape=jax.ShapeDtypeStruct((num_devices, rows, LANES), jnp.int16),
         grid_spec=pltpu.PrefetchScalarGridSpec(
             num_scalar_prefetch=1,
@@ -214,6 +228,7 @@
             scratch_shapes=[
                 pltpu.VMEM((num_experts, features), jnp.bfloat16),
                 pltpu.VMEM((num_experts, LANES), jnp.int32),
+                pltpu.SMEM((num_devices,), jnp.int32),
                 pltpu.VMEM((steps, features, BLOCK), jnp.bfloat16),
                 pltpu.SemaphoreType.DMA((steps, PIECES)),
                 pltpu.VMEM((num_experts, LANES), jnp.float32),
@@ -253,7 +268,7 @@
 
 
 def balance_kernel(num_devices, per_device, total_tokens, where, own, near, far, swapped, out, slots):
-    place, core = where[0], where[1]
+    place, core = where[0] // 2, where[0] % 2
     slots[place] = own[...]
     slots[(place + jnp.where(core == 0, 3, 1)) % 4] = near[...]
     slots[(place + 2) % 4] = far[...]
@@ -273,9 +288,8 @@
 
     dev_prob = by_device(prob)
     dev_freq = by_device(freq) / per_device
-    losses = [jnp.sum(a * b, axis=1, keepdims=True) for a, b in ((freq, prob), (dev_freq, dev_prob), (sent, dev_prob))]
-    lane = lax.broadcasted_iota(jnp.int32, (1, LANES), 1)
-    out[...] = jnp.where(lane == 0, losses[0], jnp.where(lane == 1, losses[1], losses[2]))
+    for i, (a, b) in enumerate(((freq, prob), (dev_freq, dev_prob), (sent, dev_prob))):
+        out[i] = jnp.sum(a * b)
 
 
 def local(tokens, router, device_pick, expert_pick):
@@ -285,7 +299,7 @@
     num_experts = per_device * num_devices
     total_tokens = share * num_devices * lax.axis_size(DP)
     my_index = lax.axis_index(EXPERT)
-    core, z, y = (lax.axis_index(axis) for axis in ("dp_1", "expert_0", "expert_1"))
+    core = lax.axis_index("dp_1")
     deep, wide = sizes = (lax.axis_size("expert_0"), lax.axis_size("expert_1"))
     group = num_devices // 2
 
@@ -308,7 +322,7 @@
     own = own.reshape(num_experts // 2, features)
     other = lax.ppermute(own, "dp_1", [(0, 1), (1, 0)])
 
-    where = source_devices(core, (z, y), sizes)
+    where = lax.axis_index(("dp_1", *EXPERT)).astype(jnp.int32).reshape(1)
     rows = (share // LANES + 1) * ROWS
     experts_here = lax.dynamic_slice_in_dim(expert_pick, my_index * share, share, 1)
     devices_here = lax.dynamic_slice_in_dim(device_pick, my_index * share, share, 1)
@@ -318,7 +332,7 @@
         compiler_params=pltpu.CompilerParams(vmem_limit_bytes=2 * 1024 * 1024),
         name="count",
     )(experts_here, devices_here)
-    msg = route(num_devices, per_device, where, own, other, tokens, experts_here, counts)
+    msg = route(sizes, per_device, where, own, other, tokens, experts_here, counts)
 
     recv = lax.all_to_all(msg, EXPERT, 0, 0, tiled=True)
     sums = pl.pallas_call(
@@ -349,18 +363,18 @@
     swapped = lax.ppermute(near, "dp_1", swap)
     balance = pl.pallas_call(
         functools.partial(balance_kernel, num_devices, per_device, total_tokens),
-        out_shape=jax.ShapeDtypeStruct((1, LANES), jnp.float32),
+        out_shape=jax.ShapeDtypeStruct((3,), jnp.float32),
         grid_spec=pltpu.PrefetchScalarGridSpec(
             num_scalar_prefetch=1,
             grid=(1,),
             in_specs=[pl.BlockSpec((ROWS, LANES), lambda i, w: (0, 0))] * 4,
-            out_specs=pl.BlockSpec((1, LANES), lambda i, w: (0, 0)),
+            out_specs=pl.BlockSpec(memory_space=pltpu.SMEM),
             scratch_shapes=[pltpu.VMEM((4, ROWS, LANES), jnp.float32)],
         ),
         compiler_params=pltpu.CompilerParams(vmem_limit_bytes=1024 * 1024),
         name="balance",
-    )(jnp.stack([lax.axis_index("dp_0"), core]).astype(jnp.int32), chip, near, far, swapped)
-    return (gates, device_max, balance[0, 0:3])
+    )(lax.axis_index(DP).astype(jnp.int32).reshape(1), chip, near, far, swapped)
+    return (gates, device_max, balance)
 
 
 def solution(mesh):

time: 76.4 us -> 75.3 us (0.986)
  no operation moved by 1% of the time
where the time goes in v8:
time: 75.3 us; the launch traced here: 75 us
  starting transfers between devices  27.9 us (37%)
  blocking collectives  24.5 us (33%)
  waiting for transfers between devices  10.9 us (14%)
  Pallas kernels  8.85 us (12%)
  local copies, waits for them, and re-layouts  2 us (3%)
    all_to_all x1, blocking collectives, local(): recv = lax.all_to_all(msg, EXPERT, 0, 0, tiled=True)  24.5 us
    ppermute x1, starting transfers between devices, local(): lax.ppermute(block, ('dp_1', 'expert_0'), [(deep + i, deep + (i + deep //...  9.64 us
    ppermute x3, waiting for transfers between devices, local(): lax.ppermute(column, 'expert_1', [(i, (i + k) % wide) for i in range(wide)])  6.95 us
    pallas_call x1, Pallas kernels, route(): pl.pallas_call(functools.partial(route_kernel, sizes, per_device), out_sh...  5.83 us
    ppermute x3, starting transfers between devices, local(): lax.ppermute(column, 'expert_1', [(i, (i + k) % wide) for i in range(wide)])  5.68 us
    ppermute x3, starting transfers between devices, local(): pieces.append(lax.ppermute(block, ('dp_1', 'expert_0'), pairs))  4.84 us
    ppermute x1, starting transfers between devices, local(): near = lax.ppermute(chip, ('dp_0', 'dp_1'), around)  2.48 us
    ppermute x1, starting transfers between devices, local(): chip = sums + lax.ppermute(sums, 'dp_1', swap)  2.42 us
  transfers between devices with their start and end apart: 12, of which 9 were waited for; matrix products, arithmetic and copies ran while one was open for 1% of the time, Pallas kernels for 3%

profile of v8, /device:TPU:1, one launch (start us, length us, event | category | flops | bytes accessed | tf_op | source)
XLA Modules:
  0.0 75.0 jit_solution(710872523172923190)
XLA Ops:
  0.6 0.0 copy-start
  0.6 1.1 %reshape.22 = bf16[200,128]{1,0:T(8,128)(2,1)S(1)} reshape(bf16[5,5120]{1,0:T(8,128)(2,1)} %bitcast.28) | data formatting | bytes 102400 | tf_op jit(solution)/shard_map/reshape | solution.py:306
  1.7 9.6 %collective-permute-start = (bf16[200,128]{1,0:T(8,128)(2,1)S(1)}, bf16[200,128]{1,0:T(8,128)(2,1)S(1)}, u32[]{:S(2)}, u32[]{:S(2)}) collective-permute-start(bf16[200,128]{1,0:T(8,128)(2,1)S(1)} %reshape.22), channel_id=1, source_target_pairs={{32,48},{36,52},{40,56},{44,60},{48,32},{52,36},{56,40},{60,44},{3... | collective-permute-start | bytes 153608 | tf_op jit(solution)/shard_map/ppermute | solution.py:312
  11.3 0.1 collective-permute-start.3
  11.4 4.0 %collective-permute-start.2 = (bf16[200,128]{1,0:T(8,128)(2,1)S(1)}, bf16[200,128]{1,0:T(8,128)(2,1)S(1)}, u32[]{:S(2)}, u32[]{:S(2)}) collective-permute-start(bf16[200,128]{1,0:T(8,128)(2,1)S(1)} %reshape.22), channel_id=1, source_target_pairs={{0,8},{4,12},{8,16},{12,20},{16,24},{20,28},{24,0},{28,4},{32,56},... | collective-permute-start | bytes 153608 | tf_op jit(solution)/shard_map/ppermute | solution.py:311
  15.5 0.7 collective-permute-start.1
  16.2 0.0 collective-permute-done
  16.2 0.1 collective-permute-done.3
  16.3 0.4 collective-permute-done.2
  16.7 1.7 %collective-permute-done.1 = bf16[200,128]{1,0:T(8,128)(2,1)S(1)} collective-permute-done((bf16[200,128]{1,0:T(8,128)(2,1)S(1)}, bf16[200,128]{1,0:T(8,128)(2,1)S(1)}, u32[]{:S(2)}, u32[]{:S(2)}) %collective-permute-start.1) | collective-permute-done | bytes 51232 | tf_op jit(solution)/shard_map/ppermute | solution.py:311
  18.5 3.0 %collective-permute-start.5 = (bf16[4,200,128]{2,1,0:T(8,128)(2,1)S(1)}, bf16[4,200,128]{2,1,0:T(8,128)(2,1)S(1)}, u32[]{:S(2)}, u32[]{:S(2)}) collective-permute-start(bf16[4,200,128]{2,1,0:T(8,128)(2,1)S(1)} %get-tuple-element.8), channel_id=1, source_target_pairs={{0,2},{1,3},{2,0},{3,1},{4,6},{5,7},{6,4},{7,5},{8,10},{9,11},{10,... | collective-permute-start | bytes 614408 | tf_op jit(solution)/shard_map/ppermute | solution.py:318
  21.5 0.4 collective-permute-start.4
  21.9 2.3 %collective-permute-start.6 = (bf16[4,200,128]{2,1,0:T(8,128)(2,1)S(1)}, bf16[4,200,128]{2,1,0:T(8,128)(2,1)S(1)}, u32[]{:S(2)}, u32[]{:S(2)}) collective-permute-start(bf16[4,200,128]{2,1,0:T(8,128)(2,1)S(1)} %get-tuple-element.8), channel_id=1, source_target_pairs={{0,3},{1,0},{2,1},{3,2},{4,7},{5,4},{6,5},{7,6},{8,11},{9,8},{10,9... | collective-permute-start | bytes 614408 | tf_op jit(solution)/shard_map/ppermute | solution.py:318
  24.2 2.7 %collective-permute-done.5 = bf16[4,200,128]{2,1,0:T(8,128)(2,1)S(1)} collective-permute-done((bf16[4,200,128]{2,1,0:T(8,128)(2,1)S(1)}, bf16[4,200,128]{2,1,0:T(8,128)(2,1)S(1)}, u32[]{:S(2)}, u32[]{:S(2)}) %collective-permute-start.5) | collective-permute-done | bytes 204832 | tf_op jit(solution)/shard_map/ppermute | solution.py:318
  26.9 4.2 %collective-permute-done.4 = bf16[4,200,128]{2,1,0:T(8,128)(2,1)S(1)} collective-permute-done((bf16[4,200,128]{2,1,0:T(8,128)(2,1)S(1)}, bf16[4,200,128]{2,1,0:T(8,128)(2,1)S(1)}, u32[]{:S(2)}, u32[]{:S(2)}) %collective-permute-start.4) | collective-permute-done | bytes 204832 | tf_op jit(solution)/shard_map/ppermute | solution.py:318
  31.0 0.1 collective-permute-done.6
  31.1 0.1 pad_maximum_fusion
  31.2 0.1 copy.7
  31.3 0.1 copy.10
  31.4 0.4 collective-permute-start.7
  31.9 0.7 constant_dynamic-slice_fusion.devs
  32.6 0.0 copy-done
  32.6 0.6 count.1.counts
  33.2 0.6 collective-permute-done.7.other
  33.9 5.8 %route.1 = s16[32,72,128]{2,1,0:T(8,128)(2,1)S(1)} custom-call(s32[1]{0:T(128)} %bitcast.where, bf16[80,5120]{1,0:T(8,128)(2,1)S(1)} %bitcast.22, bf16[80,5120]{1,0:T(8,128)(2,1)S(1)} %collective-permute-done.7.other, bf16[5120,1024]{1,0:T(8,128)(2,1)} %tokens.1, s32[6,1024]{1,0:T(8,128)S(1)} %constant_dynamic-slice_fusion.1.picks, f32[8,128]{1,0:T(8,128)S(1)} %count.1.counts), custom_call_target="tpu_custom_call" | custom-call | tf_op jit(solution)/shard_map/route/pallas_call | solution.py:214
  39.7 24.5 %all_to_all.5.recv = s16[32,72,128]{2,1,0:T(8,128)(2,1)S(1)} all-to-all(s16[32,72,128]{2,1,0:T(8,128)(2,1)S(1)} %route.1), channel_id=1, replica_groups=mesh['dp_0'=4,'dp_1'=2,'expert_0'=8,'expert_1'=4] {'expert_0','expert_1'}, dimensions={0} | all-to-all | bytes 1179648 | tf_op jit(solution)/shard_map/all_to_all | solution.py:337
  64.2 0.1 sums.1
  64.3 2.4 %collective-permute-start.8 = (f32[8,128]{1,0:T(8,128)S(1)}, f32[8,128]{1,0:T(8,128)S(1)}, u32[]{:S(2)}, u32[]{:S(2)}) collective-permute-start(f32[8,128]{1,0:T(8,128)S(1)} %sums.1), channel_id=1, source_target_pairs={{0,32},{32,0},{1,33},{33,1},{2,34},{34,2},{3,35},{35,3},{4,36},{36... | collective-permute-start | bytes 12296 | tf_op jit(solution)/shard_map/ppermute | solution.py:357
  66.8 0.8 %collective-permute-done.8 = f32[8,128]{1,0:T(8,128)S(1)} collective-permute-done((f32[8,128]{1,0:T(8,128)S(1)}, f32[8,128]{1,0:T(8,128)S(1)}, u32[]{:S(2)}, u32[]{:S(2)}) %collective-permute-start.8) | collective-permute-done | bytes 4128 | tf_op jit(solution)/shard_map/ppermute | solution.py:357
  67.6 2.5 %collective-permute-start.9 = (f32[8,128]{1,0:T(8,128)S(1)}, f32[8,128]{1,0:T(8,128)S(1)}, u32[]{:S(2)}, u32[]{:S(2)}) collective-permute-start(f32[8,128]{1,0:T(8,128)S(1)} %add.21.own), channel_id=1, source_target_pairs={{0,64},{64,128},{128,192},{192,0},{32,224},{96,32},{160,96},{224,1... | collective-permute-start | bytes 12296 | tf_op jit(solution)/shard_map/ppermute | solution.py:361
  70.1 0.5 collective-permute-start.10
  70.6 0.2 collective-permute-done.9.near
  70.8 1.9 %collective-permute-start.11 = (f32[8,128]{1,0:T(8,128)S(1)}, f32[8,128]{1,0:T(8,128)S(1)}, u32[]{:S(2)}, u32[]{:S(2)}) collective-permute-start(f32[8,128]{1,0:T(8,128)S(1)} %collective-permute-done.9.near), channel_id=1, source_target_pairs={{0,32},{32,0},{1,33},{33,1},{2,34},{34,2},{3,35},{35,3},{4,36},{36... | collective-permute-start | bytes 12296 | tf_op jit(solution)/shard_map/ppermute | solution.py:363
  72.8 1.5 %spread.1 = (f32[6,32768]{1,0:T(8,128)}, f32[1,32768]{1,0:T(1,128)}) custom-call(s16[32,72,128]{2,1,0:T(8,128)(2,1)S(1)} %all_to_all.5.recv), custom_call_target="tpu_custom_call" | custom-call | tf_op jit(solution)/shard_map/spread/pallas_call | solution.py:347
  74.3 0.0 collective-permute-done.10.far
  74.3 0.0 collective-permute-done.11.swapped
  74.3 0.7 balance.1
  (4 shorter events, 0.1 us)
Async XLA Ops:
  0.6 32.0 %copy-start = (s32[6,32768]{1,0:T(8,128)S(1)}, s32[6,32768]{1,0:T(8,128)}, u32[]{:S(2)}) copy-start(s32[6,32768]{1,0:T(8,128)} %param.7) | copy-start | bytes 2359300
  1.7 14.5 %collective-permute-start = (bf16[200,128]{1,0:T(8,128)(2,1)S(1)}, bf16[200,128]{1,0:T(8,128)(2,1)S(1)}, u32[]{:S(2)}, u32[]{:S(2)}) collective-permute-start(bf16[200,128]{1,0:T(8,128)(2,1)S(1)} %reshape.22), channel_id=1, source_target_pairs={{32,48},{36,52},{40,56},{44,60},{48,32},{52,36},{56,40},{60,44},{3... | collective-permute-start | bytes 153608 | tf_op jit(solution)/shard_map/ppermute | solution.py:312
  11.3 4.9 %collective-permute-start.3 = (bf16[200,128]{1,0:T(8,128)(2,1)S(1)}, bf16[200,128]{1,0:T(8,128)(2,1)S(1)}, u32[]{:S(2)}, u32[]{:S(2)}) collective-permute-start(bf16[200,128]{1,0:T(8,128)(2,1)S(1)} %reshape.22), channel_id=1, source_target_pairs={{0,12},{4,16},{8,20},{12,24},{16,28},{20,0},{24,4},{28,8},{32,52},... | collective-permute-start | bytes 153608 | tf_op jit(solution)/shard_map/ppermute | solution.py:311
  11.4 5.3 %collective-permute-start.2 = (bf16[200,128]{1,0:T(8,128)(2,1)S(1)}, bf16[200,128]{1,0:T(8,128)(2,1)S(1)}, u32[]{:S(2)}, u32[]{:S(2)}) collective-permute-start(bf16[200,128]{1,0:T(8,128)(2,1)S(1)} %reshape.22), channel_id=1, source_target_pairs={{0,8},{4,12},{8,16},{12,20},{16,24},{20,28},{24,0},{28,4},{32,56},... | collective-permute-start | bytes 153608 | tf_op jit(solution)/shard_map/ppermute | solution.py:311
  15.5 3.0 %collective-permute-start.1 = (bf16[200,128]{1,0:T(8,128)(2,1)S(1)}, bf16[200,128]{1,0:T(8,128)(2,1)S(1)}, u32[]{:S(2)}, u32[]{:S(2)}) collective-permute-start(bf16[200,128]{1,0:T(8,128)(2,1)S(1)} %reshape.22), channel_id=1, source_target_pairs={{0,4},{4,8},{8,12},{12,16},{16,20},{20,24},{24,28},{28,0},{32,60},... | collective-permute-start | bytes 153608 | tf_op jit(solution)/shard_map/ppermute | solution.py:311
  18.5 8.4 %collective-permute-start.5 = (bf16[4,200,128]{2,1,0:T(8,128)(2,1)S(1)}, bf16[4,200,128]{2,1,0:T(8,128)(2,1)S(1)}, u32[]{:S(2)}, u32[]{:S(2)}) collective-permute-start(bf16[4,200,128]{2,1,0:T(8,128)(2,1)S(1)} %get-tuple-element.8), channel_id=1, source_target_pairs={{0,2},{1,3},{2,0},{3,1},{4,6},{5,7},{6,4},{7,5},{8,10},{9,11},{10,... | collective-permute-start | bytes 614408 | tf_op jit(solution)/shard_map/ppermute | solution.py:318
  21.5 9.6 %collective-permute-start.4 = (bf16[4,200,128]{2,1,0:T(8,128)(2,1)S(1)}, bf16[4,200,128]{2,1,0:T(8,128)(2,1)S(1)}, u32[]{:S(2)}, u32[]{:S(2)}) collective-permute-start(bf16[4,200,128]{2,1,0:T(8,128)(2,1)S(1)} %get-tuple-element.8), channel_id=1, source_target_pairs={{0,1},{1,2},{2,3},{3,0},{4,5},{5,6},{6,7},{7,4},{8,9},{9,10},{10,1... | collective-permute-start | bytes 614408 | tf_op jit(solution)/shard_map/ppermute | solution.py:318
  21.9 9.2 %collective-permute-start.6 = (bf16[4,200,128]{2,1,0:T(8,128)(2,1)S(1)}, bf16[4,200,128]{2,1,0:T(8,128)(2,1)S(1)}, u32[]{:S(2)}, u32[]{:S(2)}) collective-permute-start(bf16[4,200,128]{2,1,0:T(8,128)(2,1)S(1)} %get-tuple-element.8), channel_id=1, source_target_pairs={{0,3},{1,0},{2,1},{3,2},{4,7},{5,4},{6,5},{7,6},{8,11},{9,8},{10,9... | collective-permute-start | bytes 614408 | tf_op jit(solution)/shard_map/ppermute | solution.py:318
  31.4 2.4 %collective-permute-start.7 = (bf16[80,5120]{1,0:T(8,128)(2,1)S(1)}, bf16[80,5120]{1,0:T(8,128)(2,1)S(1)}, u32[]{:S(2)}, u32[]{:S(2)}) collective-permute-start(bf16[80,5120]{1,0:T(8,128)(2,1)S(1)} %bitcast.21), channel_id=1, source_target_pairs={{0,32},{32,0},{1,33},{33,1},{2,34},{34,2},{3,35},{35,3},{4,36},{36... | collective-permute-start | bytes 2457608 | tf_op jit(solution)/shard_map/ppermute | solution.py:323
  64.3 3.2 %collective-permute-start.8 = (f32[8,128]{1,0:T(8,128)S(1)}, f32[8,128]{1,0:T(8,128)S(1)}, u32[]{:S(2)}, u32[]{:S(2)}) collective-permute-start(f32[8,128]{1,0:T(8,128)S(1)} %sums.1), channel_id=1, source_target_pairs={{0,32},{32,0},{1,33},{33,1},{2,34},{34,2},{3,35},{35,3},{4,36},{36... | collective-permute-start | bytes 12296 | tf_op jit(solution)/shard_map/ppermute | solution.py:357
  67.6 3.2 %collective-permute-start.9 = (f32[8,128]{1,0:T(8,128)S(1)}, f32[8,128]{1,0:T(8,128)S(1)}, u32[]{:S(2)}, u32[]{:S(2)}) collective-permute-start(f32[8,128]{1,0:T(8,128)S(1)} %add.21.own), channel_id=1, source_target_pairs={{0,64},{64,128},{128,192},{192,0},{32,224},{96,32},{160,96},{224,1... | collective-permute-start | bytes 12296 | tf_op jit(solution)/shard_map/ppermute | solution.py:361
  70.1 4.2 %collective-permute-start.10 = (f32[8,128]{1,0:T(8,128)S(1)}, f32[8,128]{1,0:T(8,128)S(1)}, u32[]{:S(2)}, u32[]{:S(2)}) collective-permute-start(f32[8,128]{1,0:T(8,128)S(1)} %add.21.own), channel_id=1, source_target_pairs={{0,128},{64,192},{128,0},{192,64},{1,129},{65,193},{129,1},{193,65... | collective-permute-start | bytes 12296 | tf_op jit(solution)/shard_map/ppermute | solution.py:362
  70.8 3.5 %collective-permute-start.11 = (f32[8,128]{1,0:T(8,128)S(1)}, f32[8,128]{1,0:T(8,128)S(1)}, u32[]{:S(2)}, u32[]{:S(2)}) collective-permute-start(f32[8,128]{1,0:T(8,128)S(1)} %collective-permute-done.9.near), channel_id=1, source_target_pairs={{0,32},{32,0},{1,33},{33,1},{2,34},{34,2},{3,35},{35,3},{4,36},{36... | collective-permute-start | bytes 12296 | tf_op jit(solution)/shard_map/ppermute | solution.py:363

commit v9 on v8

--- a/solution.py
+++ b/solution.py
@@ -67,9 +67,15 @@
 
 def source_device(index, row, sizes):
     deep, wide = sizes
-    core, z, y = index // (deep * wide), (index // wide) % deep, index % wide
-    half, aside, back = row // (deep * wide // 2), (row // (deep // 2)) % wide, row % (deep // 2)
-    offset = jnp.where(core == half, deep - back, back or deep // 2)
+    count = deep // 2
+    x, y, z, core = index % count, (index // count) % wide, (index // (count * wide)) % deep, index // (count * wide * deep)
+    half, aside, back = row // (deep * wide // 2), (row // count) % wide, row % count
+    if aside == wide // 2:
+        back = (x + count - back) % count
+        ahead = jnp.where(back == 0, count, back)
+    else:
+        ahead = back or count
+    offset = jnp.where(core == half, deep - back, ahead)
     return ((z + offset) % deep) * wide + (y + wide - aside) % wide
 
 
@@ -314,15 +320,22 @@
     )
     pieces[0] = jnp.where(core == 0, block, across)
     column = jnp.stack(pieces)
-    plane = [column] + [
-        lax.ppermute(column, "expert_1", [(i, (i + k) % wide) for i in range(wide)]) for k in range(1, wide)
+    quarter = lax.dynamic_index_in_dim(column, lax.axis_index("dp_0"), 0, keepdims=False)
+    quarter = lax.ppermute(quarter, "expert_1", [(i, (i + wide // 2) % wide) for i in range(wide)])
+    chips = lax.axis_size("dp_0")
+    far = [quarter] + [
+        lax.ppermute(quarter, "dp_0", [(i, (i + k) % chips) for i in range(chips)]) for k in range(1, chips)
     ]
+    near = [
+        lax.ppermute(column, "expert_1", [(i, (i + k) % wide) for i in range(wide)]) for k in (1, wide - 1)
+    ]
+    plane = [column, near[0], jnp.stack(far), near[1]]
     tall = features // LANES
     own = jnp.stack(plane).reshape(group, per_device, tall, LANES).transpose(1, 0, 2, 3)
     own = own.reshape(num_experts // 2, features)
     other = lax.ppermute(own, "dp_1", [(0, 1), (1, 0)])
 
-    where = lax.axis_index(("dp_1", *EXPERT)).astype(jnp.int32).reshape(1)
+    where = lax.axis_index(("dp_1", *EXPERT, "dp_0")).astype(jnp.int32).reshape(1)
     rows = (share // LANES + 1) * ROWS
     experts_here = lax.dynamic_slice_in_dim(expert_pick, my_index * share, share, 1)
     devices_here = lax.dynamic_slice_in_dim(device_pick, my_index * share, share, 1)

time: 75.3 us -> 77.2 us (1.025)
  starting transfers between devices: 27.9 us -> 30.9 us
  waiting for transfers between devices: 10.9 us -> 9.85 us
    ppermute x3 -> x2, waiting for transfers between devices: 6.95 us -> 0.01 us  [local(): lax.ppermute(column, 'expert_1', [(i, (i + k) % wide) for i in range(wide)])]
    ppermute x0 -> x4, starting transfers between devices: none -> 6.61 us  [the longest x3 3.6 us: local(): lax.ppermute(quarter, 'dp_0', [(i, (i + k) % chips) for i in range(chips)])]
    ppermute x0 -> x4, waiting for transfers between devices: none -> 4.95 us  [the longest x3 4.94 us: local(): lax.ppermute(quarter, 'dp_0', [(i, (i + k) % chips) for i in range(chips)])]
    ppermute x3 -> x2, starting transfers between devices: 5.68 us -> 2.68 us  [local(): lax.ppermute(column, 'expert_1', [(i, (i + k) % wide) for i in range(wide)])]
    ppermute x1, starting transfers between devices: 2.48 us -> 0.27 us  [local(): near = lax.ppermute(chip, ('dp_0', 'dp_1'), around)]
    ppermute x1, waiting for transfers between devices: 0.23 us -> 1.26 us  [local(): near = lax.ppermute(chip, ('dp_0', 'dp_1'), around)]
    ppermute x1, starting transfers between devices: 1.93 us -> 2.7 us  [local(): swapped = lax.ppermute(near, 'dp_1', swap)]
  transfers between devices with their start and end apart: 12 -> 15, of which waited for: 9 -> 9; matrix products, arithmetic and copies ran while one was open for 1% -> 1% of each run, Pallas kernels for 3% -> 3%
where the time goes in v9:
time: 77.2 us; the launch traced here: 77 us
  starting transfers between devices  30.9 us (40%)
  blocking collectives  24.5 us (32%)
  waiting for transfers between devices  9.85 us (13%)
  Pallas kernels  8.85 us (11%)
  local copies, waits for them, and re-layouts  2.01 us (3%)
    all_to_all x1, blocking collectives, local(): recv = lax.all_to_all(msg, EXPERT, 0, 0, tiled=True)  24.5 us
    ppermute x1, starting transfers between devices, local(): lax.ppermute(block, ('dp_1', 'expert_0'), [(deep + i, deep + (i + deep //...  9.64 us
    pallas_call x1, Pallas kernels, route(): pl.pallas_call(functools.partial(route_kernel, sizes, per_device), out_sh...  5.83 us
    ppermute x3, waiting for transfers between devices, local(): lax.ppermute(quarter, 'dp_0', [(i, (i + k) % chips) for i in range(chips)])  4.94 us
    ppermute x3, starting transfers between devices, local(): pieces.append(lax.ppermute(block, ('dp_1', 'expert_0'), pairs))  4.84 us
    ppermute x3, starting transfers between devices, local(): lax.ppermute(quarter, 'dp_0', [(i, (i + k) % chips) for i in range(chips)])  3.6 us
    ppermute x1, starting transfers between devices, local(): lax.ppermute(quarter, 'expert_1', [(i, (i + wide // 2) % wide) for i in r...  3 us
    ppermute x1, starting transfers between devices, local(): swapped = lax.ppermute(near, 'dp_1', swap)  2.7 us
  transfers between devices with their start and end apart: 15, of which 9 were waited for; matrix products, arithmetic and copies ran while one was open for 1% of the time, Pallas kernels for 3%

profile of v9, /device:TPU:1, one launch (start us, length us, event | category | flops | bytes accessed | tf_op | source)
XLA Modules:
  0.0 77.0 jit_solution(16637711432214438341)
XLA Ops:
  0.6 0.0 copy-start
  0.6 1.1 %reshape.22 = bf16[200,128]{1,0:T(8,128)(2,1)S(1)} reshape(bf16[5,5120]{1,0:T(8,128)(2,1)} %bitcast.34) | data formatting | bytes 102400 | tf_op jit(solution)/shard_map/reshape | solution.py:312
  1.7 9.6 %collective-permute-start = (bf16[200,128]{1,0:T(8,128)(2,1)S(1)}, bf16[200,128]{1,0:T(8,128)(2,1)S(1)}, u32[]{:S(2)}, u32[]{:S(2)}) collective-permute-start(bf16[200,128]{1,0:T(8,128)(2,1)S(1)} %reshape.22), channel_id=1, source_target_pairs={{32,48},{36,52},{40,56},{44,60},{48,32},{52,36},{56,40},{60,44},{3... | collective-permute-start | bytes 153608 | tf_op jit(solution)/shard_map/ppermute | solution.py:318
  11.3 0.1 collective-permute-start.3
  11.4 4.0 %collective-permute-start.2 = (bf16[200,128]{1,0:T(8,128)(2,1)S(1)}, bf16[200,128]{1,0:T(8,128)(2,1)S(1)}, u32[]{:S(2)}, u32[]{:S(2)}) collective-permute-start(bf16[200,128]{1,0:T(8,128)(2,1)S(1)} %reshape.22), channel_id=1, source_target_pairs={{0,8},{4,12},{8,16},{12,20},{16,24},{20,28},{24,0},{28,4},{32,56},... | collective-permute-start | bytes 153608 | tf_op jit(solution)/shard_map/ppermute | solution.py:317
  15.5 0.7 collective-permute-start.1
  16.2 0.0 collective-permute-done
  16.2 0.1 collective-permute-done.3
  16.3 0.4 collective-permute-done.2
  16.7 1.7 %collective-permute-done.1 = bf16[200,128]{1,0:T(8,128)(2,1)S(1)} collective-permute-done((bf16[200,128]{1,0:T(8,128)(2,1)S(1)}, bf16[200,128]{1,0:T(8,128)(2,1)S(1)}, u32[]{:S(2)}, u32[]{:S(2)}) %collective-permute-start.1) | collective-permute-done | bytes 51232 | tf_op jit(solution)/shard_map/ppermute | solution.py:317
  18.5 3.0 %collective-permute-start.5 = (bf16[200,128]{1,0:T(8,128)(2,1)S(1)}, bf16[200,128]{1,0:T(8,128)(2,1)S(1)}, u32[]{:S(2)}, u32[]{:S(2)}) collective-permute-start(bf16[200,128]{1,0:T(8,128)(2,1)S(1)} %dynamic-slice_bitcast_fusion), channel_id=1, source_target_pairs={{0,2},{1,3},{2,0},{3,1},{4,6},{5,7},{6,4},{7,5},{8,10},{9,11},{10,... | collective-permute-start | bytes 153608 | tf_op jit(solution)/shard_map/ppermute | solution.py:324
  21.5 0.4 collective-permute-start.4
  21.9 2.3 %collective-permute-start.9 = (bf16[4,200,128]{2,1,0:T(8,128)(2,1)S(1)}, bf16[4,200,128]{2,1,0:T(8,128)(2,1)S(1)}, u32[]{:S(2)}, u32[]{:S(2)}) collective-permute-start(bf16[4,200,128]{2,1,0:T(8,128)(2,1)S(1)} %get-tuple-element.8), channel_id=1, source_target_pairs={{0,3},{1,0},{2,1},{3,2},{4,7},{5,4},{6,5},{7,6},{8,11},{9,8},{10,9... | collective-permute-start | bytes 614408 | tf_op jit(solution)/shard_map/ppermute | solution.py:330
  24.2 0.0 collective-permute-done.5
  24.2 2.5 %collective-permute-start.8 = (bf16[200,128]{1,0:T(8,128)(2,1)S(1)}, bf16[200,128]{1,0:T(8,128)(2,1)S(1)}, u32[]{:S(2)}, u32[]{:S(2)}) collective-permute-start(bf16[200,128]{1,0:T(8,128)(2,1)S(1)} %collective-permute-done.5), channel_id=1, source_target_pairs={{0,192},{64,0},{128,64},{192,128},{1,193},{65,1},{129,65},{193,129... | collective-permute-start | bytes 153608 | tf_op jit(solution)/shard_map/ppermute | solution.py:327
  26.7 0.5 collective-permute-start.7
  27.2 0.6 collective-permute-start.6
  27.8 0.1 collective-permute-done.8
  27.9 3.3 %collective-permute-done.7 = bf16[200,128]{1,0:T(8,128)(2,1)S(1)} collective-permute-done((bf16[200,128]{1,0:T(8,128)(2,1)S(1)}, bf16[200,128]{1,0:T(8,128)(2,1)S(1)}, u32[]{:S(2)}, u32[]{:S(2)}) %collective-permute-start.7) | collective-permute-done | bytes 51232 | tf_op jit(solution)/shard_map/ppermute | solution.py:327
  31.2 1.6 %collective-permute-done.6 = bf16[200,128]{1,0:T(8,128)(2,1)S(1)} collective-permute-done((bf16[200,128]{1,0:T(8,128)(2,1)S(1)}, bf16[200,128]{1,0:T(8,128)(2,1)S(1)}, u32[]{:S(2)}, u32[]{:S(2)}) %collective-permute-start.6) | collective-permute-done | bytes 51232 | tf_op jit(solution)/shard_map/ppermute | solution.py:327
  32.8 0.0 collective-permute-done.4
  32.8 0.0 collective-permute-done.9
  32.8 0.1 pad_maximum_fusion
  32.9 0.1 copy.7
  33.0 0.1 copy.10
  33.1 0.8 %collective-permute-start.10 = (bf16[80,5120]{1,0:T(8,128)(2,1)S(1)}, bf16[80,5120]{1,0:T(8,128)(2,1)S(1)}, u32[]{:S(2)}, u32[]{:S(2)}) collective-permute-start(bf16[80,5120]{1,0:T(8,128)(2,1)S(1)} %bitcast.28), channel_id=1, source_target_pairs={{0,32},{32,0},{1,33},{33,1},{2,34},{34,2},{3,35},{35,3},{4,36},{36... | collective-permute-start | bytes 2457608 | tf_op jit(solution)/shard_map/ppermute | solution.py:336
  33.9 0.7 constant_dynamic-slice_fusion.devs
  34.7 0.0 copy-done
  34.7 0.6 count.1.counts
  35.3 0.6 collective-permute-done.10.other
  35.9 5.8 %route.1 = s16[32,72,128]{2,1,0:T(8,128)(2,1)S(1)} custom-call(s32[1]{0:T(128)} %bitcast.where, bf16[80,5120]{1,0:T(8,128)(2,1)S(1)} %bitcast.29, bf16[80,5120]{1,0:T(8,128)(2,1)S(1)} %collective-permute-done.10.other, bf16[5120,1024]{1,0:T(8,128)(2,1)} %tokens.1, s32[6,1024]{1,0:T(8,128)S(1)} %constant_dynamic-slice_fusion.1.picks, f32[8,128]{1,0:T(8,128)S(1)} %count.1.counts), custom_call_target="tpu_custom_call" | custom-call | tf_op jit(solution)/shard_map/route/pallas_call | solution.py:220
  41.7 24.5 %all_to_all.5.recv = s16[32,72,128]{2,1,0:T(8,128)(2,1)S(1)} all-to-all(s16[32,72,128]{2,1,0:T(8,128)(2,1)S(1)} %route.1), channel_id=1, replica_groups=mesh['dp_0'=4,'dp_1'=2,'expert_0'=8,'expert_1'=4] {'expert_0','expert_1'}, dimensions={0} | all-to-all | bytes 1179648 | tf_op jit(solution)/shard_map/all_to_all | solution.py:350
  66.2 0.1 sums.1
  66.3 2.4 %collective-permute-start.11 = (f32[8,128]{1,0:T(8,128)S(1)}, f32[8,128]{1,0:T(8,128)S(1)}, u32[]{:S(2)}, u32[]{:S(2)}) collective-permute-start(f32[8,128]{1,0:T(8,128)S(1)} %sums.1), channel_id=1, source_target_pairs={{0,32},{32,0},{1,33},{33,1},{2,34},{34,2},{3,35},{35,3},{4,36},{36... | collective-permute-start | bytes 12296 | tf_op jit(solution)/shard_map/ppermute | solution.py:370
  68.7 0.8 %collective-permute-done.11 = f32[8,128]{1,0:T(8,128)S(1)} collective-permute-done((f32[8,128]{1,0:T(8,128)S(1)}, f32[8,128]{1,0:T(8,128)S(1)}, u32[]{:S(2)}, u32[]{:S(2)}) %collective-permute-start.11) | collective-permute-done | bytes 4128 | tf_op jit(solution)/shard_map/ppermute | solution.py:370
  69.5 0.3 collective-permute-start.12
  69.8 0.9 %collective-permute-start.13 = (f32[8,128]{1,0:T(8,128)S(1)}, f32[8,128]{1,0:T(8,128)S(1)}, u32[]{:S(2)}, u32[]{:S(2)}) collective-permute-start(f32[8,128]{1,0:T(8,128)S(1)} %add.33.own), channel_id=1, source_target_pairs={{0,128},{64,192},{128,0},{192,64},{1,129},{65,193},{129,1},{193,65... | collective-permute-start | bytes 12296 | tf_op jit(solution)/shard_map/ppermute | solution.py:375
  70.7 1.3 %collective-permute-done.12.near = f32[8,128]{1,0:T(8,128)S(1)} collective-permute-done((f32[8,128]{1,0:T(8,128)S(1)}, f32[8,128]{1,0:T(8,128)S(1)}, u32[]{:S(2)}, u32[]{:S(2)}) %collective-permute-start.12) | collective-permute-done | bytes 4128 | tf_op jit(solution)/shard_map/ppermute | solution.py:374
  72.0 2.7 %collective-permute-start.14 = (f32[8,128]{1,0:T(8,128)S(1)}, f32[8,128]{1,0:T(8,128)S(1)}, u32[]{:S(2)}, u32[]{:S(2)}) collective-permute-start(f32[8,128]{1,0:T(8,128)S(1)} %collective-permute-done.12.near), channel_id=1, source_target_pairs={{0,32},{32,0},{1,33},{33,1},{2,34},{34,2},{3,35},{35,3},{4,36},{36... | collective-permute-start | bytes 12296 | tf_op jit(solution)/shard_map/ppermute | solution.py:376
  74.7 1.5 %spread.1 = (f32[6,32768]{1,0:T(8,128)}, f32[1,32768]{1,0:T(1,128)}) custom-call(s16[32,72,128]{2,1,0:T(8,128)(2,1)S(1)} %all_to_all.5.recv), custom_call_target="tpu_custom_call" | custom-call | tf_op jit(solution)/shard_map/spread/pallas_call | solution.py:360
  76.3 0.0 collective-permute-done.13.far
  76.3 0.0 collective-permute-done.14.swapped
  76.3 0.7 balance.1
  (6 shorter events, 0.1 us)
Async XLA Ops:
  0.6 34.0 %copy-start = (s32[6,32768]{1,0:T(8,128)S(1)}, s32[6,32768]{1,0:T(8,128)}, u32[]{:S(2)}) copy-start(s32[6,32768]{1,0:T(8,128)} %param.7) | copy-start | bytes 2359300
  1.7 14.5 %collective-permute-start = (bf16[200,128]{1,0:T(8,128)(2,1)S(1)}, bf16[200,128]{1,0:T(8,128)(2,1)S(1)}, u32[]{:S(2)}, u32[]{:S(2)}) collective-permute-start(bf16[200,128]{1,0:T(8,128)(2,1)S(1)} %reshape.22), channel_id=1, source_target_pairs={{32,48},{36,52},{40,56},{44,60},{48,32},{52,36},{56,40},{60,44},{3... | collective-permute-start | bytes 153608 | tf_op jit(solution)/shard_map/ppermute | solution.py:318
  11.3 4.9 %collective-permute-start.3 = (bf16[200,128]{1,0:T(8,128)(2,1)S(1)}, bf16[200,128]{1,0:T(8,128)(2,1)S(1)}, u32[]{:S(2)}, u32[]{:S(2)}) collective-permute-start(bf16[200,128]{1,0:T(8,128)(2,1)S(1)} %reshape.22), channel_id=1, source_target_pairs={{0,12},{4,16},{8,20},{12,24},{16,28},{20,0},{24,4},{28,8},{32,52},... | collective-permute-start | bytes 153608 | tf_op jit(solution)/shard_map/ppermute | solution.py:317
  11.4 5.3 %collective-permute-start.2 = (bf16[200,128]{1,0:T(8,128)(2,1)S(1)}, bf16[200,128]{1,0:T(8,128)(2,1)S(1)}, u32[]{:S(2)}, u32[]{:S(2)}) collective-permute-start(bf16[200,128]{1,0:T(8,128)(2,1)S(1)} %reshape.22), channel_id=1, source_target_pairs={{0,8},{4,12},{8,16},{12,20},{16,24},{20,28},{24,0},{28,4},{32,56},... | collective-permute-start | bytes 153608 | tf_op jit(solution)/shard_map/ppermute | solution.py:317
  15.5 3.0 %collective-permute-start.1 = (bf16[200,128]{1,0:T(8,128)(2,1)S(1)}, bf16[200,128]{1,0:T(8,128)(2,1)S(1)}, u32[]{:S(2)}, u32[]{:S(2)}) collective-permute-start(bf16[200,128]{1,0:T(8,128)(2,1)S(1)} %reshape.22), channel_id=1, source_target_pairs={{0,4},{4,8},{8,12},{12,16},{16,20},{20,24},{24,28},{28,0},{32,60},... | collective-permute-start | bytes 153608 | tf_op jit(solution)/shard_map/ppermute | solution.py:317
  18.5 5.7 %collective-permute-start.5 = (bf16[200,128]{1,0:T(8,128)(2,1)S(1)}, bf16[200,128]{1,0:T(8,128)(2,1)S(1)}, u32[]{:S(2)}, u32[]{:S(2)}) collective-permute-start(bf16[200,128]{1,0:T(8,128)(2,1)S(1)} %dynamic-slice_bitcast_fusion), channel_id=1, source_target_pairs={{0,2},{1,3},{2,0},{3,1},{4,6},{5,7},{6,4},{7,5},{8,10},{9,11},{10,... | collective-permute-start | bytes 153608 | tf_op jit(solution)/shard_map/ppermute | solution.py:324
  21.5 11.3 %collective-permute-start.4 = (bf16[4,200,128]{2,1,0:T(8,128)(2,1)S(1)}, bf16[4,200,128]{2,1,0:T(8,128)(2,1)S(1)}, u32[]{:S(2)}, u32[]{:S(2)}) collective-permute-start(bf16[4,200,128]{2,1,0:T(8,128)(2,1)S(1)} %get-tuple-element.8), channel_id=1, source_target_pairs={{0,1},{1,2},{2,3},{3,0},{4,5},{5,6},{6,7},{7,4},{8,9},{9,10},{10,1... | collective-permute-start | bytes 614408 | tf_op jit(solution)/shard_map/ppermute | solution.py:330
  21.9 10.9 %collective-permute-start.9 = (bf16[4,200,128]{2,1,0:T(8,128)(2,1)S(1)}, bf16[4,200,128]{2,1,0:T(8,128)(2,1)S(1)}, u32[]{:S(2)}, u32[]{:S(2)}) collective-permute-start(bf16[4,200,128]{2,1,0:T(8,128)(2,1)S(1)} %get-tuple-element.8), channel_id=1, source_target_pairs={{0,3},{1,0},{2,1},{3,2},{4,7},{5,4},{6,5},{7,6},{8,11},{9,8},{10,9... | collective-permute-start | bytes 614408 | tf_op jit(solution)/shard_map/ppermute | solution.py:330
  24.2 3.7 %collective-permute-start.8 = (bf16[200,128]{1,0:T(8,128)(2,1)S(1)}, bf16[200,128]{1,0:T(8,128)(2,1)S(1)}, u32[]{:S(2)}, u32[]{:S(2)}) collective-permute-start(bf16[200,128]{1,0:T(8,128)(2,1)S(1)} %collective-permute-done.5), channel_id=1, source_target_pairs={{0,192},{64,0},{128,64},{192,128},{1,193},{65,1},{129,65},{193,129... | collective-permute-start | bytes 153608 | tf_op jit(solution)/shard_map/ppermute | solution.py:327
  26.7 4.5 %collective-permute-start.7 = (bf16[200,128]{1,0:T(8,128)(2,1)S(1)}, bf16[200,128]{1,0:T(8,128)(2,1)S(1)}, u32[]{:S(2)}, u32[]{:S(2)}) collective-permute-start(bf16[200,128]{1,0:T(8,128)(2,1)S(1)} %collective-permute-done.5), channel_id=1, source_target_pairs={{0,128},{64,192},{128,0},{192,64},{1,129},{65,193},{129,1},{193,65... | collective-permute-start | bytes 153608 | tf_op jit(solution)/shard_map/ppermute | solution.py:327
  27.2 5.6 %collective-permute-start.6 = (bf16[200,128]{1,0:T(8,128)(2,1)S(1)}, bf16[200,128]{1,0:T(8,128)(2,1)S(1)}, u32[]{:S(2)}, u32[]{:S(2)}) collective-permute-start(bf16[200,128]{1,0:T(8,128)(2,1)S(1)} %collective-permute-done.5), channel_id=1, source_target_pairs={{0,64},{64,128},{128,192},{192,0},{1,65},{65,129},{129,193},{193,1... | collective-permute-start | bytes 153608 | tf_op jit(solution)/shard_map/ppermute | solution.py:327
  33.1 2.8 %collective-permute-start.10 = (bf16[80,5120]{1,0:T(8,128)(2,1)S(1)}, bf16[80,5120]{1,0:T(8,128)(2,1)S(1)}, u32[]{:S(2)}, u32[]{:S(2)}) collective-permute-start(bf16[80,5120]{1,0:T(8,128)(2,1)S(1)} %bitcast.28), channel_id=1, source_target_pairs={{0,32},{32,0},{1,33},{33,1},{2,34},{34,2},{3,35},{35,3},{4,36},{36... | collective-permute-start | bytes 2457608 | tf_op jit(solution)/shard_map/ppermute | solution.py:336
  66.3 3.3 %collective-permute-start.11 = (f32[8,128]{1,0:T(8,128)S(1)}, f32[8,128]{1,0:T(8,128)S(1)}, u32[]{:S(2)}, u32[]{:S(2)}) collective-permute-start(f32[8,128]{1,0:T(8,128)S(1)} %sums.1), channel_id=1, source_target_pairs={{0,32},{32,0},{1,33},{33,1},{2,34},{34,2},{3,35},{35,3},{4,36},{36... | collective-permute-start | bytes 12296 | tf_op jit(solution)/shard_map/ppermute | solution.py:370
  69.5 2.5 %collective-permute-start.12 = (f32[8,128]{1,0:T(8,128)S(1)}, f32[8,128]{1,0:T(8,128)S(1)}, u32[]{:S(2)}, u32[]{:S(2)}) collective-permute-start(f32[8,128]{1,0:T(8,128)S(1)} %add.33.own), channel_id=1, source_target_pairs={{0,64},{64,128},{128,192},{192,0},{32,224},{96,32},{160,96},{224,1... | collective-permute-start | bytes 12296 | tf_op jit(solution)/shard_map/ppermute | solution.py:374
  69.8 6.4 %collective-permute-start.13 = (f32[8,128]{1,0:T(8,128)S(1)}, f32[8,128]{1,0:T(8,128)S(1)}, u32[]{:S(2)}, u32[]{:S(2)}) collective-permute-start(f32[8,128]{1,0:T(8,128)S(1)} %add.33.own), channel_id=1, source_target_pairs={{0,128},{64,192},{128,0},{192,64},{1,129},{65,193},{129,1},{193,65... | collective-permute-start | bytes 12296 | tf_op jit(solution)/shard_map/ppermute | solution.py:375
  72.0 4.3 %collective-permute-start.14 = (f32[8,128]{1,0:T(8,128)S(1)}, f32[8,128]{1,0:T(8,128)S(1)}, u32[]{:S(2)}, u32[]{:S(2)}) collective-permute-start(f32[8,128]{1,0:T(8,128)S(1)} %collective-permute-done.12.near), channel_id=1, source_target_pairs={{0,32},{32,0},{1,33},{33,1},{2,34},{34,2},{3,35},{35,3},{4,36},{36... | collective-permute-start | bytes 12296 | tf_op jit(solution)/shard_map/ppermute | solution.py:376
